TPU v7x, 128 devices: a whole 4x4x4 slice. The times are simulated.
128 devices in a mesh: blk: 32 (over z, y, x_hi), tp: 4 (over x_lo, core).
Axes of the slice: x: 4 (x_hi: 2, x_lo: 2; x = x_hi * 2 + x_lo), y: 4, z: 4, core: 2. Of those that a mesh axis runs over, the one named last changes fastest.
Arguments:
- tokens: bfloat16 [8192, 2048], P('blk'), may hold values from -27 to 27
- order: int32 [64], replicated, may hold values from 0 to 63, each once
- gain_attn: float32 [2048], replicated, may hold values from 0.1 to 1.9
- gain_ffn: float32 [2048], replicated, may hold values from 0.1 to 1.9
- w_query: bfloat16 [2048, 2048], P(None, 'tp'), may hold values from -3.7565048 to 3.7565048
- w_key: bfloat16 [2048, 512], P(None, 'tp'), may hold values from -0.13258252 to 0.13258252
- w_value: bfloat16 [2048, 512], P(None, 'tp'), may hold values from -0.125 to 0.125
- w_out: bfloat16 [2048, 2048], P('tp'), may hold values from -0.125 to 0.125
- w_gate: bfloat16 [2048, 8192], P(None, 'tp'), may hold values from -0.125 to 0.125
- w_up: bfloat16 [2048, 8192], P(None, 'tp'), may hold values from -0.125 to 0.125
- w_down: bfloat16 [8192, 2048], P('tp'), may hold values from -0.0625 to 0.0625
Outputs:
- layer_out: bfloat16 [8192, 2048], P('blk', 'tp')
Inputs may be any that keep to these rules, and one draw needn't show every extreme that they name: `order`: every number 0 to 63 appears once; device b of blk holds stored blocks 2b and 2b + 1.
All inputs are finite; a program needn't handle non-finite values.
Results may differ from a plain program's by a relative error of at most 0.0095.
Values may be sent and summed in bfloat16 or wider, within the bound.
No kernel may reach another device: no remote copies, remote signals or barrier semaphores. Data moves between devices by JAX's collectives and lax.ppermute only.
A program may use at most 128 MiB of HBM per device.

v0:
```python
import jax
import jax.numpy as jnp
from jax import lax
from jax.sharding import PartitionSpec as P

HD = 64


EPS = 1e-05
ROPE_BASE = 500000.0
MASKED = -1e30


def gathered_total(shard, axis):
    return lax.all_gather(shard, axis).astype(jnp.float32).sum(0)


def in_blocks(shard, dim, peers):
    before, after = (shard.shape[:dim], shard.shape[dim + 1 :])
    return jnp.moveaxis(shard.reshape(*before, peers, -1, *after), dim, 0)


def sum_at_owner(shard, axis, dim):
    peers = lax.axis_size(axis)
    parts = lax.all_to_all(in_blocks(shard, dim, peers), axis, 0, 0, tiled=True)
    return jnp.sum(parts.astype(jnp.float32), axis=0)


def rotate(values, positions):
    half_dim = values.shape[-1] // 2
    freq = ROPE_BASE ** (-(jnp.arange(half_dim, dtype=jnp.float32) * 2.0 / values.shape[-1]))
    angle = positions.astype(jnp.float32)[:, None] * freq[None, :]
    cosine = jnp.cos(angle)[:, None, :]
    sine = jnp.sin(angle)[:, None, :]
    first = values[..., :half_dim]
    second = values[..., half_dim:]
    return jnp.concatenate(
        [first * cosine - second * sine, second * cosine + first * sine], axis=-1
    )


def stored_positions(order, start, count, half_rows):
    stored = start + jnp.arange(count, dtype=jnp.int32)
    which = stored // half_rows
    match = which[:, None] == jnp.arange(order.shape[0], dtype=jnp.int32)[None, :]
    first = jnp.sum(jnp.where(match, order[None, :], 0), axis=1)
    return first * half_rows + stored % half_rows


def local(tokens, order, gain_attn, gain_ffn, w_query, w_key, w_value, w_out, w_gate, w_up, w_down):
    tok_rows, model_width = tokens.shape
    half_rows = tok_rows // 2
    kv_local = w_key.shape[1] // HD
    query_local = w_query.shape[1] // HD
    group = query_local // kv_local
    score_scale = HD ** (-0.5)
    query_pos = stored_positions(order, lax.axis_index("blk") * tok_rows, tok_rows, half_rows)
    tokens_wide = tokens.astype(jnp.float32)
    normed = (
        tokens_wide
        * lax.rsqrt(jnp.mean(tokens_wide * tokens_wide, axis=-1, keepdims=True) + EPS)
        * gain_attn
    ).astype(jnp.bfloat16)
    queries = jnp.dot(normed, w_query, preferred_element_type=jnp.float32).reshape(
        tok_rows, query_local, HD
    )
    queries = rotate(queries, query_pos).astype(jnp.bfloat16).reshape(tok_rows, kv_local, group, HD)
    keys = jnp.dot(normed, w_key, preferred_element_type=jnp.float32).reshape(
        tok_rows, kv_local, HD
    )
    keys = rotate(keys, query_pos).astype(jnp.bfloat16)
    values = jnp.dot(normed, w_value, preferred_element_type=jnp.float32).astype(jnp.bfloat16)
    packed = jnp.concatenate([keys.reshape(tok_rows, kv_local * HD), values], axis=1)

    def attend(carry, block, key_pos):
        running, denominator, accum = carry
        key_block = block[:, : kv_local * HD].reshape(-1, kv_local, HD)
        value_block = block[:, kv_local * HD :].reshape(-1, kv_local, HD)
        scores = (
            jnp.einsum("qkgd,skd->kgqs", queries, key_block, preferred_element_type=jnp.float32)
            * score_scale
        )
        allowed = key_pos[None, :] <= query_pos[:, None]
        scores = jnp.where(allowed, scores, MASKED)
        newest = jnp.maximum(running, jnp.max(scores, axis=-1))
        weights = jnp.where(allowed, jnp.exp(scores - newest[..., None]), 0.0)
        factor = jnp.exp(running - newest)
        denominator = denominator * factor + jnp.sum(weights, axis=-1)
        accum = accum * factor[..., None] + jnp.einsum(
            "kgqs,skd->kgqd",
            weights.astype(jnp.bfloat16),
            value_block,
            preferred_element_type=jnp.float32,
        )
        return (newest, denominator, accum)

    def consider(carry, block, key_pos):
        return attend(carry, block, key_pos)

    start_carry = (
        jnp.full((kv_local, group, tok_rows), MASKED, jnp.float32),
        jnp.zeros((kv_local, group, tok_rows), jnp.float32),
        jnp.zeros((kv_local, group, tok_rows, HD), jnp.float32),
    )
    piece = lax.all_gather(packed, "blk", axis=0, tiled=True)
    count = piece.shape[0]
    key_pos = stored_positions(order, jnp.int32(0), count, half_rows)
    turns = min(16, count // 512)
    size = count // turns

    def one_turn(turn, inner):
        offset = turn * size
        return consider(
            inner,
            lax.dynamic_slice_in_dim(piece, offset, size, 0),
            lax.dynamic_slice_in_dim(key_pos, offset, size, 0),
        )

    running, denominator, accum = lax.fori_loop(0, turns, one_turn, start_carry)
    heads = (accum / denominator[..., None]).astype(jnp.bfloat16)
    heads = jnp.transpose(heads, (2, 0, 1, 3)).reshape(tok_rows, query_local * HD)
    partial_value = jnp.dot(heads, w_out, preferred_element_type=jnp.float32)
    share = model_width // lax.axis_size("tp")
    col_start = lax.axis_index("tp") * share
    attention = gathered_total(partial_value.astype(jnp.bfloat16), "tp").astype(jnp.float32)
    resid_full = tokens_wide + attention
    normed_ffn = (
        resid_full
        * lax.rsqrt(jnp.mean(resid_full * resid_full, axis=-1, keepdims=True) + EPS)
        * gain_ffn
    ).astype(jnp.bfloat16)
    gate = jnp.dot(normed_ffn, w_gate, preferred_element_type=jnp.float32)
    up_proj = jnp.dot(normed_ffn, w_up, preferred_element_type=jnp.float32)
    residual = lax.dynamic_slice_in_dim(resid_full, col_start, share, 1)
    hidden = (jax.nn.silu(gate) * up_proj).astype(jnp.bfloat16)
    down = jnp.dot(hidden, w_down, preferred_element_type=jnp.float32)
    feed = sum_at_owner(down.astype(jnp.bfloat16), "tp", 1)
    return (residual + feed).astype(jnp.bfloat16)


def solution(mesh):
    placed = (
        P("blk", None),
        P(),
        P(),
        P(),
        P(None, "tp"),
        P(None, "tp"),
        P(None, "tp"),
        P("tp", None),
        P(None, "tp"),
        P(None, "tp"),
        P("tp", None),
    )
    return jax.shard_map(
        local, mesh=mesh, in_specs=placed, out_specs=P("blk", "tp"), check_vma=False
    )
```

profile of v0, /device:TPU:1, one launch (start us, length us, event | category | flops | bytes accessed | tf_op | source)
XLA Modules:
  0.0 275.2 jit_solution(524990952638176915)
XLA Ops:
  6.6 1.7 fusion.14
  9.1 1.9 convolution_convert_fusion.2
  12.7 2.6 fusion.29
  15.9 75.9 %all-gather.4.cloned.1.call-done = bf16[8192,256]{0,1:T(8,128)(2,1)} async-done(((bf16[256,256]{0,1:T(8,128)(2,1)}), bf16[8192,256]{0,1:T(8,128)(2,1)}) %all-gather.4.cloned.1.call-update) | async-done | bytes 4194320 | tf_op jit(solution)/shard_map/all_gather | solution.py:105
  91.8 82.9 %while.18 = (s32[]{:T(128)}, f32[2,4,256]{2,1,0:T(4,128)S(1)}, f32[2,4,256]{2,1,0:T(4,128)S(1)}, f32[2,4,256,64]{2,3,1,0:T(8,128)}, s32[8192]{0:T(1024)S(1)}, /*...) while((s32[]{:T(128)}, f32[2,4,256]{2,1,0:T(4,128)S(1)}, ...), condition=%wide.region_6.7_spmd.clone, body=%wide.region_3.6_spmd.clone.sunk | while | flops 282601472 | bytes 19537168 | solution.py:119
  94.9 1.3 fusion.65
  100.1 1.3 fusion.65
  105.2 1.3 fusion.65
  110.4 1.3 fusion.65
  115.6 1.3 fusion.65
  120.8 1.3 fusion.65
  126.0 1.3 fusion.65
  131.1 1.3 fusion.65
  136.3 1.3 fusion.65
  141.5 1.3 fusion.65
  146.7 1.3 fusion.65
  151.9 1.3 fusion.65
  157.0 1.3 fusion.65
  162.2 1.3 fusion.65
  167.4 1.3 fusion.65
  172.6 1.3 fusion.65
  174.6 1.1 divide_convert_fusion
  175.7 1.7 convolution_convert_fusion
  177.5 47.5 %all-gather.6.cloned.1.call-done = bf16[1024,2048]{1,0:T(8,128)(2,1)} async-done(((bf16[256,2048]{1,0:T(8,128)(2,1)}), bf16[1024,2048]{1,0:T(8,128)(2,1)}) %all-gather.6.cloned.1.call-update) | async-done | bytes 4194320 | tf_op jit(solution)/shard_map/all_gather | solution.py:15
  225.0 3.3 %convert_reduce_fusion = f32[256,2048]{1,0:T(8,128)S(1)} fusion(bf16[4,256,2048]{2,1,0:T(8,128)(2,1)} %bitcast.68), kind=kLoop, calls=%fused_computation.18 | loop fusion | flops 3670016 | bytes 6291456 | tf_op jit(solution)/shard_map/reduce_sum | solution.py:15
  228.7 1.3 copy-done.2
  230.0 7.1 %fusion.28 = f32[256,2048]{1,0:T(8,128)} fusion(bf16[2048,2048]{1,0:T(8,128)(2,1)} %param.21, f32[256,2048]{1,0:T(8,128)S(1)} %get-tuple-element.193, f32[2048]{0:T(1024)S(1)} %copy-done.8, f32[256]{0:T(256)S(1)} %add_rsqrt_fusion), kind=kOutput, calls=%fused_computation.74 | convolution fusion | flops 2149056512 | bytes 12592128 | tf_op jit(solution)/shard_map/dot_general | solution.py:132
  237.1 11.7 %convolution_convert_fusion.1 = bf16[256,2048]{1,0:T(8,128)(2,1)S(1)} fusion(bf16[2048,2048]{1,0:T(8,128)(2,1)} %param.23, bf16[2048,2048]{1,0:T(8,128)(2,1)} %param.22, f32[256,2048]{1,0:T(8,128)} %fusion.28, f32[256,2048]{1,0:T(8,128)} %copy-done.2, f32[2048]{0:T(1024)S(1)} %copy-done.8, f32[256]{0:T(256)S(1)} %add_rsqrt_fusion), kind=kOutput, calls=%fused_computation.25 | convolution fusion | flops 4300210176 | bytes 22029312 | tf_op jit(solution)/shard_map/dot_general | solution.py:136
  248.8 1.1 copy.31
  249.9 3.5 %all-to-all-start = ((bf16[4,256,512]{2,1,0:T(8,128)(2,1)}), bf16[4,256,512]{2,1,0:T(8,128)(2,1)S(1)}, u32[]{:S(2)}, u32[]{:S(2)}) async-start(bf16[4,256,512]{2,1,0:T(8,128)(2,1)} %bitcast.69), calls=%async_computation | async-start | bytes 2097152 | tf_op jit(solution)/shard_map/all_to_all | solution.py:25
  253.4 13.0 %all-to-all-done = bf16[4,256,512]{2,1,0:T(8,128)(2,1)S(1)} async-done(((bf16[4,256,512]{2,1,0:T(8,128)(2,1)}), bf16[4,256,512]{2,1,0:T(8,128)(2,1)S(1)}, u32[]{:S(2)}, u32[]{:S(2)}) %all-to-all-start) | async-done | bytes 1048608 | tf_op jit(solution)/shard_map/all_to_all | solution.py:25
  266.5 1.8 add_convert_fusion
  (230 shorter events, 65.0 us)
Async XLA Ops:
  6.5 169.2 %copy-start = (bf16[512,2048]{1,0:T(8,128)(2,1)S(1)}, bf16[512,2048]{1,0:T(8,128)(2,1)}, u32[]{:S(2)}) copy-start(bf16[512,2048]{1,0:T(8,128)(2,1)} %param.20) | copy-start | bytes 6291460
  6.5 4.5 %copy-start.1 = (bf16[256,2048]{1,0:T(8,128)(2,1)S(1)}, bf16[256,2048]{1,0:T(8,128)(2,1)}, u32[]{:S(2)}) copy-start(bf16[256,2048]{1,0:T(8,128)(2,1)} %param.13) | copy-start | bytes 3145732
  6.5 4.5 %copy-start.7 = (f32[2048]{0:T(1024)S(1)}, f32[2048]{0:T(1024)}, u32[]{:S(2)}) copy-start(f32[2048]{0:T(1024)} %param.15) | copy-start | bytes 24580
  6.5 85.2 %all-gather.4.cloned.1.call-start = ((), (), s32[]{:S(2)}) async-start(), calls=%async_computation.1 | async-start | bytes 4325376 | tf_op jit(solution)/shard_map/all_gather | solution.py:105
  8.2 2.8 %copy-start.6 = (bf16[2048,128]{1,0:T(8,128)(2,1)S(1)}, bf16[2048,128]{1,0:T(8,128)(2,1)}, u32[]{:S(2)}) copy-start(bf16[2048,128]{1,0:T(8,128)(2,1)} %param.18) | copy-start | bytes 1572868
  12.6 212.4 %all-gather.6.cloned.1.call-start = ((), (), s32[]{:S(2)}) async-start(), calls=%async_computation.2 | async-start | bytes 5242880 | tf_op jit(solution)/shard_map/all_gather | solution.py:15
  12.7 2.7 copy-start.5
  93.8 1.0 copy-start.3
  96.2 0.8 copy-start.4
  99.0 1.0 copy-start.3
  101.3 0.8 copy-start.4
  104.2 1.0 copy-start.3
  109.4 1.0 copy-start.3
  111.7 0.8 copy-start.4
  114.5 1.0 copy-start.3
  116.9 0.8 copy-start.4
  119.7 1.0 copy-start.3
  124.9 1.0 copy-start.3
  127.2 0.8 copy-start.4
  130.1 1.0 copy-start.3
  132.4 0.8 copy-start.4
  135.3 1.0 copy-start.3
  140.4 1.0 copy-start.3
  145.6 1.0 copy-start.3
  150.8 1.0 copy-start.3
  156.0 1.0 copy-start.3
  161.2 1.0 copy-start.3
  166.3 1.0 copy-start.3
  171.5 1.0 copy-start.3
  228.3 1.7 copy-start.8
  228.7 1.3 copy-start.2
  249.9 16.5 %all-to-all-start = ((bf16[4,256,512]{2,1,0:T(8,128)(2,1)}), bf16[4,256,512]{2,1,0:T(8,128)(2,1)S(1)}, u32[]{:S(2)}, u32[]{:S(2)}) async-start(bf16[4,256,512]{2,1,0:T(8,128)(2,1)} %bitcast.69), calls=%async_computation | async-start | bytes 2097152 | tf_op jit(solution)/shard_map/all_to_all | solution.py:25
  (10 other events, 7.9 us)
Sparse Core Ops, SparseCore 0:
  12.7 79.0 all-gather.3
  177.6 47.3 all-gather.5
where the time goes:
time: 277 us; the launch traced here: 275 us
  waiting for transfers between devices  136 us (49%)
  matrix products  59 us (21%)
  local copies, waits for them, and re-layouts  32 us (12%)
  other arithmetic  29.5 us (11%)
  between operations  13.6 us (5%)
  starting transfers between devices  3.55 us (1%)
    all_gather x1, waiting for transfers between devices, local(): piece = lax.all_gather(packed, 'blk', axis=0, tiled=True)  75.9 us
    all_gather x1, waiting for transfers between devices, gathered_total(): return lax.all_gather(shard, axis).astype(jnp.float32).sum(0)  47.5 us
    dot_general x16, matrix products, attend(): jnp.einsum('kgqs,skd->kgqd', weights.astype(jnp.bfloat16), value_block, p...  20.3 us
    reduce_sum x16, other arithmetic, attend(): denominator = denominator * factor + jnp.sum(weights, axis=-1)  16.1 us
    slice x16, local copies, waits for them, and re-layouts, attend(): value_block = block[:, kv_local * HD:].reshape(-1, kv_local, HD)  15.9 us
    dot_general x16, matrix products, attend(): jnp.einsum('qkgd,skd->kgqs', queries, key_block, preferred_element_type=j...  13.1 us
    all_to_all x1, waiting for transfers between devices, sum_at_owner(): parts = lax.all_to_all(in_blocks(shard, dim, peers), axis, 0, 0, tiled=True)  13 us
    while x80, local copies, waits for them, and re-layouts  12.5 us
  transfers between devices with their start and end apart: 3, of which 3 were waited for; matrix products, arithmetic and copies ran while one was open for 1% of the time, Pallas kernels for 0%

commit v1 on v0

v1 whole, which is shorter than its diff:
```python
import functools
import math

import jax
import jax.numpy as jnp
import numpy as np
from jax import lax
from jax.experimental import pallas as pl
from jax.experimental.pallas import tpu as pltpu
from jax.sharding import PartitionSpec as P


HD = 64
EPS = 1e-05
ROPE_BASE = 500000.0
NEG = -1e30
HIDDEN = -2e30
HALF = 128
LOG2E = math.log2(math.e)
MIB = 2**20

VM = pl.BlockSpec(memory_space=pltpu.VMEM)
SM = pl.BlockSpec(memory_space=pltpu.SMEM)
ANY = pl.BlockSpec(memory_space=pltpu.HBM)
BF = jnp.bfloat16
F32 = jnp.float32


def params(mib):
    return pltpu.CompilerParams(vmem_limit_bytes=mib * MIB)


def dot(a, b):
    return jnp.dot(a, b, preferred_element_type=F32)


def rope(u, cos, sin):
    n = u.shape[1] // 128
    outs = []
    lane = lax.broadcasted_iota(jnp.int32, (u.shape[0], 128), 1)
    low = lane % HD < HD // 2
    for k in range(n):
        v = u[:, k * 128 : (k + 1) * 128]
        other = jnp.where(low, pltpu.roll(v, 128 - HD // 2, 1), pltpu.roll(v, HD // 2, 1))
        outs.append(v * cos + other * sin)
    return outs


def angles():
    freq = ROPE_BASE ** (-(np.arange(HD // 2, dtype=np.float64) * 2.0 / HD))
    freq = np.tile(freq, 4)[None, :]
    near = np.arange(HALF, dtype=np.float64)[:, None] * freq
    far = np.arange(64, dtype=np.float64)[:, None] * HALF * freq
    return np.concatenate([np.cos(near), np.sin(near), np.cos(far), np.sin(far)]).astype(np.float32)


def place():
    me = lax.axis_index("blk").astype(jnp.int32)
    tp = lax.axis_index("tp").astype(jnp.int32)
    return me, tp


def kv_kernel(
    order_ref, tok_hbm, gain_hbm, wk_hbm, wv_hbm, table_hbm,
    normed_ref, mine_ref, send_ref, cos_ref, sin_ref,
    kv_ref, tok_ref, gain_ref, w_ref, table_ref, sems,
):
    rows = 64
    n = tok_ref.shape[0] // rows
    gain_copy = pltpu.make_async_copy(gain_hbm, gain_ref, sems.at[9])
    gain_copy.start()
    copies = []
    for i in range(n):
        part = slice(i * rows, (i + 1) * rows)
        copies.append(pltpu.make_async_copy(tok_hbm.at[part], tok_ref.at[part], sems.at[i]))
    half = w_ref.shape[0] // 2
    for i, a in enumerate((wk_hbm, wv_hbm)):
        b = w_ref.at[:, i * 128 : (i + 1) * 128]
        for part in (slice(0, half), slice(half, 2 * half)):
            copies.append(pltpu.make_async_copy(a.at[part], b.at[part], sems.at[len(copies)]))
    copies.append(pltpu.make_async_copy(table_hbm, table_ref, sems.at[len(copies)]))
    for c in copies:
        c.start()
    me, tp = place()
    core = tp % 2
    gain_copy.wait()
    for r in range(0, n * rows, rows):
        copies[r // rows].wait()
        x = tok_ref[r : r + rows, :].astype(F32)
        scale = lax.rsqrt(jnp.mean(x * x, axis=-1, keepdims=True) + EPS)
        normed_ref[r : r + rows, :] = (x * scale * gain_ref[...]).astype(BF)
    copies[-1].wait()
    lane = lax.broadcasted_iota(jnp.int32, (HALF, 128), 1)
    sign = jnp.where(lane % HD < HD // 2, -1.0, 1.0).astype(F32)
    cos, sin = table_ref[:HALF, :], table_ref[HALF : 2 * HALF, :]
    for j in range(2):
        b = order_ref[2 * me + j]
        cb, sb = table_ref[pl.ds(256 + b, 1), :], table_ref[pl.ds(320 + b, 1), :]
        cos_ref[j * HALF : (j + 1) * HALF, :] = cos * cb - sin * sb
        sin_ref[j * HALF : (j + 1) * HALF, :] = (sin * cb + cos * sb) * sign
    for i in range(4):
        copies[n + i].wait()
    both = dot(normed_ref[...], w_ref[...])
    k = rope(both[:, :128], cos_ref[...], sin_ref[...])[0].astype(BF)
    v = jnp.transpose(both[:, 128:]).astype(BF)
    for j in range(2):
        kv_ref[j, :HALF, :] = k[j * HALF : (j + 1) * HALF]
        kv_ref[j, HALF:, :] = v[:, j * HALF : (j + 1) * HALF]
    mine_ref[...] = kv_ref[core]
    send_ref[...] = kv_ref[1 - core]


def pack_kernel(*refs):
    out = refs[-1]
    at = 0
    for r in refs[:-1]:
        out[at : at + r.shape[0]] = r[...]
        at += r.shape[0]


def q_kernel(normed_ref, wq_hbm, cos_ref, sin_ref, q_ref, wq_ref, sem):
    part = wq_ref.shape[0] // 4
    copies = []
    for i in range(4):
        at = slice(i * part, (i + 1) * part)
        copies.append(pltpu.make_async_copy(wq_hbm.at[at], wq_ref.at[at], sem.at[i]))
    for c in copies:
        c.start()
    for c in copies:
        c.wait()
    q = dot(normed_ref[...], wq_ref[...])
    parts = rope(q, cos_ref[...], sin_ref[...])
    q_ref[...] = jnp.zeros(q_ref.shape, BF)
    for k, part in enumerate(parts):
        t = jnp.transpose(part * (HD**-0.5 * LOG2E)).astype(BF)
        for a in range(2):
            head = 2 * k + a
            h, g = head // 4, head % 4
            for i in range(2):
                q_ref[h, h * HD : (h + 1) * HD, i * 512 + g * 128 : i * 512 + (g + 1) * 128] = t[
                    a * HD : (a + 1) * HD, i * HALF : (i + 1) * HALF
                ]


def attend(order_ref, src_ref, first, own, q_refs, kv_ref, m_ref, acc_ref):
    me, tp = place()
    core = tp % 2
    width = 256
    group = kv_ref.shape[0]
    pq = [order_ref[2 * me + i] for i in range(2)]
    pos = [order_ref[src_ref[first + g]] for g in range(group)]
    adds = [[jnp.where(p < q, jnp.float32(0.0), jnp.float32(HIDDEN)) for p in pos] for q in pq]
    if own:
        key = lax.broadcasted_iota(jnp.int32, (HALF, width), 0)
        tok = lax.broadcasted_iota(jnp.int32, (HALF, width), 1) % HALF
        tri = jnp.where(key <= tok, 0.0, HIDDEN).astype(F32)

    def pair(p):
        q_ref = q_refs[p]
        k_all = jnp.concatenate([kv_ref[g, p, :HALF, :] for g in range(group)], axis=0)

        def rest(h, t, s):
            sl = slice(t * width, (t + 1) * width)
            i = t * width // 512
            add = adds[i]
            parts = [s[g * HALF : (g + 1) * HALF] for g in range(group)]
            if own:
                parts[0] = parts[0] + jnp.where(core == i, tri, add[0])
                add = [jnp.float32(0.0), *add[1:]]
            m_old = jnp.full((1, width), NEG, F32) if own else m_ref[2 * p + h, :, sl]
            m_new = m_old
            for x, b in zip(parts, add):
                m_new = jnp.maximum(m_new, jnp.max(x, axis=0, keepdims=True) + b)
            e = [jnp.exp2(x + (b - m_new)).astype(BF) for x, b in zip(parts, add)]
            vt = [kv_ref[g, p, HALF + h * HD : HALF + (h + 1) * HD, :] for g in range(group)]
            vt = jnp.concatenate(vt, axis=1)
            vt = jnp.concatenate([vt, jnp.ones((16, vt.shape[1]), BF)], axis=0)
            new = dot(vt, jnp.concatenate(e, axis=0))
            if not own:
                new = acc_ref[2 * p + h, :, sl] * jnp.exp2(m_old - m_new) + new
            acc_ref[2 * p + h, :, sl] = new
            m_ref[2 * p + h, :, sl] = m_new

        prev = None
        for h in range(2):
            for t in range(1024 // width):
                s = dot(k_all, q_ref[h, :, t * width : (t + 1) * width])
                if prev is not None:
                    rest(*prev)
                prev = (h, t, s)
        rest(*prev)

    for p in range(2):
        pair(p)


def start_kernel(order_ref, src_ref, q_ref, q2_ref, kv_ref, m_ref, acc_ref):
    attend(order_ref, src_ref, 0, True, (q_ref, q2_ref), kv_ref, m_ref, acc_ref)


def next_kernel(first, order_ref, src_ref, q_ref, q2_ref, kv_ref, m_in, acc_in, m_ref, acc_ref):
    m_ref[...] = m_in[...]
    acc_ref[...] = acc_in[...]
    attend(order_ref, src_ref, first, False, (q_ref, q2_ref), kv_ref, m_ref, acc_ref)


def last_kernel(
    first, order_ref, src_ref, q_ref, q2_ref, kv_ref, m_in, acc_in, keep_ref, send_ref, m_ref, acc_ref
):
    m_ref[...] = m_in[...]
    acc_ref[...] = acc_in[...]
    attend(order_ref, src_ref, first, False, (q_ref, q2_ref), kv_ref, m_ref, acc_ref)
    core = place()[1] % 2
    for ref, i in ((keep_ref, core), (send_ref, 1 - core)):
        at = pl.ds(pl.multiple_of(i * 512, 512), 512)
        for j in range(4):
            ref[j, :72, :] = acc_ref[j, :72, at]
            ref[j, 72:, :] = jnp.broadcast_to(m_ref[j, :, at], (8, 512))


def project_kernel(mine_ref, got_ref, wo_ref, wo2_ref, out_ref, heads_ref):
    for p in range(2):
        for h in range(2):
            a, b = 2 * p + h, 2 * (1 - p) + h
            ma, mb = mine_ref[a, 72:73, :], got_ref[b, 72:73, :]
            m = jnp.maximum(ma, mb)
            fa, fb = jnp.exp2(ma - m), jnp.exp2(mb - m)
            low = mine_ref[a, HD : HD + 1, :] * fa + got_ref[b, HD : HD + 1, :] * fb
            value = (mine_ref[a, :HD, :] * fa + got_ref[b, :HD, :] * fb) / low
            for k in range(2):
                both = jnp.concatenate(
                    [value[:, (2 * k + g) * 128 : (2 * k + g + 1) * 128] for g in range(2)], axis=0
                )
                col = (p * 4 + h * 2 + k) * 128
                heads_ref[:, col : col + 128] = jnp.transpose(both).astype(BF)
    half = wo_ref.shape[0]
    out = dot(heads_ref[:, :half], wo_ref[...]) + dot(heads_ref[:, half:], wo2_ref[...])
    out_ref[...] = out.astype(BF)


def fetch_kernel(*refs):
    n = (len(refs) - 1) // 2
    parts = 8
    copies = []
    for i in range(n):
        a, b = refs[i], refs[n + i]
        rows = a.shape[0] // parts
        for j in range(parts):
            at = slice(j * rows, (j + 1) * rows)
            copies.append(pltpu.make_async_copy(a.at[at], b.at[at], refs[-1].at[i, j]))
    for c in copies:
        c.start()
    for c in copies:
        c.wait()


def ffn_kernel(
    tok_ref, own_ref, other_ref, gain_ref, wg, wu, wd,
    resid_ref, keep_ref, send_ref,
    full_ref, normed_ref, acc_ref,
):
    nt = 4
    tf = wg.shape[1] // nt
    tp = place()[1]
    core = tp % 2
    rows = 64
    for b in range(2):
        att = (own_ref, other_ref)[b]
        start = pl.multiple_of((core if b == 0 else 1 - core) * HALF, HALF)
        for r in range(0, HALF, rows):
            at = pl.ds(start + r, rows)
            x = tok_ref[at, :].astype(F32) + att[r : r + rows, :].astype(F32)
            full_ref[at, :] = x
            scale = lax.rsqrt(jnp.mean(x * x, axis=-1, keepdims=True) + EPS)
            normed_ref[at, :] = (x * scale * gain_ref[...]).astype(BF)
    share = resid_ref.shape[1]
    resid_ref[...] = full_ref[:, pl.ds(pl.multiple_of(tp * share, share), share)]
    acc_ref[...] = jnp.zeros(acc_ref.shape, F32)

    def body(t, carry):
        c = pl.ds(pl.multiple_of(t * tf, tf), tf)
        gate = dot(normed_ref[...], wg[:, c])
        up = dot(normed_ref[...], wu[:, c])
        hidden = (gate / (1.0 + jnp.exp(-gate)) * up).astype(BF)
        acc_ref[...] += dot(hidden, wd[c, :])
        return carry

    lax.fori_loop(0, nt, body, 0)
    for k in range(2):
        a = pl.ds(pl.multiple_of((2 * k + core) * share, share), share)
        b = pl.ds(pl.multiple_of((2 * k + 1 - core) * share, share), share)
        keep_ref[k, :, :] = acc_ref[:, a]
        send_ref[k, :, :] = acc_ref[:, b].astype(BF)


def sum_kernel(a_ref, b_ref, out_ref):
    out_ref[...] = (a_ref[...].astype(F32) + b_ref[...].astype(F32)).astype(BF)


def sds(shape, dtype=BF):
    return jax.ShapeDtypeStruct(shape, dtype)


def index_of(z, y, x):
    return z % 4 * 8 + y % 4 * 2 + x


GRID = [(z, y, x) for z in range(4) for y in range(4) for x in range(2)]
STEPS = (1, 3, 2)
BACK = (3, 1, 2)
FLIP_X = [(index_of(z, y, x), index_of(z, y, 1 - x)) for z, y, x in GRID]
CORES = [(0, 1), (1, 0), (2, 3), (3, 2)]
CHIPS = [(0, 2), (2, 0), (1, 3), (3, 1)]


def along(second, k):
    out = []
    for z, y, x in GRID:
        for tp in range(4):
            if (tp % 2 == 0) != second:
                to = index_of(z + k, y, x)
            else:
                to = index_of(z, y + k, x)
            out.append((index_of(z, y, x) * 4 + tp, to * 4 + tp))
    return out


def arrivals(z, y, x, core):
    out = []
    for k in (0, *BACK):
        for d in (0, *STEPS):
            dz, dy = (d, k) if core == 0 else (k, d)
            for xx in (x, 1 - x):
                out.append(2 * index_of(z - dz, y - dy, xx) + core)
    return out


def stay(x):
    return pltpu.with_memory_space_constraint(x, pltpu.HBM)


def call(kernel, out, ins, outs, args, scratch=(), mib=56, flops=10**7, nbytes=MIB):
    return pl.pallas_call(
        kernel,
        out_shape=out,
        in_specs=ins,
        out_specs=outs,
        scratch_shapes=scratch,
        compiler_params=params(mib),
        cost_estimate=pl.CostEstimate(flops=flops, bytes_accessed=nbytes, transcendentals=0),
    )(*args)


def layer(tokens, order, gain_attn, gain_ffn, w_query, w_key, w_value, w_out, w_gate, w_up, w_down):
    rows, width = tokens.shape
    me, tp = place()
    chip = tp // 2
    every = ("blk", "tp")
    order = stay(order)
    table = jnp.asarray(angles())
    src = jnp.asarray(np.array([arrivals(*g, c) for g in GRID for c in range(2)], np.int32))
    src = lax.dynamic_slice_in_dim(src, 2 * me + tp % 2, 1, 0)[0]
    trig = sds((rows, 128), F32)
    half = sds((2 * HALF, 128))
    dma = pltpu.SemaphoreType.DMA

    normed, mine, send, cos, sin = call(
        kv_kernel,
        [sds((rows, width)), half, half, trig, trig],
        [SM, ANY, ANY, ANY, ANY, ANY], [VM] * 5,
        (order, stay(tokens), stay(gain_attn[None, :]), stay(w_key), stay(w_value), stay(table)),
        [
            pltpu.VMEM((2, 2 * HALF, 128), BF),
            pltpu.VMEM(tokens.shape, BF),
            pltpu.VMEM((1, width), F32),
            pltpu.VMEM((width, 256), BF),
            pltpu.VMEM(table.shape, F32),
            dma((10,)),
        ],
        mib=14,
    )
    got = lax.ppermute(send, "tp", CORES)
    one = call(pack_kernel, sds((2, 2 * HALF, 128)), [VM] * 2, VM, (mine[None], got[None]), mib=4)
    other = lax.ppermute(one, "blk", FLIP_X)
    two = call(
        pack_kernel, sds((2, 2, 2 * HALF, 128)), [VM] * 2, VM, (one[None], other[None]), mib=4
    )
    near = [lax.ppermute(two, every, along(False, k)) for k in STEPS]
    eight = call(pack_kernel, sds((8, 2, 2 * HALF, 128)), [VM] * 4, VM, (two, *near), mib=8)
    q = call(
        q_kernel, sds((2, 128, 1024)),
        [VM, ANY, VM, VM], VM,
        (normed, w_query, cos, sin),
        [pltpu.VMEM(w_query.shape, BF), dma((4,))],
        mib=16, flops=10**9, nbytes=4 * MIB,
    )
    q2 = lax.ppermute(q, "tp", CORES)
    wo2 = lax.ppermute(w_out, "tp", CORES)
    far = [lax.ppermute(eight, every, along(True, k)) for k in BACK[:2]]
    far.append(lax.ppermute(far[0], every, along(True, 3)))

    state = [sds((4, 1, 1024), F32), sds((4, 80, 1024), F32)]
    m, acc = call(
        start_kernel, state, [SM] * 2 + [VM] * 3, [VM] * 2, (order, src, q, q2, eight),
        mib=16, flops=2 * 10**9, nbytes=2 * MIB,
    )
    for j in range(2):
        m, acc = call(
            functools.partial(next_kernel, 8 * (j + 1)), state,
            [SM] * 2 + [VM] * 5, [VM] * 2, (order, src, q, q2, far[j], m, acc),
            mib=16, flops=2 * 10**9, nbytes=2 * MIB,
        )
    keep, send = call(
        functools.partial(last_kernel, 24), [sds((4, 80, 512), F32)] * 2,
        [SM] * 2 + [VM] * 5, [VM] * 2, (order, src, q, q2, far[2], m, acc),
        [pltpu.VMEM(s.shape, F32) for s in state],
        mib=16, flops=2 * 10**9, nbytes=2 * MIB,
    )
    got = lax.ppermute(send, "tp", CORES)
    here = call(
        project_kernel, sds((HALF, width)), [VM] * 4, VM, (keep, got, w_out, wo2),
        [pltpu.VMEM((HALF, 2 * w_out.shape[0]), BF)],
        mib=16, flops=10**9, nbytes=4 * MIB,
    )
    there = lax.ppermute(here, "tp", CHIPS)
    weights = (w_gate, w_up, w_down)
    weights = call(
        fetch_kernel, [sds(w.shape) for w in weights], [ANY] * 3, [VM] * 3,
        tuple(stay(w) for w in weights), [dma((3, 8))], mib=2, nbytes=24 * MIB,
    )
    weights = [pltpu.with_memory_space_constraint(w, pltpu.VMEM) for w in weights]
    own = call(sum_kernel, sds((HALF, width)), [VM] * 2, VM, (here, there), mib=4)
    other = lax.ppermute(own, "tp", CORES)

    share = width // lax.axis_size("tp")
    resid, keep, send = call(
        ffn_kernel,
        [sds((rows, share), F32), sds((2, rows, share), F32), sds((2, rows, share))],
        [VM] * 7, [VM] * 3,
        (tokens, own, other, gain_ffn[None, :], *weights),
        [
            pltpu.VMEM((rows, width), F32),
            pltpu.VMEM((rows, width), BF),
            pltpu.VMEM((rows, width), F32),
        ],
        mib=16, flops=7 * 10**9, nbytes=24 * MIB,
    )
    both = keep + lax.ppermute(send, "tp", CORES).astype(F32)
    mine = lax.dynamic_index_in_dim(both, chip, 0, keepdims=False)
    away = lax.dynamic_index_in_dim(both, 1 - chip, 0, keepdims=False).astype(BF)
    feed = mine + lax.ppermute(away, "tp", CHIPS).astype(F32)
    return (resid + feed).astype(BF)


def solution(mesh):
    placed = (
        P("blk", None),
        P(),
        P(),
        P(),
        P(None, "tp"),
        P(None, "tp"),
        P(None, "tp"),
        P("tp", None),
        P(None, "tp"),
        P(None, "tp"),
        P("tp", None),
    )
    return jax.shard_map(
        layer, mesh=mesh, in_specs=placed, out_specs=P("blk", "tp"), check_vma=False
    )
```

time: 277 us -> 118 us (0.43)
  waiting for transfers between devices: 136 us -> 37.4 us
  matrix products: 59 us -> 0 us
  Pallas kernels: 0 us -> 49.8 us
  local copies, waits for them, and re-layouts: 32 us -> 2.34 us
  other arithmetic: 29.5 us -> 1 us
  starting transfers between devices: 3.55 us -> 26.8 us
  between operations: 13.6 us -> 0.19 us
    all_gather x2 -> x0, waiting for transfers between devices: 123 us -> none  [the longest x1 75.9 us: local(): piece = lax.all_gather(packed, 'blk', axis=0, tiled=True)]
    dot_general x38 -> x0, matrix products: 59 us -> none  [the longest x16 20.3 us: attend(): jnp.einsum('kgqs,skd->kgqd', weights.astype(jnp.bfloat16), value_block, p...]
    pallas_call x0 -> x13, Pallas kernels: none -> 49.8 us  [call(): pl.pallas_call(kernel, out_shape=out, in_specs=ins, out_specs=outs, scrat...]
    ppermute x0 -> x15, waiting for transfers between devices: none -> 37.4 us  [the longest x1 11.9 us: layer(): there = lax.ppermute(here, 'tp', CHIPS)]
    ppermute x0 -> x15, starting transfers between devices: none -> 26.8 us  [the longest x2 4.88 us: layer(): got = lax.ppermute(send, 'tp', CORES)]
    reduce_sum x22 -> x0, other arithmetic: 22.8 us -> none  [the longest x16 16.1 us: attend(): denominator = denominator * factor + jnp.sum(weights, axis=-1)]
    slice x16 -> x0, local copies, waits for them, and re-layouts: 15.9 us -> none  [attend(): value_block = block[:, kv_local * HD:].reshape(-1, kv_local, HD)]
    all_to_all x1 -> x0, waiting for transfers between devices: 13 us -> none  [sum_at_owner(): parts = lax.all_to_all(in_blocks(shard, dim, peers), axis, 0, 0, tiled=True)]
  transfers between devices with their start and end apart: 3 -> 15, of which waited for: 3 -> 10; matrix products, arithmetic and copies ran while one was open for 1% -> 1% of each run, Pallas kernels for 0% -> 32%
where the time goes in v1:
time: 118 us; the launch traced here: 117 us
  Pallas kernels  49.8 us (42%)
  waiting for transfers between devices  37.4 us (32%)
  starting transfers between devices  26.8 us (23%)
  local copies, waits for them, and re-layouts  2.34 us (2%)
    pallas_call x13, Pallas kernels, call(): pl.pallas_call(kernel, out_shape=out, in_specs=ins, out_specs=outs, scrat...  49.8 us
    ppermute x1, waiting for transfers between devices, layer(): there = lax.ppermute(here, 'tp', CHIPS)  11.9 us
    ppermute x1, waiting for transfers between devices, layer(): feed = mine + lax.ppermute(away, 'tp', CHIPS).astype(F32)  6.49 us
    ppermute x3, waiting for transfers between devices, layer(): near = [lax.ppermute(two, every, along(False, k)) for k in STEPS]  6.04 us
    ppermute x2, waiting for transfers between devices, layer(): far = [lax.ppermute(eight, every, along(True, k)) for k in BACK[:2]]  5.16 us
    ppermute x2, starting transfers between devices, layer(): got = lax.ppermute(send, 'tp', CORES)  4.88 us
    ppermute x3, starting transfers between devices, layer(): near = [lax.ppermute(two, every, along(False, k)) for k in STEPS]  4.57 us
    ppermute x2, starting transfers between devices, layer(): far = [lax.ppermute(eight, every, along(True, k)) for k in BACK[:2]]  4.17 us
  transfers between devices with their start and end apart: 15, of which 10 were waited for; matrix products, arithmetic and copies ran while one was open for 1% of the time, Pallas kernels for 32%

profile of v1, /device:TPU:1, one launch (start us, length us, event | category | flops | bytes accessed | tf_op | source)
XLA Modules:
  0.0 117.5 jit_solution(1882132294146726665)
XLA Ops:
  0.0 3.0 %shard_map.127 = (bf16[256,2048]{1,0:T(8,128)(2,1)S(1)}, bf16[256,128]{1,0:T(8,128)(2,1)S(1)}, bf16[256,128]{1,0:T(8,128)(2,1)S(1)}, f32[256,128]{1,0:T(8,128)S(1)}, f32[256,128]{1,0:T(8,128)S(1)}) custom-call(s32[64]{0:T(128)} %order_ref.9, bf16[256,2048]{1,0:T(8,128)(2,1)} %tok_ref.1, f32[1,2048]{1,0:T(1,128)} %bitcast.21, bf16[2048,128]{1,0:T(8,128)(2,1)} %wk_hbm.1, ...), custom_call_target="tpu_custom_call" | custom-call | flops 10000000 | bytes 1048576 | tf_op jit(solution)/shard_map/pallas_call | solution.py:343
  3.0 1.5 %collective-permute-start.1 = (bf16[256,128]{1,0:T(8,128)(2,1)S(1)}, bf16[256,128]{1,0:T(8,128)(2,1)S(1)}, u32[]{:S(2)}, u32[]{:S(2)}) collective-permute-start(bf16[256,128]{1,0:T(8,128)(2,1)S(1)} %get-tuple-element.28), channel_id=1, source_target_pairs={{0,1},{1,0},{2,3},{3,2},{4,5},{5,4},{6,7},{7,6},{8,9},{9,8},{10,11... | collective-permute-start | bytes 196616 | tf_op jit(solution)/shard_map/ppermute | solution.py:382
  4.5 0.9 collective-permute-done.1
  5.4 2.9 %collective-permute-start.2 = (bf16[2,256,128]{2,1,0:T(8,128)(2,1)S(1)}, bf16[2,256,128]{2,1,0:T(8,128)(2,1)S(1)}, u32[]{:S(2)}, u32[]{:S(2)}) collective-permute-start(bf16[2,256,128]{2,1,0:T(8,128)(2,1)S(1)} %shard_map.129), channel_id=1, source_target_pairs={{0,4},{4,0},{8,12},{12,8},{16,20},{20,16},{24,28},{28,24},{32,36},... | collective-permute-start | bytes 393224 | tf_op jit(solution)/shard_map/ppermute | solution.py:384
  8.3 3.3 %collective-permute-done.2 = bf16[2,256,128]{2,1,0:T(8,128)(2,1)S(1)} collective-permute-done((bf16[2,256,128]{2,1,0:T(8,128)(2,1)S(1)}, bf16[2,256,128]{2,1,0:T(8,128)(2,1)S(1)}, u32[]{:S(2)}, u32[]{:S(2)}) %collective-permute-start.2) | collective-permute-done | bytes 131104 | tf_op jit(solution)/shard_map/ppermute | solution.py:384
  11.7 3.1 %collective-permute-start.5 = (bf16[2,2,256,128]{3,2,1,0:T(8,128)(2,1)S(1)}, bf16[2,2,256,128]{3,2,1,0:T(8,128)(2,1)S(1)}, u32[]{:S(2)}, u32[]{:S(2)}) collective-permute-start(bf16[2,2,256,128]{3,2,1,0:T(8,128)(2,1)S(1)} %shard_map.130.refs_0_), channel_id=1, source_target_pairs={{0,64},{1,17},{2,66},{3,19},{4,68},{5,21},{6,70},{7,23},{8,72},{9,... | collective-permute-start | bytes 786440 | tf_op jit(solution)/shard_map/ppermute | solution.py:388
  14.8 0.8 collective-permute-start.4
  15.6 0.7 collective-permute-start.3
  16.3 2.6 %collective-permute-done.5.refs_3_ = bf16[2,2,256,128]{3,2,1,0:T(8,128)(2,1)S(1)} collective-permute-done((bf16[2,2,256,128]{3,2,1,0:T(8,128)(2,1)S(1)}, bf16[2,2,256,128]{3,2,1,0:T(8,128)(2,1)S(1)}, u32[]{:S(2)}, u32[]{:S(2)}) %collective-permute-start.5) | collective-permute-done | bytes 262176 | tf_op jit(solution)/shard_map/ppermute | solution.py:388
  18.9 3.2 %collective-permute-done.4.refs_2_ = bf16[2,2,256,128]{3,2,1,0:T(8,128)(2,1)S(1)} collective-permute-done((bf16[2,2,256,128]{3,2,1,0:T(8,128)(2,1)S(1)}, bf16[2,2,256,128]{3,2,1,0:T(8,128)(2,1)S(1)}, u32[]{:S(2)}, u32[]{:S(2)}) %collective-permute-start.4) | collective-permute-done | bytes 262176 | tf_op jit(solution)/shard_map/ppermute | solution.py:388
  22.4 3.8 %collective-permute-start.6 = (bf16[8,2,256,128]{3,2,1,0:T(8,128)(2,1)S(1)}, bf16[8,2,256,128]{3,2,1,0:T(8,128)(2,1)}, u32[]{:S(2)}, u32[]{:S(2)}) collective-permute-start(bf16[8,2,256,128]{3,2,1,0:T(8,128)(2,1)S(1)} %shard_map.131.kv_ref), channel_id=1, source_target_pairs={{0,24},{1,97},{2,26},{3,99},{4,28},{5,101},{6,30},{7,103},{8,0},{9... | collective-permute-start | bytes 3145736 | tf_op jit(solution)/shard_map/ppermute | solution.py:399
  26.2 2.5 %collective-permute-start.10 = (bf16[512,2048]{1,0:T(8,128)(2,1)}, bf16[512,2048]{1,0:T(8,128)(2,1)S(1)}, u32[]{:S(2)}, u32[]{:S(2)}) collective-permute-start(bf16[512,2048]{1,0:T(8,128)(2,1)} %wo_ref.1), channel_id=1, source_target_pairs={{0,1},{1,0},{2,3},{3,2},{4,5},{5,4},{6,7},{7,6},{8,9},{9,8},{10,11... | collective-permute-start | bytes 6291464 | tf_op jit(solution)/shard_map/ppermute | solution.py:398
  29.0 1.6 %copy-done.2 = bf16[2048,512]{1,0:T(8,128)(2,1)S(1)} copy-done((bf16[2048,512]{1,0:T(8,128)(2,1)S(1)}, bf16[2048,512]{1,0:T(8,128)(2,1)}, u32[]{:S(2)}) %copy-start.2) | copy-done | bytes 2097176
  30.6 2.1 %shard_map.128.q_ref = bf16[2,128,1024]{2,1,0:T(8,128)(2,1)} custom-call(bf16[256,2048]{1,0:T(8,128)(2,1)S(1)} %get-tuple-element.24.normed_ref, bf16[2048,512]{1,0:T(8,128)(2,1)S(1)} %copy-done.2, f32[256,128]{1,0:T(8,128)S(1)} %get-tuple-element.25.cos_ref, f32[256,128]{1,0:T(8,128)S(1)} %get-tuple-element.26.sin_ref), custom_call_target="tpu_custom_call" | custom-call | flops 1000000000 | bytes 4194304 | tf_op jit(solution)/shard_map/pallas_call | solution.py:343
  32.8 5.2 %collective-permute-done.6.kv_ref = bf16[8,2,256,128]{3,2,1,0:T(8,128)(2,1)} collective-permute-done((bf16[8,2,256,128]{3,2,1,0:T(8,128)(2,1)S(1)}, bf16[8,2,256,128]{3,2,1,0:T(8,128)(2,1)}, u32[]{:S(2)}, u32[]{:S(2)}) %collective-permute-start.6) | collective-permute-done | bytes 1048608 | tf_op jit(solution)/shard_map/ppermute | solution.py:399
  37.9 3.5 %collective-permute-start.7 = (bf16[8,2,256,128]{3,2,1,0:T(8,128)(2,1)}, bf16[8,2,256,128]{3,2,1,0:T(8,128)(2,1)}, u32[]{:S(2)}, u32[]{:S(2)}) collective-permute-start(bf16[8,2,256,128]{3,2,1,0:T(8,128)(2,1)} %collective-permute-done.6.kv_ref), channel_id=1, source_target_pairs={{0,24},{1,97},{2,26},{3,99},{4,28},{5,101},{6,30},{7,103},{8,0},{9... | collective-permute-start | bytes 3145736 | tf_op jit(solution)/shard_map/ppermute | solution.py:400
  42.2 6.5 %shard_map.132 = (f32[4,1,1024]{2,1,0:T(1,128)S(1)}, f32[4,80,1024]{2,1,0:T(8,128)S(1)}) custom-call(s32[64]{0:T(128)} %order_ref.9, s32[32]{0:T(128)S(1)} %fusion.3.src_ref, bf16[2,128,1024]{2,1,0:T(8,128)(2,1)} %shard_map.128.q_ref, bf16[2,128,1024]{2,1,0:T(8,128)(2,1)} %collective-permute-done.q2_ref, bf16[8,2,256,128]{3,2,1,0:T(8,128)(2,1)S(1)} %shard_map.131.kv_ref), custom_call_target="tpu_custom_call" | custom-call | flops 2000000000 | bytes 2097152 | tf_op jit(solution)/shard_map/pallas_call | solution.py:343
  48.6 6.6 %shard_map.133 = (f32[4,1,1024]{2,1,0:T(1,128)S(1)}, f32[4,80,1024]{2,1,0:T(8,128)S(1)}) custom-call(s32[64]{0:T(128)} %order_ref.9, s32[32]{0:T(128)S(1)} %fusion.3.src_ref, bf16[2,128,1024]{2,1,0:T(8,128)(2,1)} %shard_map.128.q_ref, bf16[2,128,1024]{2,1,0:T(8,128)(2,1)} %collective-permute-done.q2_ref, ...), custom_call_target="tpu_custom_call" | custom-call | flops 2000000000 | bytes 2097152 | tf_op jit(solution)/shard_map/pallas_call | solution.py:343
  55.2 6.9 %shard_map.134 = (f32[4,1,1024]{2,1,0:T(1,128)S(1)}, f32[4,80,1024]{2,1,0:T(8,128)S(1)}) custom-call(s32[64]{0:T(128)} %order_ref.9, s32[32]{0:T(128)S(1)} %fusion.3.src_ref, bf16[2,128,1024]{2,1,0:T(8,128)(2,1)} %shard_map.128.q_ref, bf16[2,128,1024]{2,1,0:T(8,128)(2,1)} %collective-permute-done.q2_ref, ...), custom_call_target="tpu_custom_call" | custom-call | flops 2000000000 | bytes 2097152 | tf_op jit(solution)/shard_map/pallas_call | solution.py:343
  62.2 6.7 %shard_map.135 = (f32[4,80,512]{2,1,0:T(8,128)S(1)}, f32[4,80,512]{2,1,0:T(8,128)S(1)}) custom-call(s32[64]{0:T(128)} %order_ref.9, s32[32]{0:T(128)S(1)} %fusion.3.src_ref, bf16[2,128,1024]{2,1,0:T(8,128)(2,1)} %shard_map.128.q_ref, bf16[2,128,1024]{2,1,0:T(8,128)(2,1)} %collective-permute-done.q2_ref, ...), custom_call_target="tpu_custom_call" | custom-call | flops 2000000000 | bytes 2097152 | tf_op jit(solution)/shard_map/pallas_call | solution.py:343
  68.9 3.4 %collective-permute-start.9 = (f32[4,80,512]{2,1,0:T(8,128)S(1)}, f32[4,80,512]{2,1,0:T(8,128)S(1)}, u32[]{:S(2)}, u32[]{:S(2)}) collective-permute-start(f32[4,80,512]{2,1,0:T(8,128)S(1)} %get-tuple-element.36), channel_id=1, source_target_pairs={{0,1},{1,0},{2,3},{3,2},{4,5},{5,4},{6,7},{7,6},{8,9},{9,8},{10,11... | collective-permute-start | bytes 1966088 | tf_op jit(solution)/shard_map/ppermute | solution.py:419
  72.3 1.7 %collective-permute-done.9.got_ref = f32[4,80,512]{2,1,0:T(8,128)S(1)} collective-permute-done((f32[4,80,512]{2,1,0:T(8,128)S(1)}, f32[4,80,512]{2,1,0:T(8,128)S(1)}, u32[]{:S(2)}, u32[]{:S(2)}) %collective-permute-start.9) | collective-permute-done | bytes 655392 | tf_op jit(solution)/shard_map/ppermute | solution.py:419
  74.1 0.8 shard_map.136.a_ref
  74.9 1.3 %collective-permute-start.11 = (bf16[128,2048]{1,0:T(8,128)(2,1)S(1)}, bf16[128,2048]{1,0:T(8,128)(2,1)S(1)}, u32[]{:S(2)}, u32[]{:S(2)}) collective-permute-start(bf16[128,2048]{1,0:T(8,128)(2,1)S(1)} %shard_map.136.a_ref), channel_id=1, source_target_pairs={{0,2},{2,0},{1,3},{3,1},{4,6},{6,4},{5,7},{7,5},{8,10},{10,8},{9,1... | collective-permute-start | bytes 1572872 | tf_op jit(solution)/shard_map/ppermute | solution.py:425
  76.2 11.9 %collective-permute-done.11.b_ref = bf16[128,2048]{1,0:T(8,128)(2,1)S(1)} collective-permute-done((bf16[128,2048]{1,0:T(8,128)(2,1)S(1)}, bf16[128,2048]{1,0:T(8,128)(2,1)S(1)}, u32[]{:S(2)}, u32[]{:S(2)}) %collective-permute-start.11) | collective-permute-done | bytes 524320 | tf_op jit(solution)/shard_map/ppermute | solution.py:425
  88.2 1.3 %collective-permute-start.12 = (bf16[128,2048]{1,0:T(8,128)(2,1)S(1)}, bf16[128,2048]{1,0:T(8,128)(2,1)S(1)}, u32[]{:S(2)}, u32[]{:S(2)}) collective-permute-start(bf16[128,2048]{1,0:T(8,128)(2,1)S(1)} %shard_map.137.own_ref), channel_id=1, source_target_pairs={{0,1},{1,0},{2,3},{3,2},{4,5},{5,4},{6,7},{7,6},{8,9},{9,8},{10,11... | collective-permute-start | bytes 1572872 | tf_op jit(solution)/shard_map/ppermute | solution.py:433
  89.5 8.4 %shard_map.138 = (bf16[2048,2048]{1,0:T(8,128)(2,1)S(1)}, bf16[2048,2048]{1,0:T(8,128)(2,1)S(1)}, bf16[2048,2048]{1,0:T(8,128)(2,1)S(1)}) custom-call(bf16[2048,2048]{1,0:T(8,128)(2,1)} %refs_0_.1, bf16[2048,2048]{1,0:T(8,128)(2,1)} %refs_1_.1, bf16[2048,2048]{1,0:T(8,128)(2,1)} %refs_2_.1), custom_call_target="tpu_custom_call" | custom-call | flops 10000000 | bytes 25165824 | tf_op jit(solution)/shard_map/pallas_call | solution.py:343
  98.0 8.7 %shard_map.139 = (f32[256,512]{1,0:T(8,128)S(1)}, f32[2,256,512]{2,1,0:T(8,128)S(1)}, bf16[2,256,512]{2,1,0:T(8,128)(2,1)S(1)}) custom-call(bf16[256,2048]{1,0:T(8,128)(2,1)S(1)} %copy-done, bf16[128,2048]{1,0:T(8,128)(2,1)S(1)} %shard_map.137.own_ref, bf16[128,2048]{1,0:T(8,128)(2,1)S(1)} %collective-permute-done.12.other_ref, f32[1,2048]{1,0:T(1,128)S(1)} %bitcast.20, ...), custom_call_target="tpu_custom_call" | custom-call | flops 7000000000 | bytes 25165824 | tf_op jit(solution)/shard_map/pallas_call | solution.py:343
  106.8 1.8 %collective-permute-done.13 = bf16[2,256,512]{2,1,0:T(8,128)(2,1)S(1)} collective-permute-done((bf16[2,256,512]{2,1,0:T(8,128)(2,1)S(1)}, bf16[2,256,512]{2,1,0:T(8,128)(2,1)S(1)}, u32[]{:S(2)}, u32[]{:S(2)}) %collective-permute-start.13) | collective-permute-done | bytes 524320 | tf_op jit(solution)/shard_map/ppermute | solution.py:448
  108.8 1.3 %collective-permute-start.14 = (bf16[256,512]{1,0:T(8,128)(2,1)S(1)}, bf16[256,512]{1,0:T(8,128)(2,1)S(1)}, u32[]{:S(2)}, u32[]{:S(2)}) collective-permute-start(bf16[256,512]{1,0:T(8,128)(2,1)S(1)} %fusion.2), channel_id=1, source_target_pairs={{0,2},{2,0},{1,3},{3,1},{4,6},{6,4},{5,7},{7,5},{8,10},{10,8},{9,1... | collective-permute-start | bytes 786440 | tf_op jit(solution)/shard_map/ppermute | solution.py:451
  110.2 6.5 %collective-permute-done.14 = bf16[256,512]{1,0:T(8,128)(2,1)S(1)} collective-permute-done((bf16[256,512]{1,0:T(8,128)(2,1)S(1)}, bf16[256,512]{1,0:T(8,128)(2,1)S(1)}, u32[]{:S(2)}, u32[]{:S(2)}) %collective-permute-start.14) | collective-permute-done | bytes 262176 | tf_op jit(solution)/shard_map/ppermute | solution.py:451
  116.7 0.8 fusion.1
  (23 shorter events, 2.0 us)
Async XLA Ops:
  3.0 2.4 %collective-permute-start.1 = (bf16[256,128]{1,0:T(8,128)(2,1)S(1)}, bf16[256,128]{1,0:T(8,128)(2,1)S(1)}, u32[]{:S(2)}, u32[]{:S(2)}) collective-permute-start(bf16[256,128]{1,0:T(8,128)(2,1)S(1)} %get-tuple-element.28), channel_id=1, source_target_pairs={{0,1},{1,0},{2,3},{3,2},{4,5},{5,4},{6,7},{7,6},{8,9},{9,8},{10,11... | collective-permute-start | bytes 196616 | tf_op jit(solution)/shard_map/ppermute | solution.py:382
  5.4 6.3 %collective-permute-start.2 = (bf16[2,256,128]{2,1,0:T(8,128)(2,1)S(1)}, bf16[2,256,128]{2,1,0:T(8,128)(2,1)S(1)}, u32[]{:S(2)}, u32[]{:S(2)}) collective-permute-start(bf16[2,256,128]{2,1,0:T(8,128)(2,1)S(1)} %shard_map.129), channel_id=1, source_target_pairs={{0,4},{4,0},{8,12},{12,8},{16,20},{20,16},{24,28},{28,24},{32,36},... | collective-permute-start | bytes 393224 | tf_op jit(solution)/shard_map/ppermute | solution.py:384
  11.7 7.2 %collective-permute-start.5 = (bf16[2,2,256,128]{3,2,1,0:T(8,128)(2,1)S(1)}, bf16[2,2,256,128]{3,2,1,0:T(8,128)(2,1)S(1)}, u32[]{:S(2)}, u32[]{:S(2)}) collective-permute-start(bf16[2,2,256,128]{3,2,1,0:T(8,128)(2,1)S(1)} %shard_map.130.refs_0_), channel_id=1, source_target_pairs={{0,64},{1,17},{2,66},{3,19},{4,68},{5,21},{6,70},{7,23},{8,72},{9,... | collective-permute-start | bytes 786440 | tf_op jit(solution)/shard_map/ppermute | solution.py:388
  14.8 7.3 %collective-permute-start.4 = (bf16[2,2,256,128]{3,2,1,0:T(8,128)(2,1)S(1)}, bf16[2,2,256,128]{3,2,1,0:T(8,128)(2,1)S(1)}, u32[]{:S(2)}, u32[]{:S(2)}) collective-permute-start(bf16[2,2,256,128]{3,2,1,0:T(8,128)(2,1)S(1)} %shard_map.130.refs_0_), channel_id=1, source_target_pairs={{0,96},{1,25},{2,98},{3,27},{4,100},{5,29},{6,102},{7,31},{8,104},... | collective-permute-start | bytes 786440 | tf_op jit(solution)/shard_map/ppermute | solution.py:388
  15.6 6.7 %collective-permute-start.3 = (bf16[2,2,256,128]{3,2,1,0:T(8,128)(2,1)S(1)}, bf16[2,2,256,128]{3,2,1,0:T(8,128)(2,1)S(1)}, u32[]{:S(2)}, u32[]{:S(2)}) collective-permute-start(bf16[2,2,256,128]{3,2,1,0:T(8,128)(2,1)S(1)} %shard_map.130.refs_0_), channel_id=1, source_target_pairs={{0,32},{1,9},{2,34},{3,11},{4,36},{5,13},{6,38},{7,15},{8,40},{9,1... | collective-permute-start | bytes 786440 | tf_op jit(solution)/shard_map/ppermute | solution.py:388
  22.4 15.6 %collective-permute-start.6 = (bf16[8,2,256,128]{3,2,1,0:T(8,128)(2,1)S(1)}, bf16[8,2,256,128]{3,2,1,0:T(8,128)(2,1)}, u32[]{:S(2)}, u32[]{:S(2)}) collective-permute-start(bf16[8,2,256,128]{3,2,1,0:T(8,128)(2,1)S(1)} %shard_map.131.kv_ref), channel_id=1, source_target_pairs={{0,24},{1,97},{2,26},{3,99},{4,28},{5,101},{6,30},{7,103},{8,0},{9... | collective-permute-start | bytes 3145736 | tf_op jit(solution)/shard_map/ppermute | solution.py:399
  26.2 46.1 %collective-permute-start.10 = (bf16[512,2048]{1,0:T(8,128)(2,1)}, bf16[512,2048]{1,0:T(8,128)(2,1)S(1)}, u32[]{:S(2)}, u32[]{:S(2)}) collective-permute-start(bf16[512,2048]{1,0:T(8,128)(2,1)} %wo_ref.1), channel_id=1, source_target_pairs={{0,1},{1,0},{2,3},{3,2},{4,5},{5,4},{6,7},{7,6},{8,9},{9,8},{10,11... | collective-permute-start | bytes 6291464 | tf_op jit(solution)/shard_map/ppermute | solution.py:398
  28.7 26.5 %collective-permute-start.8 = (bf16[8,2,256,128]{3,2,1,0:T(8,128)(2,1)S(1)}, bf16[8,2,256,128]{3,2,1,0:T(8,128)(2,1)}, u32[]{:S(2)}, u32[]{:S(2)}) collective-permute-start(bf16[8,2,256,128]{3,2,1,0:T(8,128)(2,1)S(1)} %shard_map.131.kv_ref), channel_id=1, source_target_pairs={{0,8},{1,33},{2,10},{3,35},{4,12},{5,37},{6,14},{7,39},{8,16},{9,4... | collective-permute-start | bytes 3145736 | tf_op jit(solution)/shard_map/ppermute | solution.py:399
  29.0 1.6 %copy-start.2 = (bf16[2048,512]{1,0:T(8,128)(2,1)S(1)}, bf16[2048,512]{1,0:T(8,128)(2,1)}, u32[]{:S(2)}) copy-start(bf16[2048,512]{1,0:T(8,128)(2,1)} %wq_hbm.1) | copy-start | bytes 6291460
  32.7 9.5 %collective-permute-start = (bf16[2,128,1024]{2,1,0:T(8,128)(2,1)}, bf16[2,128,1024]{2,1,0:T(8,128)(2,1)}, u32[]{:S(2)}, u32[]{:S(2)}) collective-permute-start(bf16[2,128,1024]{2,1,0:T(8,128)(2,1)} %shard_map.128.q_ref), channel_id=1, source_target_pairs={{0,1},{1,0},{2,3},{3,2},{4,5},{5,4},{6,7},{7,6},{8,9},{9,8},{10,11... | collective-permute-start | bytes 1572872 | tf_op jit(solution)/shard_map/ppermute | solution.py:397
  37.9 24.2 %collective-permute-start.7 = (bf16[8,2,256,128]{3,2,1,0:T(8,128)(2,1)}, bf16[8,2,256,128]{3,2,1,0:T(8,128)(2,1)}, u32[]{:S(2)}, u32[]{:S(2)}) collective-permute-start(bf16[8,2,256,128]{3,2,1,0:T(8,128)(2,1)} %collective-permute-done.6.kv_ref), channel_id=1, source_target_pairs={{0,24},{1,97},{2,26},{3,99},{4,28},{5,101},{6,30},{7,103},{8,0},{9... | collective-permute-start | bytes 3145736 | tf_op jit(solution)/shard_map/ppermute | solution.py:400
  55.2 18.9 %copy-start.1 = (bf16[512,2048]{1,0:T(8,128)(2,1)S(1)}, bf16[512,2048]{1,0:T(8,128)(2,1)}, u32[]{:S(2)}) copy-start(bf16[512,2048]{1,0:T(8,128)(2,1)} %wo_ref.1) | copy-start | bytes 6291460
  68.9 5.2 %collective-permute-start.9 = (f32[4,80,512]{2,1,0:T(8,128)S(1)}, f32[4,80,512]{2,1,0:T(8,128)S(1)}, u32[]{:S(2)}, u32[]{:S(2)}) collective-permute-start(f32[4,80,512]{2,1,0:T(8,128)S(1)} %get-tuple-element.36), channel_id=1, source_target_pairs={{0,1},{1,0},{2,3},{3,2},{4,5},{5,4},{6,7},{7,6},{8,9},{9,8},{10,11... | collective-permute-start | bytes 1966088 | tf_op jit(solution)/shard_map/ppermute | solution.py:419
  74.9 13.2 %collective-permute-start.11 = (bf16[128,2048]{1,0:T(8,128)(2,1)S(1)}, bf16[128,2048]{1,0:T(8,128)(2,1)S(1)}, u32[]{:S(2)}, u32[]{:S(2)}) collective-permute-start(bf16[128,2048]{1,0:T(8,128)(2,1)S(1)} %shard_map.136.a_ref), channel_id=1, source_target_pairs={{0,2},{2,0},{1,3},{3,1},{4,6},{6,4},{5,7},{7,5},{8,10},{10,8},{9,1... | collective-permute-start | bytes 1572872 | tf_op jit(solution)/shard_map/ppermute | solution.py:425
  88.2 9.7 %copy-start = (bf16[256,2048]{1,0:T(8,128)(2,1)S(1)}, bf16[256,2048]{1,0:T(8,128)(2,1)}, u32[]{:S(2)}) copy-start(bf16[256,2048]{1,0:T(8,128)(2,1)} %tok_ref.1) | copy-start | bytes 3145732
  88.2 9.7 %copy-start.3 = (f32[2048]{0:T(1024)S(1)}, f32[2048]{0:T(1024)}, u32[]{:S(2)}) copy-start(f32[2048]{0:T(1024)} %param.16) | copy-start | bytes 24580
  88.2 9.7 %collective-permute-start.12 = (bf16[128,2048]{1,0:T(8,128)(2,1)S(1)}, bf16[128,2048]{1,0:T(8,128)(2,1)S(1)}, u32[]{:S(2)}, u32[]{:S(2)}) collective-permute-start(bf16[128,2048]{1,0:T(8,128)(2,1)S(1)} %shard_map.137.own_ref), channel_id=1, source_target_pairs={{0,1},{1,0},{2,3},{3,2},{4,5},{5,4},{6,7},{7,6},{8,9},{9,8},{10,11... | collective-permute-start | bytes 1572872 | tf_op jit(solution)/shard_map/ppermute | solution.py:433
  106.6 2.0 %collective-permute-start.13 = (bf16[2,256,512]{2,1,0:T(8,128)(2,1)S(1)}, bf16[2,256,512]{2,1,0:T(8,128)(2,1)S(1)}, u32[]{:S(2)}, u32[]{:S(2)}) collective-permute-start(bf16[2,256,512]{2,1,0:T(8,128)(2,1)S(1)} %get-tuple-element.42), channel_id=1, source_target_pairs={{0,1},{1,0},{2,3},{3,2},{4,5},{5,4},{6,7},{7,6},{8,9},{9,8},{10,11... | collective-permute-start | bytes 1572872 | tf_op jit(solution)/shard_map/ppermute | solution.py:448
  108.8 7.8 %collective-permute-start.14 = (bf16[256,512]{1,0:T(8,128)(2,1)S(1)}, bf16[256,512]{1,0:T(8,128)(2,1)S(1)}, u32[]{:S(2)}, u32[]{:S(2)}) collective-permute-start(bf16[256,512]{1,0:T(8,128)(2,1)S(1)} %fusion.2), channel_id=1, source_target_pairs={{0,2},{2,0},{1,3},{3,1},{4,6},{6,4},{5,7},{7,5},{8,10},{10,8},{9,1... | collective-permute-start | bytes 786440 | tf_op jit(solution)/shard_map/ppermute | solution.py:451

commit v2 on v1

--- a/solution.py
+++ b/solution.py
@@ -13,6 +13,7 @@
 HD = 64
 EPS = 1e-05
 ROPE_BASE = 500000.0
+COLUMNS = (0, 1, 3, 2)
 NEG = -1e30
 HIDDEN = -2e30
 HALF = 128
@@ -142,74 +143,81 @@
                 ]
 
 
-def attend(order_ref, src_ref, first, own, q_refs, kv_ref, m_ref, acc_ref):
+def attend(order_ref, blocks, own, q_refs, m_ref, acc_ref):
     me, tp = place()
     core = tp % 2
     width = 256
-    group = kv_ref.shape[0]
     pq = [order_ref[2 * me + i] for i in range(2)]
-    pos = [order_ref[src_ref[first + g]] for g in range(group)]
+    z, y, x = me // 8, me // 2 % 4, me % 2
+    pos = []
+    for _, _, d, k, flip in blocks:
+        zz = (z + 4 - jnp.where(core == 0, d, k)) % 4
+        yy = (y + 4 - jnp.where(core == 0, k, d)) % 4
+        xx = 1 - x if flip else x
+        pos.append(order_ref[2 * (zz * 8 + yy * 2 + xx) + core])
     adds = [[jnp.where(p < q, jnp.float32(0.0), jnp.float32(HIDDEN)) for p in pos] for q in pq]
     if own:
         key = lax.broadcasted_iota(jnp.int32, (HALF, width), 0)
         tok = lax.broadcasted_iota(jnp.int32, (HALF, width), 1) % HALF
         tri = jnp.where(key <= tok, 0.0, HIDDEN).astype(F32)
 
-    def pair(p):
-        q_ref = q_refs[p]
-        k_all = jnp.concatenate([kv_ref[g, p, :HALF, :] for g in range(group)], axis=0)
-
-        def rest(h, t, s):
-            sl = slice(t * width, (t + 1) * width)
-            i = t * width // 512
-            add = adds[i]
-            parts = [s[g * HALF : (g + 1) * HALF] for g in range(group)]
-            if own:
-                parts[0] = parts[0] + jnp.where(core == i, tri, add[0])
-                add = [jnp.float32(0.0), *add[1:]]
-            m_old = jnp.full((1, width), NEG, F32) if own else m_ref[2 * p + h, :, sl]
-            m_new = m_old
-            for x, b in zip(parts, add):
-                m_new = jnp.maximum(m_new, jnp.max(x, axis=0, keepdims=True) + b)
-            e = [jnp.exp2(x + (b - m_new)).astype(BF) for x, b in zip(parts, add)]
-            vt = [kv_ref[g, p, HALF + h * HD : HALF + (h + 1) * HD, :] for g in range(group)]
-            vt = jnp.concatenate(vt, axis=1)
-            vt = jnp.concatenate([vt, jnp.ones((16, vt.shape[1]), BF)], axis=0)
-            new = dot(vt, jnp.concatenate(e, axis=0))
-            if not own:
-                new = acc_ref[2 * p + h, :, sl] * jnp.exp2(m_old - m_new) + new
-            acc_ref[2 * p + h, :, sl] = new
-            m_ref[2 * p + h, :, sl] = m_new
-
-        prev = None
+    def scores(p, h, t):
+        keys = jnp.concatenate([r[g, p, :HALF, :] for r, g, _, _, _ in blocks], axis=0)
+        return dot(keys, q_refs[p][h, :, t * width : (t + 1) * width])
+
+    def rest(p, h, t, s):
+        sl = slice(t * width, (t + 1) * width)
+        i = t * width // 512
+        add = adds[i]
+        parts = [s[g * HALF : (g + 1) * HALF] for g in range(len(blocks))]
+        if own:
+            parts[0] = parts[0] + jnp.where(core == i, tri, add[0])
+            add = [jnp.float32(0.0), *add[1:]]
+        m_old = jnp.full((1, width), NEG, F32) if own else m_ref[2 * p + h, :, sl]
+        m_new = m_old
+        for v, b in zip(parts, add):
+            m_new = jnp.maximum(m_new, jnp.max(v, axis=0, keepdims=True) + b)
+        e = [jnp.exp2(v + (b - m_new)).astype(BF) for v, b in zip(parts, add)]
+        vt = [r[g, p, HALF + h * HD : HALF + (h + 1) * HD, :] for r, g, _, _, _ in blocks]
+        vt = jnp.concatenate(vt, axis=1)
+        vt = jnp.concatenate([vt, jnp.ones((16, vt.shape[1]), BF)], axis=0)
+        new = dot(vt, jnp.concatenate(e, axis=0))
+        if not own:
+            new = acc_ref[2 * p + h, :, sl] * jnp.exp2(m_old - m_new) + new
+        acc_ref[2 * p + h, :, sl] = new
+        m_ref[2 * p + h, :, sl] = m_new
+
+    waiting = []
+    for p in range(2):
         for h in range(2):
             for t in range(1024 // width):
-                s = dot(k_all, q_ref[h, :, t * width : (t + 1) * width])
-                if prev is not None:
-                    rest(*prev)
-                prev = (h, t, s)
-        rest(*prev)
-
-    for p in range(2):
-        pair(p)
-
-
-def start_kernel(order_ref, src_ref, q_ref, q2_ref, kv_ref, m_ref, acc_ref):
-    attend(order_ref, src_ref, 0, True, (q_ref, q2_ref), kv_ref, m_ref, acc_ref)
-
-
-def next_kernel(first, order_ref, src_ref, q_ref, q2_ref, kv_ref, m_in, acc_in, m_ref, acc_ref):
+                waiting.append((p, h, t, scores(p, h, t)))
+                if len(waiting) > 3:
+                    rest(*waiting.pop(0))
+    for w in waiting:
+        rest(*w)
+
+
+def all_of(ref, columns, k):
+    return [(ref, 2 * i + f, d, k, f == 1) for i, d in enumerate(columns) for f in range(2)]
+
+
+def start_kernel(order_ref, q_ref, q2_ref, kv_ref, m_ref, acc_ref):
+    attend(order_ref, all_of(kv_ref, COLUMNS, 0), True, (q_ref, q2_ref), m_ref, acc_ref)
+
+
+def next_kernel(step, order_ref, q_ref, q2_ref, kv_ref, m_in, acc_in, m_ref, acc_ref):
     m_ref[...] = m_in[...]
     acc_ref[...] = acc_in[...]
-    attend(order_ref, src_ref, first, False, (q_ref, q2_ref), kv_ref, m_ref, acc_ref)
+    attend(order_ref, all_of(kv_ref, COLUMNS, step), False, (q_ref, q2_ref), m_ref, acc_ref)
 
 
 def last_kernel(
-    first, order_ref, src_ref, q_ref, q2_ref, kv_ref, m_in, acc_in, keep_ref, send_ref, m_ref, acc_ref
+    step, order_ref, q_ref, q2_ref, kv_ref, m_in, acc_in, keep_ref, send_ref, m_ref, acc_ref
 ):
     m_ref[...] = m_in[...]
     acc_ref[...] = acc_in[...]
-    attend(order_ref, src_ref, first, False, (q_ref, q2_ref), kv_ref, m_ref, acc_ref)
+    attend(order_ref, all_of(kv_ref, COLUMNS, step), False, (q_ref, q2_ref), m_ref, acc_ref)
     core = place()[1] % 2
     for ref, i in ((keep_ref, core), (send_ref, 1 - core)):
         at = pl.ds(pl.multiple_of(i * 512, 512), 512)
@@ -218,7 +226,7 @@
             ref[j, 72:, :] = jnp.broadcast_to(m_ref[j, :, at], (8, 512))
 
 
-def project_kernel(mine_ref, got_ref, wo_ref, wo2_ref, out_ref, heads_ref):
+def join_kernel(mine_ref, got_ref, heads_ref):
     for p in range(2):
         for h in range(2):
             a, b = 2 * p + h, 2 * (1 - p) + h
@@ -233,64 +241,98 @@
                 )
                 col = (p * 4 + h * 2 + k) * 128
                 heads_ref[:, col : col + 128] = jnp.transpose(both).astype(BF)
+
+
+def project_kernel(heads_ref, wo_ref, wo2_ref, out_ref):
     half = wo_ref.shape[0]
-    out = dot(heads_ref[:, :half], wo_ref[...]) + dot(heads_ref[:, half:], wo2_ref[...])
-    out_ref[...] = out.astype(BF)
-
-
-def fetch_kernel(*refs):
-    n = (len(refs) - 1) // 2
-    parts = 8
-    copies = []
-    for i in range(n):
-        a, b = refs[i], refs[n + i]
-        rows = a.shape[0] // parts
-        for j in range(parts):
-            at = slice(j * rows, (j + 1) * rows)
-            copies.append(pltpu.make_async_copy(a.at[at], b.at[at], refs[-1].at[i, j]))
-    for c in copies:
-        c.start()
-    for c in copies:
-        c.wait()
-
-
-def ffn_kernel(
-    tok_ref, own_ref, other_ref, gain_ref, wg, wu, wd,
-    resid_ref, keep_ref, send_ref,
-    full_ref, normed_ref, acc_ref,
+    out_ref[...] = dot(heads_ref[:, :half], wo_ref[...]) + dot(heads_ref[:, half:], wo2_ref[...])
+
+
+def rows_of(i):
+    return pl.ds(pl.multiple_of(i * HALF, HALF), HALF)
+
+
+def normalize(x, gain_ref):
+    scale = lax.rsqrt(jnp.mean(x * x, axis=-1, keepdims=True) + EPS)
+    return (x * scale * gain_ref[...]).astype(BF)
+
+
+def residual_rows(tok_ref, att_ref, gain_ref, block, normed_ref, resid_ref, full_ref):
+    rows = 64
+    start = pl.multiple_of(block * HALF, HALF)
+    for r in range(0, HALF, rows):
+        x = tok_ref[pl.ds(start + r, rows), :].astype(F32) + att_ref[r : r + rows, :].astype(F32)
+        full_ref[r : r + rows, :] = x
+        normed_ref[r : r + rows, :] = normalize(x, gain_ref)
+    share = resid_ref.shape[1]
+    tp = place()[1]
+    resid_ref[...] = full_ref[:, pl.ds(pl.multiple_of(tp * share, share), share)]
+
+
+def own_kernel(
+    part_ref, heads_ref, wo_ref, wo2_ref, tok_ref, gain_ref, att_ref, normed_ref, resid_ref, full_ref
 ):
-    nt = 4
-    tf = wg.shape[1] // nt
-    tp = place()[1]
-    core = tp % 2
-    rows = 64
-    for b in range(2):
-        att = (own_ref, other_ref)[b]
-        start = pl.multiple_of((core if b == 0 else 1 - core) * HALF, HALF)
-        for r in range(0, HALF, rows):
-            at = pl.ds(start + r, rows)
-            x = tok_ref[at, :].astype(F32) + att[r : r + rows, :].astype(F32)
-            full_ref[at, :] = x
-            scale = lax.rsqrt(jnp.mean(x * x, axis=-1, keepdims=True) + EPS)
-            normed_ref[at, :] = (x * scale * gain_ref[...]).astype(BF)
-    share = resid_ref.shape[1]
-    resid_ref[...] = full_ref[:, pl.ds(pl.multiple_of(tp * share, share), share)]
-    acc_ref[...] = jnp.zeros(acc_ref.shape, F32)
+    half = wo_ref.shape[0]
+    att = part_ref[...] + dot(heads_ref[:, :half], wo_ref[...])
+    att_ref[...] = (att + dot(heads_ref[:, half:], wo2_ref[...])).astype(BF)
+    core = place()[1] % 2
+    residual_rows(tok_ref, att_ref, gain_ref, core, normed_ref, resid_ref, full_ref)
+
+
+def gated(normed, wg, wu, store):
+    tf = 512
 
     def body(t, carry):
         c = pl.ds(pl.multiple_of(t * tf, tf), tf)
-        gate = dot(normed_ref[...], wg[:, c])
-        up = dot(normed_ref[...], wu[:, c])
-        hidden = (gate / (1.0 + jnp.exp(-gate)) * up).astype(BF)
-        acc_ref[...] += dot(hidden, wd[c, :])
+        gate = dot(normed[...], wg[:, c])
+        up = dot(normed[...], wu[:, c])
+        store(c, (gate / (1.0 + jnp.exp(-gate)) * up).astype(BF))
         return carry
 
-    lax.fori_loop(0, nt, body, 0)
-    for k in range(2):
-        a = pl.ds(pl.multiple_of((2 * k + core) * share, share), share)
-        b = pl.ds(pl.multiple_of((2 * k + 1 - core) * share, share), share)
-        keep_ref[k, :, :] = acc_ref[:, a]
-        send_ref[k, :, :] = acc_ref[:, b].astype(BF)
+    lax.fori_loop(0, wg.shape[1] // tf, body, 0)
+
+
+def hidden_kernel(normed_ref, wg, wu, hidden_ref):
+    def store(c, value):
+        hidden_ref[:, c] = value
+
+    gated(normed_ref, wg, wu, store)
+
+
+def down_slice(hidden_ref, wd, i):
+    return dot(hidden_ref[...], wd[:, pl.ds(pl.multiple_of(i * 512, 512), 512)])
+
+
+def away_kernel(
+    tok_ref, att_ref, gain_ref, mine_ref, wg, wu, wd,
+    resid_ref, hidden_ref, keep_ref, send_ref,
+    normed_ref, full_ref,
+):
+    tp = place()[1]
+    core, chip = tp % 2, tp // 2
+    residual_rows(tok_ref, att_ref, gain_ref, 1 - core, normed_ref, resid_ref, full_ref)
+    hidden_ref[rows_of(core), :] = mine_ref[...]
+
+    def store(c, value):
+        hidden_ref[rows_of(1 - core), c] = value
+
+    gated(normed_ref, wg, wu, store)
+    keep_ref[...] = down_slice(hidden_ref, wd, 2 * (1 - chip) + core)
+    send_ref[...] = down_slice(hidden_ref, wd, 2 * (1 - chip) + 1 - core).astype(BF)
+
+
+def home_kernel(hidden_ref, wd, own_ref, other_ref, keep_ref, send_ref):
+    tp = place()[1]
+    core, chip = tp % 2, tp // 2
+    part = down_slice(hidden_ref, wd, 2 * chip + core)
+    keep_ref[...] = part
+    for i, ref in ((core, own_ref), (1 - core, other_ref)):
+        keep_ref[rows_of(i), :] += ref[...]
+    send_ref[...] = down_slice(hidden_ref, wd, 2 * chip + 1 - core).astype(BF)
+
+
+def final_kernel(keep_ref, a_ref, b_ref, out_ref):
+    out_ref[...] = (keep_ref[...] + a_ref[...].astype(F32) + b_ref[...].astype(F32)).astype(BF)
 
 
 def sum_kernel(a_ref, b_ref, out_ref):
@@ -325,16 +367,6 @@
     return out
 
 
-def arrivals(z, y, x, core):
-    out = []
-    for k in (0, *BACK):
-        for d in (0, *STEPS):
-            dz, dy = (d, k) if core == 0 else (k, d)
-            for xx in (x, 1 - x):
-                out.append(2 * index_of(z - dz, y - dy, xx) + core)
-    return out
-
-
 def stay(x):
     return pltpu.with_memory_space_constraint(x, pltpu.HBM)
 
@@ -354,12 +386,9 @@
 def layer(tokens, order, gain_attn, gain_ffn, w_query, w_key, w_value, w_out, w_gate, w_up, w_down):
     rows, width = tokens.shape
     me, tp = place()
-    chip = tp // 2
     every = ("blk", "tp")
     order = stay(order)
     table = jnp.asarray(angles())
-    src = jnp.asarray(np.array([arrivals(*g, c) for g in GRID for c in range(2)], np.int32))
-    src = lax.dynamic_slice_in_dim(src, 2 * me + tp % 2, 1, 0)[0]
     trig = sds((rows, 128), F32)
     half = sds((2 * HALF, 128))
     dma = pltpu.SemaphoreType.DMA
@@ -396,60 +425,65 @@
     )
     q2 = lax.ppermute(q, "tp", CORES)
     wo2 = lax.ppermute(w_out, "tp", CORES)
+    wx = lax.ppermute(lax.optimization_barrier((w_out, two))[0], "tp", CHIPS)
+    wx2 = lax.ppermute(wx, "tp", CORES)
     far = [lax.ppermute(eight, every, along(True, k)) for k in BACK[:2]]
     far.append(lax.ppermute(far[0], every, along(True, 3)))
 
     state = [sds((4, 1, 1024), F32), sds((4, 80, 1024), F32)]
     m, acc = call(
-        start_kernel, state, [SM] * 2 + [VM] * 3, [VM] * 2, (order, src, q, q2, eight),
+        start_kernel, state, [SM] + [VM] * 3, [VM] * 2, (order, q, q2, eight),
         mib=16, flops=2 * 10**9, nbytes=2 * MIB,
     )
     for j in range(2):
         m, acc = call(
-            functools.partial(next_kernel, 8 * (j + 1)), state,
-            [SM] * 2 + [VM] * 5, [VM] * 2, (order, src, q, q2, far[j], m, acc),
+            functools.partial(next_kernel, BACK[j]), state,
+            [SM] + [VM] * 5, [VM] * 2, (order, q, q2, far[j], m, acc),
             mib=16, flops=2 * 10**9, nbytes=2 * MIB,
         )
     keep, send = call(
-        functools.partial(last_kernel, 24), [sds((4, 80, 512), F32)] * 2,
-        [SM] * 2 + [VM] * 5, [VM] * 2, (order, src, q, q2, far[2], m, acc),
+        functools.partial(last_kernel, BACK[2]), [sds((4, 80, 512), F32)] * 2,
+        [SM] + [VM] * 5, [VM] * 2, (order, q, q2, far[2], m, acc),
         [pltpu.VMEM(s.shape, F32) for s in state],
         mib=16, flops=2 * 10**9, nbytes=2 * MIB,
     )
     got = lax.ppermute(send, "tp", CORES)
+    heads = call(join_kernel, sds((HALF, 2 * w_out.shape[0])), [VM] * 2, VM, (keep, got), mib=8)
+    there = lax.ppermute(heads, "tp", CHIPS)
     here = call(
-        project_kernel, sds((HALF, width)), [VM] * 4, VM, (keep, got, w_out, wo2),
-        [pltpu.VMEM((HALF, 2 * w_out.shape[0]), BF)],
-        mib=16, flops=10**9, nbytes=4 * MIB,
-    )
-    there = lax.ppermute(here, "tp", CHIPS)
+        project_kernel, sds((HALF, width), F32), [VM] * 3, VM, (heads, w_out, wo2),
+        mib=8, flops=10**9, nbytes=4 * MIB,
+    )
     weights = (w_gate, w_up, w_down)
-    weights = call(
-        fetch_kernel, [sds(w.shape) for w in weights], [ANY] * 3, [VM] * 3,
-        tuple(stay(w) for w in weights), [dma((3, 8))], mib=2, nbytes=24 * MIB,
-    )
     weights = [pltpu.with_memory_space_constraint(w, pltpu.VMEM) for w in weights]
-    own = call(sum_kernel, sds((HALF, width)), [VM] * 2, VM, (here, there), mib=4)
-    other = lax.ppermute(own, "tp", CORES)
-
     share = width // lax.axis_size("tp")
-    resid, keep, send = call(
-        ffn_kernel,
-        [sds((rows, share), F32), sds((2, rows, share), F32), sds((2, rows, share))],
-        [VM] * 7, [VM] * 3,
-        (tokens, own, other, gain_ffn[None, :], *weights),
-        [
-            pltpu.VMEM((rows, width), F32),
-            pltpu.VMEM((rows, width), BF),
-            pltpu.VMEM((rows, width), F32),
-        ],
-        mib=16, flops=7 * 10**9, nbytes=24 * MIB,
-    )
-    both = keep + lax.ppermute(send, "tp", CORES).astype(F32)
-    mine = lax.dynamic_index_in_dim(both, chip, 0, keepdims=False)
-    away = lax.dynamic_index_in_dim(both, 1 - chip, 0, keepdims=False).astype(BF)
-    feed = mine + lax.ppermute(away, "tp", CHIPS).astype(F32)
-    return (resid + feed).astype(BF)
+    gain = gain_ffn[None, :]
+    part = sds((HALF, width))
+    slab = sds((rows, share))
+    wide = sds((rows, share), F32)
+    thin = sds((HALF, share), F32)
+    att, normed, own = call(
+        own_kernel, [part, part, thin], [VM] * 6, [VM] * 3,
+        (here, there, wx, wx2, tokens, gain),
+        [pltpu.VMEM((HALF, width), F32)], mib=8,
+    )
+    att = lax.ppermute(att, "tp", CORES)
+    hidden = call(hidden_kernel, part, [VM] * 3, VM, (normed, *weights[:2]), mib=8, flops=2 * 10**9)
+    other, hidden, keep, send = call(
+        away_kernel, [thin, sds((rows, width)), wide, slab], [VM] * 7, [VM] * 4,
+        (tokens, att, gain, hidden, *weights),
+        [pltpu.VMEM((HALF, width), BF), pltpu.VMEM((HALF, width), F32)],
+        mib=14, flops=4 * 10**9,
+    )
+    got = lax.ppermute(send, "tp", CORES)
+    away = call(sum_kernel, slab, [VM] * 2, VM, (keep, got), mib=4)
+    far_sum = lax.ppermute(away, "tp", CHIPS)
+    keep, send = call(
+        home_kernel, [wide, slab], [VM] * 4, [VM] * 2, (hidden, weights[2], own, other),
+        mib=10, flops=10**9,
+    )
+    near_sum = lax.ppermute(send, "tp", CORES)
+    return call(final_kernel, slab, [VM] * 3, VM, (keep, near_sum, far_sum), mib=8)
 
 
 def solution(mesh):

time: 118 us -> 111 us (0.941)
  Pallas kernels: 49.8 us -> 35.8 us
  waiting for transfers between devices: 37.4 us -> 47.1 us
  local copies, waits for them, and re-layouts: 2.34 us -> 0.07 us
    pallas_call x13 -> x17, Pallas kernels: 49.8 us -> 35.8 us  [call(): pl.pallas_call(kernel, out_shape=out, in_specs=ins, out_specs=outs, scrat...]
    ppermute x4 -> x6, waiting for transfers between devices: 20.2 us -> 27 us  [the longest x1 14.8 us: layer(): wx = lax.ppermute(lax.optimization_barrier((w_out, two))[0], 'tp', CHIPS)]
    ppermute x4 -> x6, starting transfers between devices: 4.11 us -> 7.89 us  [the longest x1 2.07 us: layer(): wx2 = lax.ppermute(wx, 'tp', CORES)]
    ppermute x2 -> x3, starting transfers between devices: 4.88 us -> 1.67 us  [layer(): got = lax.ppermute(send, 'tp', CORES)]
    ppermute x1, starting transfers between devices: 0.09 us -> 2.7 us  [layer(): q2 = lax.ppermute(q, 'tp', CORES)]
    ppermute x2, waiting for transfers between devices: 5.16 us -> 7.67 us  [layer(): far = [lax.ppermute(eight, every, along(True, k)) for k in BACK[:2]]]
    ppermute x1, starting transfers between devices: 2.49 us -> 0.09 us  [layer(): wo2 = lax.ppermute(w_out, 'tp', CORES)]
    unnamed x8 -> x20, local copies, waits for them, and re-layouts: 1.61 us -> 0.07 us
  transfers between devices with their start and end apart: 15 -> 18, of which waited for: 10 -> 9; matrix products, arithmetic and copies ran while one was open for 1% -> 0% of each run, Pallas kernels for 32% -> 23%
where the time goes in v2:
time: 111 us; the launch traced here: 110 us
  waiting for transfers between devices  47.1 us (42%)
  Pallas kernels  35.8 us (32%)
  starting transfers between devices  27.2 us (25%)
    pallas_call x17, Pallas kernels, call(): pl.pallas_call(kernel, out_shape=out, in_specs=ins, out_specs=outs, scrat...  35.8 us
    ppermute x1, waiting for transfers between devices, layer(): wx = lax.ppermute(lax.optimization_barrier((w_out, two))[0], 'tp', CHIPS)  14.8 us
    ppermute x2, waiting for transfers between devices, layer(): far = [lax.ppermute(eight, every, along(True, k)) for k in BACK[:2]]  7.67 us
    ppermute x1, waiting for transfers between devices, layer(): far_sum = lax.ppermute(away, 'tp', CHIPS)  6.48 us
    ppermute x3, waiting for transfers between devices, layer(): near = [lax.ppermute(two, every, along(False, k)) for k in STEPS]  6.1 us
    ppermute x1, waiting for transfers between devices, layer(): there = lax.ppermute(heads, 'tp', CHIPS)  5.67 us
    ppermute x3, starting transfers between devices, layer(): near = [lax.ppermute(two, every, along(False, k)) for k in STEPS]  4.38 us
    ppermute x2, starting transfers between devices, layer(): far = [lax.ppermute(eight, every, along(True, k)) for k in BACK[:2]]  4.12 us
  transfers between devices with their start and end apart: 18, of which 9 were waited for; matrix products, arithmetic and copies ran while one was open for 0% of the time, Pallas kernels for 23%

profile of v2, /device:TPU:1, one launch (start us, length us, event | category | flops | bytes accessed | tf_op | source)
XLA Modules:
  0.0 110.5 jit_solution(4396861170123021703)
XLA Ops:
  0.0 3.5 %shard_map.118 = (bf16[256,2048]{1,0:T(8,128)(2,1)S(1)}, bf16[256,128]{1,0:T(8,128)(2,1)S(1)}, bf16[256,128]{1,0:T(8,128)(2,1)S(1)}, f32[256,128]{1,0:T(8,128)S(1)}, f32[256,128]{1,0:T(8,128)S(1)}) custom-call(s32[64]{0:T(128)} %order_ref.9, bf16[256,2048]{1,0:T(8,128)(2,1)} %tok_ref.3, f32[1,2048]{1,0:T(1,128)} %bitcast.18, bf16[2048,128]{1,0:T(8,128)(2,1)} %wk_hbm.1, ...), custom_call_target="tpu_custom_call" | custom-call | flops 10000000 | bytes 1048576 | tf_op jit(solution)/shard_map/pallas_call | solution.py:375
  3.5 1.5 %collective-permute-start.1 = (bf16[256,128]{1,0:T(8,128)(2,1)S(1)}, bf16[256,128]{1,0:T(8,128)(2,1)S(1)}, u32[]{:S(2)}, u32[]{:S(2)}) collective-permute-start(bf16[256,128]{1,0:T(8,128)(2,1)S(1)} %get-tuple-element.32), channel_id=1, source_target_pairs={{0,1},{1,0},{2,3},{3,2},{4,5},{5,4},{6,7},{7,6},{8,9},{9,8},{10,11... | collective-permute-start | bytes 196616 | tf_op jit(solution)/shard_map/ppermute | solution.py:411
  5.0 0.9 collective-permute-done.1
  5.9 2.9 %collective-permute-start.2 = (bf16[2,256,128]{2,1,0:T(8,128)(2,1)S(1)}, bf16[2,256,128]{2,1,0:T(8,128)(2,1)S(1)}, u32[]{:S(2)}, u32[]{:S(2)}) collective-permute-start(bf16[2,256,128]{2,1,0:T(8,128)(2,1)S(1)} %shard_map.120), channel_id=1, source_target_pairs={{0,4},{4,0},{8,12},{12,8},{16,20},{20,16},{24,28},{28,24},{32,36},... | collective-permute-start | bytes 393224 | tf_op jit(solution)/shard_map/ppermute | solution.py:413
  8.8 3.3 %collective-permute-done.2 = bf16[2,256,128]{2,1,0:T(8,128)(2,1)S(1)} collective-permute-done((bf16[2,256,128]{2,1,0:T(8,128)(2,1)S(1)}, bf16[2,256,128]{2,1,0:T(8,128)(2,1)S(1)}, u32[]{:S(2)}, u32[]{:S(2)}) %collective-permute-start.2) | collective-permute-done | bytes 131104 | tf_op jit(solution)/shard_map/ppermute | solution.py:413
  12.2 1.4 %collective-permute-start.12 = (bf16[512,2048]{1,0:T(8,128)(2,1)S(1)}, bf16[512,2048]{1,0:T(8,128)(2,1)S(1)}, u32[]{:S(2)}, u32[]{:S(2)}) collective-permute-start(bf16[512,2048]{1,0:T(8,128)(2,1)S(1)} %copy-done.1), channel_id=1, source_target_pairs={{0,2},{2,0},{1,3},{3,1},{4,6},{6,4},{5,7},{7,5},{8,10},{10,8},{9,1... | collective-permute-start | bytes 6291464 | tf_op jit(solution)/shard_map/ppermute | solution.py:428
  13.6 1.3 %collective-permute-start.3 = (bf16[2,2,256,128]{3,2,1,0:T(8,128)(2,1)S(1)}, bf16[2,2,256,128]{3,2,1,0:T(8,128)(2,1)S(1)}, u32[]{:S(2)}, u32[]{:S(2)}) collective-permute-start(bf16[2,2,256,128]{3,2,1,0:T(8,128)(2,1)S(1)} %shard_map.121.refs_0_), channel_id=1, source_target_pairs={{0,32},{1,9},{2,34},{3,11},{4,36},{5,13},{6,38},{7,15},{8,40},{9,1... | collective-permute-start | bytes 786440 | tf_op jit(solution)/shard_map/ppermute | solution.py:417
  14.9 1.4 %collective-permute-start.4 = (bf16[2,2,256,128]{3,2,1,0:T(8,128)(2,1)S(1)}, bf16[2,2,256,128]{3,2,1,0:T(8,128)(2,1)S(1)}, u32[]{:S(2)}, u32[]{:S(2)}) collective-permute-start(bf16[2,2,256,128]{3,2,1,0:T(8,128)(2,1)S(1)} %shard_map.121.refs_0_), channel_id=1, source_target_pairs={{0,96},{1,25},{2,98},{3,27},{4,100},{5,29},{6,102},{7,31},{8,104},... | collective-permute-start | bytes 786440 | tf_op jit(solution)/shard_map/ppermute | solution.py:417
  16.4 1.6 %collective-permute-start.5 = (bf16[2,2,256,128]{3,2,1,0:T(8,128)(2,1)S(1)}, bf16[2,2,256,128]{3,2,1,0:T(8,128)(2,1)S(1)}, u32[]{:S(2)}, u32[]{:S(2)}) collective-permute-start(bf16[2,2,256,128]{3,2,1,0:T(8,128)(2,1)S(1)} %shard_map.121.refs_0_), channel_id=1, source_target_pairs={{0,64},{1,17},{2,66},{3,19},{4,68},{5,21},{6,70},{7,23},{8,72},{9,... | collective-permute-start | bytes 786440 | tf_op jit(solution)/shard_map/ppermute | solution.py:417
  18.0 2.4 %collective-permute-done.3.refs_1_ = bf16[2,2,256,128]{3,2,1,0:T(8,128)(2,1)S(1)} collective-permute-done((bf16[2,2,256,128]{3,2,1,0:T(8,128)(2,1)S(1)}, bf16[2,2,256,128]{3,2,1,0:T(8,128)(2,1)S(1)}, u32[]{:S(2)}, u32[]{:S(2)}) %collective-permute-start.3) | collective-permute-done | bytes 262176 | tf_op jit(solution)/shard_map/ppermute | solution.py:417
  20.4 3.7 %collective-permute-done.5.refs_3_ = bf16[2,2,256,128]{3,2,1,0:T(8,128)(2,1)S(1)} collective-permute-done((bf16[2,2,256,128]{3,2,1,0:T(8,128)(2,1)S(1)}, bf16[2,2,256,128]{3,2,1,0:T(8,128)(2,1)S(1)}, u32[]{:S(2)}, u32[]{:S(2)}) %collective-permute-start.5) | collective-permute-done | bytes 262176 | tf_op jit(solution)/shard_map/ppermute | solution.py:417
  24.2 4.1 %collective-permute-start.6 = (bf16[8,2,256,128]{3,2,1,0:T(8,128)(2,1)S(1)}, bf16[8,2,256,128]{3,2,1,0:T(8,128)(2,1)S(1)}, u32[]{:S(2)}, u32[]{:S(2)}) collective-permute-start(bf16[8,2,256,128]{3,2,1,0:T(8,128)(2,1)S(1)} %shard_map.122.kv_ref), channel_id=1, source_target_pairs={{0,24},{1,97},{2,26},{3,99},{4,28},{5,101},{6,30},{7,103},{8,0},{9... | collective-permute-start | bytes 3145736 | tf_op jit(solution)/shard_map/ppermute | solution.py:430
  28.3 1.3 %shard_map.119.q_ref = bf16[2,128,1024]{2,1,0:T(8,128)(2,1)S(1)} custom-call(bf16[256,2048]{1,0:T(8,128)(2,1)S(1)} %get-tuple-element.28.normed_ref, bf16[2048,512]{1,0:T(8,128)(2,1)S(1)} %copy-done.2, f32[256,128]{1,0:T(8,128)S(1)} %get-tuple-element.29.cos_ref, f32[256,128]{1,0:T(8,128)S(1)} %get-tuple-element.30.sin_ref), custom_call_target="tpu_custom_call" | custom-call | flops 1000000000 | bytes 4194304 | tf_op jit(solution)/shard_map/pallas_call | solution.py:375
  29.6 2.7 %collective-permute-start = (bf16[2,128,1024]{2,1,0:T(8,128)(2,1)S(1)}, bf16[2,128,1024]{2,1,0:T(8,128)(2,1)S(1)}, u32[]{:S(2)}, u32[]{:S(2)}) collective-permute-start(bf16[2,128,1024]{2,1,0:T(8,128)(2,1)S(1)} %shard_map.119.q_ref), channel_id=1, source_target_pairs={{0,1},{1,0},{2,3},{3,2},{4,5},{5,4},{6,7},{7,6},{8,9},{9,8},{10,11... | collective-permute-start | bytes 1572872 | tf_op jit(solution)/shard_map/ppermute | solution.py:426
  32.4 7.7 %collective-permute-done.6.kv_ref = bf16[8,2,256,128]{3,2,1,0:T(8,128)(2,1)S(1)} collective-permute-done((bf16[8,2,256,128]{3,2,1,0:T(8,128)(2,1)S(1)}, bf16[8,2,256,128]{3,2,1,0:T(8,128)(2,1)S(1)}, u32[]{:S(2)}, u32[]{:S(2)}) %collective-permute-start.6) | collective-permute-done | bytes 1048608 | tf_op jit(solution)/shard_map/ppermute | solution.py:430
  40.0 3.4 %collective-permute-start.7 = (bf16[8,2,256,128]{3,2,1,0:T(8,128)(2,1)S(1)}, bf16[8,2,256,128]{3,2,1,0:T(8,128)(2,1)S(1)}, u32[]{:S(2)}, u32[]{:S(2)}) collective-permute-start(bf16[8,2,256,128]{3,2,1,0:T(8,128)(2,1)S(1)} %collective-permute-done.6.kv_ref), channel_id=1, source_target_pairs={{0,24},{1,97},{2,26},{3,99},{4,28},{5,101},{6,30},{7,103},{8,0},{9... | collective-permute-start | bytes 3145736 | tf_op jit(solution)/shard_map/ppermute | solution.py:431
  43.5 14.8 %collective-permute-done.12.wo_ref = bf16[512,2048]{1,0:T(8,128)(2,1)S(1)} collective-permute-done((bf16[512,2048]{1,0:T(8,128)(2,1)S(1)}, bf16[512,2048]{1,0:T(8,128)(2,1)S(1)}, u32[]{:S(2)}, u32[]{:S(2)}) %collective-permute-start.12) | collective-permute-done | bytes 2097184 | tf_op jit(solution)/shard_map/ppermute | solution.py:428
  58.3 2.1 %collective-permute-start.13 = (bf16[512,2048]{1,0:T(8,128)(2,1)S(1)}, bf16[512,2048]{1,0:T(8,128)(2,1)S(1)}, u32[]{:S(2)}, u32[]{:S(2)}) collective-permute-start(bf16[512,2048]{1,0:T(8,128)(2,1)S(1)} %collective-permute-done.12.wo_ref), channel_id=1, source_target_pairs={{0,1},{1,0},{2,3},{3,2},{4,5},{5,4},{6,7},{7,6},{8,9},{9,8},{10,11... | collective-permute-start | bytes 6291464 | tf_op jit(solution)/shard_map/ppermute | solution.py:429
  60.4 4.7 %shard_map.123 = (f32[4,1,1024]{2,1,0:T(1,128)S(1)}, f32[4,80,1024]{2,1,0:T(8,128)S(1)}) custom-call(s32[64]{0:T(128)} %order_ref.9, bf16[2,128,1024]{2,1,0:T(8,128)(2,1)S(1)} %shard_map.119.q_ref, bf16[2,128,1024]{2,1,0:T(8,128)(2,1)S(1)} %collective-permute-done.q2_ref, bf16[8,2,256,128]{3,2,1,0:T(8,128)(2,1)S(1)} %shard_map.122.kv_ref), custom_call_target="tpu_custom_call" | custom-call | flops 2000000000 | bytes 2097152 | tf_op jit(solution)/shard_map/pallas_call | solution.py:375
  65.1 4.6 %shard_map.124 = (f32[4,1,1024]{2,1,0:T(1,128)S(1)}, f32[4,80,1024]{2,1,0:T(8,128)S(1)}) custom-call(s32[64]{0:T(128)} %order_ref.9, bf16[2,128,1024]{2,1,0:T(8,128)(2,1)S(1)} %shard_map.119.q_ref, bf16[2,128,1024]{2,1,0:T(8,128)(2,1)S(1)} %collective-permute-done.q2_ref, bf16[8,2,256,128]{3,2,1,0:T(8,128)(2,1)S(1)} %collective-permute-done.6.kv_ref, ...), custom_call_target="tpu_custom_call" | custom-call | flops 2000000000 | bytes 2097152 | tf_op jit(solution)/shard_map/pallas_call | solution.py:375
  69.7 4.8 %shard_map.125 = (f32[4,1,1024]{2,1,0:T(1,128)S(1)}, f32[4,80,1024]{2,1,0:T(8,128)S(1)}) custom-call(s32[64]{0:T(128)} %order_ref.9, bf16[2,128,1024]{2,1,0:T(8,128)(2,1)S(1)} %shard_map.119.q_ref, bf16[2,128,1024]{2,1,0:T(8,128)(2,1)S(1)} %collective-permute-done.q2_ref, bf16[8,2,256,128]{3,2,1,0:T(8,128)(2,1)S(1)} %collective-permute-done.8.kv_ref, ...), custom_call_target="tpu_custom_call" | custom-call | flops 2000000000 | bytes 2097152 | tf_op jit(solution)/shard_map/pallas_call | solution.py:375
  74.5 5.2 %shard_map.126 = (f32[4,80,512]{2,1,0:T(8,128)S(1)}, f32[4,80,512]{2,1,0:T(8,128)S(1)}) custom-call(s32[64]{0:T(128)} %order_ref.9, bf16[2,128,1024]{2,1,0:T(8,128)(2,1)S(1)} %shard_map.119.q_ref, bf16[2,128,1024]{2,1,0:T(8,128)(2,1)S(1)} %collective-permute-done.q2_ref, bf16[8,2,256,128]{3,2,1,0:T(8,128)(2,1)S(1)} %collective-permute-done.7.kv_ref, ...), custom_call_target="tpu_custom_call" | custom-call | flops 2000000000 | bytes 2097152 | tf_op jit(solution)/shard_map/pallas_call | solution.py:375
  79.9 2.1 %collective-permute-done.9.got_ref = f32[4,80,512]{2,1,0:T(8,128)S(1)} collective-permute-done((f32[4,80,512]{2,1,0:T(8,128)S(1)}, f32[4,80,512]{2,1,0:T(8,128)S(1)}, u32[]{:S(2)}, u32[]{:S(2)}) %collective-permute-start.9) | collective-permute-done | bytes 655392 | tf_op jit(solution)/shard_map/ppermute | solution.py:450
  82.2 1.4 %collective-permute-start.11 = (bf16[128,1024]{1,0:T(8,128)(2,1)S(1)}, bf16[128,1024]{1,0:T(8,128)(2,1)S(1)}, u32[]{:S(2)}, u32[]{:S(2)}) collective-permute-start(bf16[128,1024]{1,0:T(8,128)(2,1)S(1)} %shard_map.127.heads_ref), channel_id=1, source_target_pairs={{0,2},{2,0},{1,3},{3,1},{4,6},{6,4},{5,7},{7,5},{8,10},{10,8},{9,1... | collective-permute-start | bytes 786440 | tf_op jit(solution)/shard_map/ppermute | solution.py:452
  84.3 5.7 %collective-permute-done.11.heads_ref = bf16[128,1024]{1,0:T(8,128)(2,1)S(1)} collective-permute-done((bf16[128,1024]{1,0:T(8,128)(2,1)S(1)}, bf16[128,1024]{1,0:T(8,128)(2,1)S(1)}, u32[]{:S(2)}, u32[]{:S(2)}) %collective-permute-start.11) | collective-permute-done | bytes 262176 | tf_op jit(solution)/shard_map/ppermute | solution.py:452
  90.0 1.0 shard_map.129
  91.0 1.1 collective-permute-start.14
  92.1 3.0 %shard_map.130.mine_ref = bf16[128,2048]{1,0:T(8,128)(2,1)S(1)} custom-call(bf16[128,2048]{1,0:T(8,128)(2,1)S(1)} %get-tuple-element.43.normed_ref, bf16[2048,2048]{1,0:T(8,128)(2,1)S(1)} %bitcast.7, bf16[2048,2048]{1,0:T(8,128)(2,1)S(1)} %bitcast.9), custom_call_target="tpu_custom_call" | custom-call | flops 2000000000 | bytes 1048576 | tf_op jit(solution)/shard_map/pallas_call | solution.py:375
  95.1 4.6 %shard_map.131 = (f32[128,512]{1,0:T(8,128)S(1)}, bf16[256,2048]{1,0:T(8,128)(2,1)S(1)}, f32[256,512]{1,0:T(8,128)S(1)}, bf16[256,512]{1,0:T(8,128)(2,1)S(1)}) custom-call(bf16[256,2048]{1,0:T(8,128)(2,1)S(1)} %copy-done, bf16[128,2048]{1,0:T(8,128)(2,1)S(1)} %collective-permute-done.14.att_ref, f32[1,2048]{1,0:T(1,128)S(1)} %bitcast.17, ...), custom_call_target="tpu_custom_call" | custom-call | flops 4000000000 | bytes 1048576 | tf_op jit(solution)/shard_map/pallas_call | solution.py:375
  99.8 1.4 %shard_map.132 = (f32[256,512]{1,0:T(8,128)S(1)}, bf16[256,512]{1,0:T(8,128)(2,1)S(1)}) custom-call(bf16[256,2048]{1,0:T(8,128)(2,1)S(1)} %get-tuple-element.44.hidden_ref, bf16[2048,2048]{1,0:T(8,128)(2,1)S(1)} %bitcast.11, f32[128,512]{1,0:T(8,128)S(1)} %get-tuple-element.45.own_ref, f32[128,512]{1,0:T(8,128)S(1)} %get-tuple-element.46.other_ref), custom_call_target="tpu_custom_call" | custom-call | flops 1000000000 | bytes 1048576 | tf_op jit(solution)/shard_map/pallas_call | solution.py:375
  101.8 1.4 %collective-permute-start.17 = (bf16[256,512]{1,0:T(8,128)(2,1)S(1)}, bf16[256,512]{1,0:T(8,128)(2,1)S(1)}, u32[]{:S(2)}, u32[]{:S(2)}) collective-permute-start(bf16[256,512]{1,0:T(8,128)(2,1)S(1)} %shard_map.133), channel_id=1, source_target_pairs={{0,2},{2,0},{1,3},{3,1},{4,6},{6,4},{5,7},{7,5},{8,10},{10,8},{9,1... | collective-permute-start | bytes 786440 | tf_op jit(solution)/shard_map/ppermute | solution.py:480
  103.2 6.5 %collective-permute-done.17.b_ref = bf16[256,512]{1,0:T(8,128)(2,1)S(1)} collective-permute-done((bf16[256,512]{1,0:T(8,128)(2,1)S(1)}, bf16[256,512]{1,0:T(8,128)(2,1)S(1)}, u32[]{:S(2)}, u32[]{:S(2)}) %collective-permute-start.17) | collective-permute-done | bytes 262176 | tf_op jit(solution)/shard_map/ppermute | solution.py:480
  (44 shorter events, 2.8 us)
Async XLA Ops:
  0.0 12.2 %copy-start.1 = (bf16[512,2048]{1,0:T(8,128)(2,1)S(1)}, bf16[512,2048]{1,0:T(8,128)(2,1)}, u32[]{:S(2)}) copy-start(bf16[512,2048]{1,0:T(8,128)(2,1)} %wo_ref.1) | copy-start | bytes 6291460
  0.0 28.3 %copy-start.2 = (bf16[2048,512]{1,0:T(8,128)(2,1)S(1)}, bf16[2048,512]{1,0:T(8,128)(2,1)}, u32[]{:S(2)}) copy-start(bf16[2048,512]{1,0:T(8,128)(2,1)} %wq_hbm.1) | copy-start | bytes 6291460
  3.5 2.4 %collective-permute-start.1 = (bf16[256,128]{1,0:T(8,128)(2,1)S(1)}, bf16[256,128]{1,0:T(8,128)(2,1)S(1)}, u32[]{:S(2)}, u32[]{:S(2)}) collective-permute-start(bf16[256,128]{1,0:T(8,128)(2,1)S(1)} %get-tuple-element.32), channel_id=1, source_target_pairs={{0,1},{1,0},{2,3},{3,2},{4,5},{5,4},{6,7},{7,6},{8,9},{9,8},{10,11... | collective-permute-start | bytes 196616 | tf_op jit(solution)/shard_map/ppermute | solution.py:411
  5.9 6.3 %collective-permute-start.2 = (bf16[2,256,128]{2,1,0:T(8,128)(2,1)S(1)}, bf16[2,256,128]{2,1,0:T(8,128)(2,1)S(1)}, u32[]{:S(2)}, u32[]{:S(2)}) collective-permute-start(bf16[2,256,128]{2,1,0:T(8,128)(2,1)S(1)} %shard_map.120), channel_id=1, source_target_pairs={{0,4},{4,0},{8,12},{12,8},{16,20},{20,16},{24,28},{28,24},{32,36},... | collective-permute-start | bytes 393224 | tf_op jit(solution)/shard_map/ppermute | solution.py:413
  12.2 46.1 %collective-permute-start.12 = (bf16[512,2048]{1,0:T(8,128)(2,1)S(1)}, bf16[512,2048]{1,0:T(8,128)(2,1)S(1)}, u32[]{:S(2)}, u32[]{:S(2)}) collective-permute-start(bf16[512,2048]{1,0:T(8,128)(2,1)S(1)} %copy-done.1), channel_id=1, source_target_pairs={{0,2},{2,0},{1,3},{3,1},{4,6},{6,4},{5,7},{7,5},{8,10},{10,8},{9,1... | collective-permute-start | bytes 6291464 | tf_op jit(solution)/shard_map/ppermute | solution.py:428
  13.6 6.8 %collective-permute-start.3 = (bf16[2,2,256,128]{3,2,1,0:T(8,128)(2,1)S(1)}, bf16[2,2,256,128]{3,2,1,0:T(8,128)(2,1)S(1)}, u32[]{:S(2)}, u32[]{:S(2)}) collective-permute-start(bf16[2,2,256,128]{3,2,1,0:T(8,128)(2,1)S(1)} %shard_map.121.refs_0_), channel_id=1, source_target_pairs={{0,32},{1,9},{2,34},{3,11},{4,36},{5,13},{6,38},{7,15},{8,40},{9,1... | collective-permute-start | bytes 786440 | tf_op jit(solution)/shard_map/ppermute | solution.py:417
  14.9 5.5 %collective-permute-start.4 = (bf16[2,2,256,128]{3,2,1,0:T(8,128)(2,1)S(1)}, bf16[2,2,256,128]{3,2,1,0:T(8,128)(2,1)S(1)}, u32[]{:S(2)}, u32[]{:S(2)}) collective-permute-start(bf16[2,2,256,128]{3,2,1,0:T(8,128)(2,1)S(1)} %shard_map.121.refs_0_), channel_id=1, source_target_pairs={{0,96},{1,25},{2,98},{3,27},{4,100},{5,29},{6,102},{7,31},{8,104},... | collective-permute-start | bytes 786440 | tf_op jit(solution)/shard_map/ppermute | solution.py:417
  16.4 7.7 %collective-permute-start.5 = (bf16[2,2,256,128]{3,2,1,0:T(8,128)(2,1)S(1)}, bf16[2,2,256,128]{3,2,1,0:T(8,128)(2,1)S(1)}, u32[]{:S(2)}, u32[]{:S(2)}) collective-permute-start(bf16[2,2,256,128]{3,2,1,0:T(8,128)(2,1)S(1)} %shard_map.121.refs_0_), channel_id=1, source_target_pairs={{0,64},{1,17},{2,66},{3,19},{4,68},{5,21},{6,70},{7,23},{8,72},{9,... | collective-permute-start | bytes 786440 | tf_op jit(solution)/shard_map/ppermute | solution.py:417
  24.2 15.9 %collective-permute-start.6 = (bf16[8,2,256,128]{3,2,1,0:T(8,128)(2,1)S(1)}, bf16[8,2,256,128]{3,2,1,0:T(8,128)(2,1)S(1)}, u32[]{:S(2)}, u32[]{:S(2)}) collective-permute-start(bf16[8,2,256,128]{3,2,1,0:T(8,128)(2,1)S(1)} %shard_map.122.kv_ref), channel_id=1, source_target_pairs={{0,24},{1,97},{2,26},{3,99},{4,28},{5,101},{6,30},{7,103},{8,0},{9... | collective-permute-start | bytes 3145736 | tf_op jit(solution)/shard_map/ppermute | solution.py:430
  28.3 41.4 %collective-permute-start.8 = (bf16[8,2,256,128]{3,2,1,0:T(8,128)(2,1)S(1)}, bf16[8,2,256,128]{3,2,1,0:T(8,128)(2,1)S(1)}, u32[]{:S(2)}, u32[]{:S(2)}) collective-permute-start(bf16[8,2,256,128]{3,2,1,0:T(8,128)(2,1)S(1)} %shard_map.122.kv_ref), channel_id=1, source_target_pairs={{0,8},{1,33},{2,10},{3,35},{4,12},{5,37},{6,14},{7,39},{8,16},{9,4... | collective-permute-start | bytes 3145736 | tf_op jit(solution)/shard_map/ppermute | solution.py:430
  29.6 30.8 %collective-permute-start = (bf16[2,128,1024]{2,1,0:T(8,128)(2,1)S(1)}, bf16[2,128,1024]{2,1,0:T(8,128)(2,1)S(1)}, u32[]{:S(2)}, u32[]{:S(2)}) collective-permute-start(bf16[2,128,1024]{2,1,0:T(8,128)(2,1)S(1)} %shard_map.119.q_ref), channel_id=1, source_target_pairs={{0,1},{1,0},{2,3},{3,2},{4,5},{5,4},{6,7},{7,6},{8,9},{9,8},{10,11... | collective-permute-start | bytes 1572872 | tf_op jit(solution)/shard_map/ppermute | solution.py:426
  32.3 51.3 %collective-permute-start.10 = (bf16[512,2048]{1,0:T(8,128)(2,1)S(1)}, bf16[512,2048]{1,0:T(8,128)(2,1)S(1)}, u32[]{:S(2)}, u32[]{:S(2)}) collective-permute-start(bf16[512,2048]{1,0:T(8,128)(2,1)S(1)} %copy-done.1), channel_id=1, source_target_pairs={{0,1},{1,0},{2,3},{3,2},{4,5},{5,4},{6,7},{7,6},{8,9},{9,8},{10,11... | collective-permute-start | bytes 6291464 | tf_op jit(solution)/shard_map/ppermute | solution.py:427
  40.0 34.4 %collective-permute-start.7 = (bf16[8,2,256,128]{3,2,1,0:T(8,128)(2,1)S(1)}, bf16[8,2,256,128]{3,2,1,0:T(8,128)(2,1)S(1)}, u32[]{:S(2)}, u32[]{:S(2)}) collective-permute-start(bf16[8,2,256,128]{3,2,1,0:T(8,128)(2,1)S(1)} %collective-permute-done.6.kv_ref), channel_id=1, source_target_pairs={{0,24},{1,97},{2,26},{3,99},{4,28},{5,101},{6,30},{7,103},{8,0},{9... | collective-permute-start | bytes 3145736 | tf_op jit(solution)/shard_map/ppermute | solution.py:431
  58.3 31.7 %collective-permute-start.13 = (bf16[512,2048]{1,0:T(8,128)(2,1)S(1)}, bf16[512,2048]{1,0:T(8,128)(2,1)S(1)}, u32[]{:S(2)}, u32[]{:S(2)}) collective-permute-start(bf16[512,2048]{1,0:T(8,128)(2,1)S(1)} %collective-permute-done.12.wo_ref), channel_id=1, source_target_pairs={{0,1},{1,0},{2,3},{3,2},{4,5},{5,4},{6,7},{7,6},{8,9},{9,8},{10,11... | collective-permute-start | bytes 6291464 | tf_op jit(solution)/shard_map/ppermute | solution.py:429
  69.7 22.4 %slice-start.2 = ((s8[8388608]{0:T(1024)(128)(4,1)}), s8[4194304]{0:T(1024)(128)(4,1)S(1)}, s32[]{:S(2)}) async-start(s8[8388608]{0:T(1024)(128)(4,1)} %bitcast.8), calls=%async_computation.2 | async-start | bytes 8388608
  74.5 17.6 %slice-start = ((s8[8388608]{0:T(1024)(128)(4,1)}), s8[4194304]{0:T(1024)(128)(4,1)S(1)}, s32[]{:S(2)}) async-start(s8[8388608]{0:T(1024)(128)(4,1)} %bitcast.6), calls=%async_computation | async-start | bytes 8388608
  74.5 17.6 %slice-start.3 = ((s8[8388608]{0:T(1024)(128)(4,1)}), s8[4194304]{0:T(1024)(128)(4,1)S(1)}, s32[]{:S(2)}) async-start(s8[8388608]{0:T(1024)(128)(4,1)} %bitcast.8), calls=%async_computation.3 | async-start | bytes 8388608
  79.8 2.2 %collective-permute-start.9 = (f32[4,80,512]{2,1,0:T(8,128)S(1)}, f32[4,80,512]{2,1,0:T(8,128)S(1)}, u32[]{:S(2)}, u32[]{:S(2)}) collective-permute-start(f32[4,80,512]{2,1,0:T(8,128)S(1)} %get-tuple-element.40), channel_id=1, source_target_pairs={{0,1},{1,0},{2,3},{3,2},{4,5},{5,4},{6,7},{7,6},{8,9},{9,8},{10,11... | collective-permute-start | bytes 1966088 | tf_op jit(solution)/shard_map/ppermute | solution.py:450
  82.1 7.9 %copy-start = (bf16[256,2048]{1,0:T(8,128)(2,1)S(1)}, bf16[256,2048]{1,0:T(8,128)(2,1)}, u32[]{:S(2)}) copy-start(bf16[256,2048]{1,0:T(8,128)(2,1)} %tok_ref.3) | copy-start | bytes 3145732
  82.2 7.8 %copy-start.3 = (f32[2048]{0:T(1024)S(1)}, f32[2048]{0:T(1024)}, u32[]{:S(2)}) copy-start(f32[2048]{0:T(1024)} %param.15) | copy-start | bytes 24580
  82.2 9.9 %slice-start.1 = ((s8[8388608]{0:T(1024)(128)(4,1)}), s8[4194304]{0:T(1024)(128)(4,1)S(1)}, s32[]{:S(2)}) async-start(s8[8388608]{0:T(1024)(128)(4,1)} %bitcast.6), calls=%async_computation.1 | async-start | bytes 8388608
  82.2 7.8 %collective-permute-start.11 = (bf16[128,1024]{1,0:T(8,128)(2,1)S(1)}, bf16[128,1024]{1,0:T(8,128)(2,1)S(1)}, u32[]{:S(2)}, u32[]{:S(2)}) collective-permute-start(bf16[128,1024]{1,0:T(8,128)(2,1)S(1)} %shard_map.127.heads_ref), channel_id=1, source_target_pairs={{0,2},{2,0},{1,3},{3,1},{4,6},{6,4},{5,7},{7,5},{8,10},{10,8},{9,1... | collective-permute-start | bytes 786440 | tf_op jit(solution)/shard_map/ppermute | solution.py:452
  90.0 5.1 %slice-start.4 = ((s8[8388608]{0:T(1024)(128)(4,1)}), s8[4194304]{0:T(1024)(128)(4,1)S(1)}, s32[]{:S(2)}) async-start(s8[8388608]{0:T(1024)(128)(4,1)} %bitcast.10), calls=%async_computation.4 | async-start | bytes 8388608
  91.0 4.1 %collective-permute-start.14 = (bf16[128,2048]{1,0:T(8,128)(2,1)S(1)}, bf16[128,2048]{1,0:T(8,128)(2,1)S(1)}, u32[]{:S(2)}, u32[]{:S(2)}) collective-permute-start(bf16[128,2048]{1,0:T(8,128)(2,1)S(1)} %get-tuple-element.42), channel_id=1, source_target_pairs={{0,1},{1,0},{2,3},{3,2},{4,5},{5,4},{6,7},{7,6},{8,9},{9,8},{10,11... | collective-permute-start | bytes 1572872 | tf_op jit(solution)/shard_map/ppermute | solution.py:470
  92.1 3.0 %slice-start.5 = ((s8[8388608]{0:T(1024)(128)(4,1)}), s8[4194304]{0:T(1024)(128)(4,1)S(1)}, s32[]{:S(2)}) async-start(s8[8388608]{0:T(1024)(128)(4,1)} %bitcast.10), calls=%async_computation.5 | async-start | bytes 8388608
  99.7 2.0 %collective-permute-start.16 = (bf16[256,512]{1,0:T(8,128)(2,1)S(1)}, bf16[256,512]{1,0:T(8,128)(2,1)S(1)}, u32[]{:S(2)}, u32[]{:S(2)}) collective-permute-start(bf16[256,512]{1,0:T(8,128)(2,1)S(1)} %get-tuple-element.50), channel_id=1, source_target_pairs={{0,1},{1,0},{2,3},{3,2},{4,5},{5,4},{6,7},{7,6},{8,9},{9,8},{10,11... | collective-permute-start | bytes 786440 | tf_op jit(solution)/shard_map/ppermute | solution.py:478
  101.2 2.0 %collective-permute-start.15 = (bf16[256,512]{1,0:T(8,128)(2,1)S(1)}, bf16[256,512]{1,0:T(8,128)(2,1)S(1)}, u32[]{:S(2)}, u32[]{:S(2)}) collective-permute-start(bf16[256,512]{1,0:T(8,128)(2,1)S(1)} %get-tuple-element.48), channel_id=1, source_target_pairs={{0,1},{1,0},{2,3},{3,2},{4,5},{5,4},{6,7},{7,6},{8,9},{9,8},{10,11... | collective-permute-start | bytes 786440 | tf_op jit(solution)/shard_map/ppermute | solution.py:485
  101.8 7.9 %collective-permute-start.17 = (bf16[256,512]{1,0:T(8,128)(2,1)S(1)}, bf16[256,512]{1,0:T(8,128)(2,1)S(1)}, u32[]{:S(2)}, u32[]{:S(2)}) collective-permute-start(bf16[256,512]{1,0:T(8,128)(2,1)S(1)} %shard_map.133), channel_id=1, source_target_pairs={{0,2},{2,0},{1,3},{3,1},{4,6},{6,4},{5,7},{7,5},{8,10},{10,8},{9,1... | collective-permute-start | bytes 786440 | tf_op jit(solution)/shard_map/ppermute | solution.py:480

commit v3 on v2

--- a/solution.py
+++ b/solution.py
@@ -13,7 +13,7 @@
 HD = 64
 EPS = 1e-05
 ROPE_BASE = 500000.0
-COLUMNS = (0, 1, 3, 2)
+COLUMNS = (0, 1, 3)
 NEG = -1e30
 HIDDEN = -2e30
 HALF = 128
@@ -143,7 +143,7 @@
                 ]
 
 
-def attend(order_ref, blocks, own, q_refs, m_ref, acc_ref):
+def attend(order_ref, blocks, own, q_refs, m_in, acc_in, m_ref, acc_ref):
     me, tp = place()
     core = tp % 2
     width = 256
@@ -173,7 +173,7 @@
         if own:
             parts[0] = parts[0] + jnp.where(core == i, tri, add[0])
             add = [jnp.float32(0.0), *add[1:]]
-        m_old = jnp.full((1, width), NEG, F32) if own else m_ref[2 * p + h, :, sl]
+        m_old = jnp.full((1, width), NEG, F32) if own else m_in[2 * p + h, :, sl]
         m_new = m_old
         for v, b in zip(parts, add):
             m_new = jnp.maximum(m_new, jnp.max(v, axis=0, keepdims=True) + b)
@@ -183,7 +183,7 @@
         vt = jnp.concatenate([vt, jnp.ones((16, vt.shape[1]), BF)], axis=0)
         new = dot(vt, jnp.concatenate(e, axis=0))
         if not own:
-            new = acc_ref[2 * p + h, :, sl] * jnp.exp2(m_old - m_new) + new
+            new = acc_in[2 * p + h, :, sl] * jnp.exp2(m_old - m_new) + new
         acc_ref[2 * p + h, :, sl] = new
         m_ref[2 * p + h, :, sl] = m_new
 
@@ -203,21 +203,21 @@
 
 
 def start_kernel(order_ref, q_ref, q2_ref, kv_ref, m_ref, acc_ref):
-    attend(order_ref, all_of(kv_ref, COLUMNS, 0), True, (q_ref, q2_ref), m_ref, acc_ref)
-
-
-def next_kernel(step, order_ref, q_ref, q2_ref, kv_ref, m_in, acc_in, m_ref, acc_ref):
-    m_ref[...] = m_in[...]
-    acc_ref[...] = acc_in[...]
-    attend(order_ref, all_of(kv_ref, COLUMNS, step), False, (q_ref, q2_ref), m_ref, acc_ref)
-
-
-def last_kernel(
-    step, order_ref, q_ref, q2_ref, kv_ref, m_in, acc_in, keep_ref, send_ref, m_ref, acc_ref
-):
-    m_ref[...] = m_in[...]
-    acc_ref[...] = acc_in[...]
-    attend(order_ref, all_of(kv_ref, COLUMNS, step), False, (q_ref, q2_ref), m_ref, acc_ref)
+    blocks = all_of(kv_ref, COLUMNS, 0)
+    attend(order_ref, blocks, True, (q_ref, q2_ref), None, None, m_ref, acc_ref)
+
+
+def next_kernel(places, order_ref, q_ref, q2_ref, *refs):
+    n = len(places)
+    m_in, acc_in, m_ref, acc_ref = refs[n:]
+    blocks = [b for r, (d, k) in zip(refs, places) for b in all_of(r, d, k)]
+    attend(order_ref, blocks, False, (q_ref, q2_ref), m_in, acc_in, m_ref, acc_ref)
+
+
+def last_kernel(places, order_ref, q_ref, q2_ref, *refs):
+    n = len(places)
+    m_in, acc_in, keep_ref, send_ref, m_ref, acc_ref = refs[n:]
+    next_kernel(places, order_ref, q_ref, q2_ref, *refs[:n], m_in, acc_in, m_ref, acc_ref)
     core = place()[1] % 2
     for ref, i in ((keep_ref, core), (send_ref, 1 - core)):
         at = pl.ds(pl.multiple_of(i * 512, 512), 512)
@@ -348,8 +348,6 @@
 
 
 GRID = [(z, y, x) for z in range(4) for y in range(4) for x in range(2)]
-STEPS = (1, 3, 2)
-BACK = (3, 1, 2)
 FLIP_X = [(index_of(z, y, x), index_of(z, y, 1 - x)) for z, y, x in GRID]
 CORES = [(0, 1), (1, 0), (2, 3), (3, 2)]
 CHIPS = [(0, 2), (2, 0), (1, 3), (3, 1)]
@@ -414,8 +412,9 @@
     two = call(
         pack_kernel, sds((2, 2, 2 * HALF, 128)), [VM] * 2, VM, (one[None], other[None]), mib=4
     )
-    near = [lax.ppermute(two, every, along(False, k)) for k in STEPS]
-    eight = call(pack_kernel, sds((8, 2, 2 * HALF, 128)), [VM] * 4, VM, (two, *near), mib=8)
+    near = [lax.ppermute(two, every, along(False, k)) for k in COLUMNS[1:]]
+    six = call(pack_kernel, sds((6, 2, 2 * HALF, 128)), [VM] * 3, VM, (two, *near), mib=8)
+    column = lax.ppermute(near[1], every, along(False, 3))
     q = call(
         q_kernel, sds((2, 128, 1024)),
         [VM, ANY, VM, VM], VM,
@@ -425,27 +424,35 @@
     )
     q2 = lax.ppermute(q, "tp", CORES)
     wo2 = lax.ppermute(w_out, "tp", CORES)
-    wx = lax.ppermute(lax.optimization_barrier((w_out, two))[0], "tp", CHIPS)
+    wx = lax.ppermute(w_out, "tp", CHIPS)
     wx2 = lax.ppermute(wx, "tp", CORES)
-    far = [lax.ppermute(eight, every, along(True, k)) for k in BACK[:2]]
-    far.append(lax.ppermute(far[0], every, along(True, 3)))
+    far = {k: lax.ppermute(six, every, along(True, k)) for k in (3, 1)}
+    side = {k: lax.ppermute(column, every, along(True, k)) for k in (3, 1)}
+    far[2] = lax.ppermute(far[3], every, along(True, 3))
+    side[2] = lax.ppermute(side[3], every, along(True, 3))
+    side[0] = column
 
     state = [sds((4, 1, 1024), F32), sds((4, 80, 1024), F32)]
     m, acc = call(
-        start_kernel, state, [SM] + [VM] * 3, [VM] * 2, (order, q, q2, eight),
-        mib=16, flops=2 * 10**9, nbytes=2 * MIB,
-    )
-    for j in range(2):
-        m, acc = call(
-            functools.partial(next_kernel, BACK[j]), state,
-            [SM] + [VM] * 5, [VM] * 2, (order, q, q2, far[j], m, acc),
-            mib=16, flops=2 * 10**9, nbytes=2 * MIB,
+        start_kernel, state, [SM] + [VM] * 3, [VM] * 2, (order, q, q2, six),
+        mib=14, flops=2 * 10**9, nbytes=2 * MIB,
+    )
+
+    def add(kernel, parts, out, scratch=()):
+        places = [((2,) if s is side else COLUMNS, k) for s, k in parts]
+        return call(
+            functools.partial(kernel, places), out,
+            [SM] + [VM] * (4 + len(parts)), [VM] * 2,
+            (order, q, q2, *[s[k] for s, k in parts], m, acc), scratch,
+            mib=14, flops=2 * 10**9, nbytes=2 * MIB,
         )
-    keep, send = call(
-        functools.partial(last_kernel, BACK[2]), [sds((4, 80, 512), F32)] * 2,
-        [SM] + [VM] * 5, [VM] * 2, (order, q, q2, far[2], m, acc),
+
+    m, acc = add(next_kernel, [(far, 3)], state)
+    m, acc = add(next_kernel, [(far, 1)], state)
+    m, acc = add(next_kernel, [(side, 0), (side, 3), (side, 1)], state)
+    keep, send = add(
+        last_kernel, [(far, 2), (side, 2)], [sds((4, 80, 512), F32)] * 2,
         [pltpu.VMEM(s.shape, F32) for s in state],
-        mib=16, flops=2 * 10**9, nbytes=2 * MIB,
     )
     got = lax.ppermute(send, "tp", CORES)
     heads = call(join_kernel, sds((HALF, 2 * w_out.shape[0])), [VM] * 2, VM, (keep, got), mib=8)

time: 111 us -> 137 us (1.23)
  waiting for transfers between devices: 47.1 us -> 67.4 us
  starting transfers between devices: 27.2 us -> 32.6 us
    ppermute x1, waiting for transfers between devices: 3.35 us -> 43 us  [layer(): other = lax.ppermute(one, 'blk', FLIP_X)]
    ppermute x7 -> x10, waiting for transfers between devices: 28.6 us -> 7.19 us  [the longest x1 4.2 us: layer(): column = lax.ppermute(near[1], every, along(False, 3))]
    ppermute x7 -> x10, starting transfers between devices: 13.3 us -> 18.7 us  [the longest x2 3.83 us: layer(): far = {k: lax.ppermute(six, every, along(True, k)) for k in (3, 1)}]
    ppermute x1, starting transfers between devices: 0.09 us -> 3.03 us  [layer(): wo2 = lax.ppermute(w_out, 'tp', CORES)]
    ppermute x1, starting transfers between devices: 2.07 us -> 0.1 us  [layer(): wx2 = lax.ppermute(wx, 'tp', CORES)]
    ppermute x3, starting transfers between devices: 1.67 us -> 3.06 us  [layer(): got = lax.ppermute(send, 'tp', CORES)]
    pallas_call x17 -> x18, Pallas kernels: 35.8 us -> 36.1 us  [call(): pl.pallas_call(kernel, out_shape=out, in_specs=ins, out_specs=outs, scrat...]
  transfers between devices with their start and end apart: 18 -> 21, of which waited for: 9 -> 9; matrix products, arithmetic and copies ran while one was open for 0% -> 0% of each run, Pallas kernels for 23% -> 22%
where the time goes in v3:
time: 137 us; the launch traced here: 136 us
  waiting for transfers between devices  67.4 us (49%)
  Pallas kernels  36.1 us (26%)
  starting transfers between devices  32.6 us (24%)
    ppermute x1, waiting for transfers between devices, layer(): other = lax.ppermute(one, 'blk', FLIP_X)  43 us
    pallas_call x18, Pallas kernels, call(): pl.pallas_call(kernel, out_shape=out, in_specs=ins, out_specs=outs, scrat...  36.1 us
    ppermute x1, waiting for transfers between devices, layer(): far_sum = lax.ppermute(away, 'tp', CHIPS)  6.8 us
    ppermute x1, waiting for transfers between devices, layer(): there = lax.ppermute(heads, 'tp', CHIPS)  6.74 us
    ppermute x1, waiting for transfers between devices, layer(): column = lax.ppermute(near[1], every, along(False, 3))  4.2 us
    ppermute x2, starting transfers between devices, layer(): far = {k: lax.ppermute(six, every, along(True, k)) for k in (3, 1)}  3.83 us
    ppermute x2, starting transfers between devices, layer(): side = {k: lax.ppermute(column, every, along(True, k)) for k in (3, 1)}  3.61 us
    ppermute x1, starting transfers between devices, layer(): far[2] = lax.ppermute(far[3], every, along(True, 3))  3.41 us
  transfers between devices with their start and end apart: 21, of which 9 were waited for; matrix products, arithmetic and copies ran while one was open for 0% of the time, Pallas kernels for 22%

profile of v3, /device:TPU:1, one launch (start us, length us, event | category | flops | bytes accessed | tf_op | source)
XLA Modules:
  0.0 136.5 jit_solution(8829810207972877323)
XLA Ops:
  0.0 2.0 %collective-permute-start.15 = (bf16[512,2048]{1,0:T(8,128)(2,1)}, bf16[512,2048]{1,0:T(8,128)(2,1)S(1)}, u32[]{:S(2)}, u32[]{:S(2)}) collective-permute-start(bf16[512,2048]{1,0:T(8,128)(2,1)} %wo_ref.1), channel_id=1, source_target_pairs={{0,2},{2,0},{1,3},{3,1},{4,6},{6,4},{5,7},{7,5},{8,10},{10,8},{9,1... | collective-permute-start | bytes 6291464 | tf_op jit(solution)/shard_map/ppermute | solution.py:427
  2.0 3.0 %shard_map.118 = (bf16[256,2048]{1,0:T(8,128)(2,1)S(1)}, bf16[256,128]{1,0:T(8,128)(2,1)S(1)}, bf16[256,128]{1,0:T(8,128)(2,1)S(1)}, f32[256,128]{1,0:T(8,128)S(1)}, f32[256,128]{1,0:T(8,128)S(1)}) custom-call(s32[64]{0:T(128)} %order_ref.11, bf16[256,2048]{1,0:T(8,128)(2,1)} %tok_ref.3, f32[1,2048]{1,0:T(1,128)} %bitcast.18, bf16[2048,128]{1,0:T(8,128)(2,1)} %wk_hbm.1, ...), custom_call_target="tpu_custom_call" | custom-call | flops 10000000 | bytes 1048576 | tf_op jit(solution)/shard_map/pallas_call | solution.py:373
  5.0 1.0 collective-permute-start.1
  6.1 0.9 collective-permute-done.1
  7.0 2.5 %collective-permute-start.2 = (bf16[2,256,128]{2,1,0:T(8,128)(2,1)S(1)}, bf16[2,256,128]{2,1,0:T(8,128)(2,1)S(1)}, u32[]{:S(2)}, u32[]{:S(2)}) collective-permute-start(bf16[2,256,128]{2,1,0:T(8,128)(2,1)S(1)} %shard_map.120), channel_id=1, source_target_pairs={{0,4},{4,0},{8,12},{12,8},{16,20},{20,16},{24,28},{28,24},{32,36},... | collective-permute-start | bytes 393224 | tf_op jit(solution)/shard_map/ppermute | solution.py:411
  9.5 43.0 %collective-permute-done.2 = bf16[2,256,128]{2,1,0:T(8,128)(2,1)S(1)} collective-permute-done((bf16[2,256,128]{2,1,0:T(8,128)(2,1)S(1)}, bf16[2,256,128]{2,1,0:T(8,128)(2,1)S(1)}, u32[]{:S(2)}, u32[]{:S(2)}) %collective-permute-start.2) | collective-permute-done | bytes 131104 | tf_op jit(solution)/shard_map/ppermute | solution.py:411
  52.6 2.8 %collective-permute-start.4 = (bf16[2,2,256,128]{3,2,1,0:T(8,128)(2,1)S(1)}, bf16[2,2,256,128]{3,2,1,0:T(8,128)(2,1)S(1)}, u32[]{:S(2)}, u32[]{:S(2)}) collective-permute-start(bf16[2,2,256,128]{3,2,1,0:T(8,128)(2,1)S(1)} %shard_map.121.refs_0_), channel_id=1, source_target_pairs={{0,96},{1,25},{2,98},{3,27},{4,100},{5,29},{6,102},{7,31},{8,104},... | collective-permute-start | bytes 786440 | tf_op jit(solution)/shard_map/ppermute | solution.py:415
  55.4 1.3 shard_map.119.q_ref
  56.7 2.9 %collective-permute-start = (bf16[2,128,1024]{2,1,0:T(8,128)(2,1)S(1)}, bf16[2,128,1024]{2,1,0:T(8,128)(2,1)S(1)}, u32[]{:S(2)}, u32[]{:S(2)}) collective-permute-start(bf16[2,128,1024]{2,1,0:T(8,128)(2,1)S(1)} %shard_map.119.q_ref), channel_id=1, source_target_pairs={{0,1},{1,0},{2,3},{3,2},{4,5},{5,4},{6,7},{7,6},{8,9},{9,8},{10,11... | collective-permute-start | bytes 1572872 | tf_op jit(solution)/shard_map/ppermute | solution.py:425
  59.6 2.2 %collective-permute-done.3.refs_1_ = bf16[2,2,256,128]{3,2,1,0:T(8,128)(2,1)S(1)} collective-permute-done((bf16[2,2,256,128]{3,2,1,0:T(8,128)(2,1)S(1)}, bf16[2,2,256,128]{3,2,1,0:T(8,128)(2,1)S(1)}, u32[]{:S(2)}, u32[]{:S(2)}) %collective-permute-start.3) | collective-permute-done | bytes 262176 | tf_op jit(solution)/shard_map/ppermute | solution.py:415
  61.9 3.8 %collective-permute-start.5 = (bf16[6,2,256,128]{3,2,1,0:T(8,128)(2,1)S(1)}, bf16[6,2,256,128]{3,2,1,0:T(8,128)(2,1)S(1)}, u32[]{:S(2)}, u32[]{:S(2)}) collective-permute-start(bf16[6,2,256,128]{3,2,1,0:T(8,128)(2,1)S(1)} %shard_map.122.kv_ref), channel_id=1, source_target_pairs={{0,24},{1,97},{2,26},{3,99},{4,28},{5,101},{6,30},{7,103},{8,0},{9... | collective-permute-start | bytes 2359304 | tf_op jit(solution)/shard_map/ppermute | solution.py:429
  66.0 3.0 %collective-permute-start.13 = (bf16[512,2048]{1,0:T(8,128)(2,1)S(1)}, bf16[512,2048]{1,0:T(8,128)(2,1)S(1)}, u32[]{:S(2)}, u32[]{:S(2)}) collective-permute-start(bf16[512,2048]{1,0:T(8,128)(2,1)S(1)} %copy-done.1), channel_id=1, source_target_pairs={{0,1},{1,0},{2,3},{3,2},{4,5},{5,4},{6,7},{7,6},{8,9},{9,8},{10,11... | collective-permute-start | bytes 6291464 | tf_op jit(solution)/shard_map/ppermute | solution.py:426
  69.1 4.2 %collective-permute-done.7.refs_0_ = bf16[2,2,256,128]{3,2,1,0:T(8,128)(2,1)S(1)} collective-permute-done((bf16[2,2,256,128]{3,2,1,0:T(8,128)(2,1)S(1)}, bf16[2,2,256,128]{3,2,1,0:T(8,128)(2,1)S(1)}, u32[]{:S(2)}, u32[]{:S(2)}) %collective-permute-start.7) | collective-permute-done | bytes 262176 | tf_op jit(solution)/shard_map/ppermute | solution.py:417
  73.3 3.4 %collective-permute-start.8 = (bf16[2,2,256,128]{3,2,1,0:T(8,128)(2,1)S(1)}, bf16[2,2,256,128]{3,2,1,0:T(8,128)(2,1)S(1)}, u32[]{:S(2)}, u32[]{:S(2)}) collective-permute-start(bf16[2,2,256,128]{3,2,1,0:T(8,128)(2,1)S(1)} %collective-permute-done.7.refs_0_), channel_id=1, source_target_pairs={{0,24},{1,97},{2,26},{3,99},{4,28},{5,101},{6,30},{7,103},{8,0},{9... | collective-permute-start | bytes 786440 | tf_op jit(solution)/shard_map/ppermute | solution.py:430
  77.4 3.4 %collective-permute-start.6 = (bf16[6,2,256,128]{3,2,1,0:T(8,128)(2,1)S(1)}, bf16[6,2,256,128]{3,2,1,0:T(8,128)(2,1)S(1)}, u32[]{:S(2)}, u32[]{:S(2)}) collective-permute-start(bf16[6,2,256,128]{3,2,1,0:T(8,128)(2,1)S(1)} %collective-permute-done.5.refs_0_), channel_id=1, source_target_pairs={{0,24},{1,97},{2,26},{3,99},{4,28},{5,101},{6,30},{7,103},{8,0},{9... | collective-permute-start | bytes 2359304 | tf_op jit(solution)/shard_map/ppermute | solution.py:431
  80.8 3.8 %shard_map.123 = (f32[4,1,1024]{2,1,0:T(1,128)S(1)}, f32[4,80,1024]{2,1,0:T(8,128)S(1)}) custom-call(s32[64]{0:T(128)} %order_ref.11, bf16[2,128,1024]{2,1,0:T(8,128)(2,1)S(1)} %shard_map.119.q_ref, bf16[2,128,1024]{2,1,0:T(8,128)(2,1)S(1)} %collective-permute-done.q2_ref, bf16[6,2,256,128]{3,2,1,0:T(8,128)(2,1)S(1)} %shard_map.122.kv_ref), custom_call_target="tpu_custom_call" | custom-call | flops 2000000000 | bytes 2097152 | tf_op jit(solution)/shard_map/pallas_call | solution.py:373
  84.9 3.8 %shard_map.124 = (f32[4,1,1024]{2,1,0:T(1,128)S(1)}, f32[4,80,1024]{2,1,0:T(8,128)S(1)}) custom-call(s32[64]{0:T(128)} %order_ref.11, bf16[2,128,1024]{2,1,0:T(8,128)(2,1)S(1)} %shard_map.119.q_ref, bf16[2,128,1024]{2,1,0:T(8,128)(2,1)S(1)} %collective-permute-done.q2_ref, bf16[6,2,256,128]{3,2,1,0:T(8,128)(2,1)S(1)} %collective-permute-done.5.refs_0_, ...), custom_call_target="tpu_custom_call" | custom-call | flops 2000000000 | bytes 2097152 | tf_op jit(solution)/shard_map/pallas_call | solution.py:373
  88.7 2.7 %collective-permute-start.9 = (bf16[2,2,256,128]{3,2,1,0:T(8,128)(2,1)S(1)}, bf16[2,2,256,128]{3,2,1,0:T(8,128)(2,1)S(1)}, u32[]{:S(2)}, u32[]{:S(2)}) collective-permute-start(bf16[2,2,256,128]{3,2,1,0:T(8,128)(2,1)S(1)} %collective-permute-done.8.refs_1_), channel_id=1, source_target_pairs={{0,24},{1,97},{2,26},{3,99},{4,28},{5,101},{6,30},{7,103},{8,0},{9... | collective-permute-start | bytes 786440 | tf_op jit(solution)/shard_map/ppermute | solution.py:432
  91.4 3.7 %shard_map.125 = (f32[4,1,1024]{2,1,0:T(1,128)S(1)}, f32[4,80,1024]{2,1,0:T(8,128)S(1)}) custom-call(s32[64]{0:T(128)} %order_ref.11, bf16[2,128,1024]{2,1,0:T(8,128)(2,1)S(1)} %shard_map.119.q_ref, bf16[2,128,1024]{2,1,0:T(8,128)(2,1)S(1)} %collective-permute-done.q2_ref, bf16[6,2,256,128]{3,2,1,0:T(8,128)(2,1)S(1)} %collective-permute-done.11.refs_0_, ...), custom_call_target="tpu_custom_call" | custom-call | flops 2000000000 | bytes 2097152 | tf_op jit(solution)/shard_map/pallas_call | solution.py:373
  95.2 3.9 %shard_map.126 = (f32[4,1,1024]{2,1,0:T(1,128)S(1)}, f32[4,80,1024]{2,1,0:T(8,128)S(1)}) custom-call(s32[64]{0:T(128)} %order_ref.11, bf16[2,128,1024]{2,1,0:T(8,128)(2,1)S(1)} %shard_map.119.q_ref, bf16[2,128,1024]{2,1,0:T(8,128)(2,1)S(1)} %collective-permute-done.q2_ref, bf16[2,2,256,128]{3,2,1,0:T(8,128)(2,1)S(1)} %collective-permute-done.7.refs_0_, ...), custom_call_target="tpu_custom_call" | custom-call | flops 2000000000 | bytes 2097152 | tf_op jit(solution)/shard_map/pallas_call | solution.py:373
  99.1 4.9 %shard_map.127 = (f32[4,80,512]{2,1,0:T(8,128)S(1)}, f32[4,80,512]{2,1,0:T(8,128)S(1)}) custom-call(s32[64]{0:T(128)} %order_ref.11, bf16[2,128,1024]{2,1,0:T(8,128)(2,1)S(1)} %shard_map.119.q_ref, bf16[2,128,1024]{2,1,0:T(8,128)(2,1)S(1)} %collective-permute-done.q2_ref, bf16[6,2,256,128]{3,2,1,0:T(8,128)(2,1)S(1)} %collective-permute-done.6.refs_0_, ...), custom_call_target="tpu_custom_call" | custom-call | flops 2000000000 | bytes 2097152 | tf_op jit(solution)/shard_map/pallas_call | solution.py:373
  104.1 1.9 %collective-permute-start.12 = (f32[4,80,512]{2,1,0:T(8,128)S(1)}, f32[4,80,512]{2,1,0:T(8,128)S(1)}, u32[]{:S(2)}, u32[]{:S(2)}) collective-permute-start(f32[4,80,512]{2,1,0:T(8,128)S(1)} %get-tuple-element.43), channel_id=1, source_target_pairs={{0,1},{1,0},{2,3},{3,2},{4,5},{5,4},{6,7},{7,6},{8,9},{9,8},{10,11... | collective-permute-start | bytes 1966088 | tf_op jit(solution)/shard_map/ppermute | solution.py:457
  106.0 1.7 %collective-permute-done.12.got_ref = f32[4,80,512]{2,1,0:T(8,128)S(1)} collective-permute-done((f32[4,80,512]{2,1,0:T(8,128)S(1)}, f32[4,80,512]{2,1,0:T(8,128)S(1)}, u32[]{:S(2)}, u32[]{:S(2)}) %collective-permute-start.12) | collective-permute-done | bytes 655392 | tf_op jit(solution)/shard_map/ppermute | solution.py:457
  108.7 6.7 %collective-permute-done.14.heads_ref = bf16[128,1024]{1,0:T(8,128)(2,1)S(1)} collective-permute-done((bf16[128,1024]{1,0:T(8,128)(2,1)S(1)}, bf16[128,1024]{1,0:T(8,128)(2,1)S(1)}, u32[]{:S(2)}, u32[]{:S(2)}) %collective-permute-start.14) | collective-permute-done | bytes 262176 | tf_op jit(solution)/shard_map/ppermute | solution.py:459
  115.5 1.0 shard_map.130
  116.5 1.5 %collective-permute-start.17 = (bf16[128,2048]{1,0:T(8,128)(2,1)S(1)}, bf16[128,2048]{1,0:T(8,128)(2,1)S(1)}, u32[]{:S(2)}, u32[]{:S(2)}) collective-permute-start(bf16[128,2048]{1,0:T(8,128)(2,1)S(1)} %get-tuple-element.44), channel_id=1, source_target_pairs={{0,1},{1,0},{2,3},{3,2},{4,5},{5,4},{6,7},{7,6},{8,9},{9,8},{10,11... | collective-permute-start | bytes 1572872 | tf_op jit(solution)/shard_map/ppermute | solution.py:477
  118.1 3.0 %shard_map.131.mine_ref = bf16[128,2048]{1,0:T(8,128)(2,1)S(1)} custom-call(bf16[128,2048]{1,0:T(8,128)(2,1)S(1)} %get-tuple-element.45.normed_ref, bf16[2048,2048]{1,0:T(8,128)(2,1)S(1)} %bitcast.7, bf16[2048,2048]{1,0:T(8,128)(2,1)S(1)} %bitcast.9), custom_call_target="tpu_custom_call" | custom-call | flops 2000000000 | bytes 1048576 | tf_op jit(solution)/shard_map/pallas_call | solution.py:373
  121.1 4.6 %shard_map.132 = (f32[128,512]{1,0:T(8,128)S(1)}, bf16[256,2048]{1,0:T(8,128)(2,1)S(1)}, f32[256,512]{1,0:T(8,128)S(1)}, bf16[256,512]{1,0:T(8,128)(2,1)S(1)}) custom-call(bf16[256,2048]{1,0:T(8,128)(2,1)S(1)} %copy-done, bf16[128,2048]{1,0:T(8,128)(2,1)S(1)} %collective-permute-done.17.att_ref, f32[1,2048]{1,0:T(1,128)S(1)} %bitcast.17, ...), custom_call_target="tpu_custom_call" | custom-call | flops 4000000000 | bytes 1048576 | tf_op jit(solution)/shard_map/pallas_call | solution.py:373
  125.8 1.4 shard_map.133
  127.9 1.0 collective-permute-done.18.a_ref
  128.9 6.8 %collective-permute-done.20.b_ref = bf16[256,512]{1,0:T(8,128)(2,1)S(1)} collective-permute-done((bf16[256,512]{1,0:T(8,128)(2,1)S(1)}, bf16[256,512]{1,0:T(8,128)(2,1)S(1)}, u32[]{:S(2)}, u32[]{:S(2)}) %collective-permute-start.20) | collective-permute-done | bytes 262176 | tf_op jit(solution)/shard_map/ppermute | solution.py:487
  135.7 0.8 shard_map.135
  (51 shorter events, 3.4 us)
Async XLA Ops:
  0.0 55.4 %copy-start.2 = (bf16[2048,512]{1,0:T(8,128)(2,1)S(1)}, bf16[2048,512]{1,0:T(8,128)(2,1)}, u32[]{:S(2)}) copy-start(bf16[2048,512]{1,0:T(8,128)(2,1)} %wq_hbm.1) | copy-start | bytes 6291460
  0.0 69.0 %collective-permute-start.15 = (bf16[512,2048]{1,0:T(8,128)(2,1)}, bf16[512,2048]{1,0:T(8,128)(2,1)S(1)}, u32[]{:S(2)}, u32[]{:S(2)}) collective-permute-start(bf16[512,2048]{1,0:T(8,128)(2,1)} %wo_ref.1), channel_id=1, source_target_pairs={{0,2},{2,0},{1,3},{3,1},{4,6},{6,4},{5,7},{7,5},{8,10},{10,8},{9,1... | collective-permute-start | bytes 6291464 | tf_op jit(solution)/shard_map/ppermute | solution.py:427
  5.0 1.9 %collective-permute-start.1 = (bf16[256,128]{1,0:T(8,128)(2,1)S(1)}, bf16[256,128]{1,0:T(8,128)(2,1)S(1)}, u32[]{:S(2)}, u32[]{:S(2)}) collective-permute-start(bf16[256,128]{1,0:T(8,128)(2,1)S(1)} %get-tuple-element.33), channel_id=1, source_target_pairs={{0,1},{1,0},{2,3},{3,2},{4,5},{5,4},{6,7},{7,6},{8,9},{9,8},{10,11... | collective-permute-start | bytes 196616 | tf_op jit(solution)/shard_map/ppermute | solution.py:409
  7.0 45.6 %collective-permute-start.2 = (bf16[2,256,128]{2,1,0:T(8,128)(2,1)S(1)}, bf16[2,256,128]{2,1,0:T(8,128)(2,1)S(1)}, u32[]{:S(2)}, u32[]{:S(2)}) collective-permute-start(bf16[2,256,128]{2,1,0:T(8,128)(2,1)S(1)} %shard_map.120), channel_id=1, source_target_pairs={{0,4},{4,0},{8,12},{12,8},{16,20},{20,16},{24,28},{28,24},{32,36},... | collective-permute-start | bytes 393224 | tf_op jit(solution)/shard_map/ppermute | solution.py:411
  52.6 7.0 %collective-permute-start.4 = (bf16[2,2,256,128]{3,2,1,0:T(8,128)(2,1)S(1)}, bf16[2,2,256,128]{3,2,1,0:T(8,128)(2,1)S(1)}, u32[]{:S(2)}, u32[]{:S(2)}) collective-permute-start(bf16[2,2,256,128]{3,2,1,0:T(8,128)(2,1)S(1)} %shard_map.121.refs_0_), channel_id=1, source_target_pairs={{0,96},{1,25},{2,98},{3,27},{4,100},{5,29},{6,102},{7,31},{8,104},... | collective-permute-start | bytes 786440 | tf_op jit(solution)/shard_map/ppermute | solution.py:415
  55.4 6.4 %collective-permute-start.3 = (bf16[2,2,256,128]{3,2,1,0:T(8,128)(2,1)S(1)}, bf16[2,2,256,128]{3,2,1,0:T(8,128)(2,1)S(1)}, u32[]{:S(2)}, u32[]{:S(2)}) collective-permute-start(bf16[2,2,256,128]{3,2,1,0:T(8,128)(2,1)S(1)} %shard_map.121.refs_0_), channel_id=1, source_target_pairs={{0,32},{1,9},{2,34},{3,11},{4,36},{5,13},{6,38},{7,15},{8,40},{9,1... | collective-permute-start | bytes 786440 | tf_op jit(solution)/shard_map/ppermute | solution.py:415
  55.4 10.6 %copy-start.1 = (bf16[512,2048]{1,0:T(8,128)(2,1)S(1)}, bf16[512,2048]{1,0:T(8,128)(2,1)}, u32[]{:S(2)}) copy-start(bf16[512,2048]{1,0:T(8,128)(2,1)} %wo_ref.1) | copy-start | bytes 6291460
  56.7 9.3 %collective-permute-start = (bf16[2,128,1024]{2,1,0:T(8,128)(2,1)S(1)}, bf16[2,128,1024]{2,1,0:T(8,128)(2,1)S(1)}, u32[]{:S(2)}, u32[]{:S(2)}) collective-permute-start(bf16[2,128,1024]{2,1,0:T(8,128)(2,1)S(1)} %shard_map.119.q_ref), channel_id=1, source_target_pairs={{0,1},{1,0},{2,3},{3,2},{4,5},{5,4},{6,7},{7,6},{8,9},{9,8},{10,11... | collective-permute-start | bytes 1572872 | tf_op jit(solution)/shard_map/ppermute | solution.py:425
  61.9 15.6 %collective-permute-start.5 = (bf16[6,2,256,128]{3,2,1,0:T(8,128)(2,1)S(1)}, bf16[6,2,256,128]{3,2,1,0:T(8,128)(2,1)S(1)}, u32[]{:S(2)}, u32[]{:S(2)}) collective-permute-start(bf16[6,2,256,128]{3,2,1,0:T(8,128)(2,1)S(1)} %shard_map.122.kv_ref), channel_id=1, source_target_pairs={{0,24},{1,97},{2,26},{3,99},{4,28},{5,101},{6,30},{7,103},{8,0},{9... | collective-permute-start | bytes 2359304 | tf_op jit(solution)/shard_map/ppermute | solution.py:429
  65.7 23.0 %collective-permute-start.11 = (bf16[6,2,256,128]{3,2,1,0:T(8,128)(2,1)S(1)}, bf16[6,2,256,128]{3,2,1,0:T(8,128)(2,1)S(1)}, u32[]{:S(2)}, u32[]{:S(2)}) collective-permute-start(bf16[6,2,256,128]{3,2,1,0:T(8,128)(2,1)S(1)} %shard_map.122.kv_ref), channel_id=1, source_target_pairs={{0,8},{1,33},{2,10},{3,35},{4,12},{5,37},{6,14},{7,39},{8,16},{9,4... | collective-permute-start | bytes 2359304 | tf_op jit(solution)/shard_map/ppermute | solution.py:429
  65.7 7.6 %collective-permute-start.7 = (bf16[2,2,256,128]{3,2,1,0:T(8,128)(2,1)S(1)}, bf16[2,2,256,128]{3,2,1,0:T(8,128)(2,1)S(1)}, u32[]{:S(2)}, u32[]{:S(2)}) collective-permute-start(bf16[2,2,256,128]{3,2,1,0:T(8,128)(2,1)S(1)} %collective-permute-done.4.refs_2_), channel_id=1, source_target_pairs={{0,96},{1,25},{2,98},{3,27},{4,100},{5,29},{6,102},{7,31},{8,104},... | collective-permute-start | bytes 786440 | tf_op jit(solution)/shard_map/ppermute | solution.py:417
  66.0 42.0 %collective-permute-start.13 = (bf16[512,2048]{1,0:T(8,128)(2,1)S(1)}, bf16[512,2048]{1,0:T(8,128)(2,1)S(1)}, u32[]{:S(2)}, u32[]{:S(2)}) collective-permute-start(bf16[512,2048]{1,0:T(8,128)(2,1)S(1)} %copy-done.1), channel_id=1, source_target_pairs={{0,1},{1,0},{2,3},{3,2},{4,5},{5,4},{6,7},{7,6},{8,9},{9,8},{10,11... | collective-permute-start | bytes 6291464 | tf_op jit(solution)/shard_map/ppermute | solution.py:426
  69.0 46.4 %collective-permute-start.16 = (bf16[512,2048]{1,0:T(8,128)(2,1)S(1)}, bf16[512,2048]{1,0:T(8,128)(2,1)S(1)}, u32[]{:S(2)}, u32[]{:S(2)}) collective-permute-start(bf16[512,2048]{1,0:T(8,128)(2,1)S(1)} %collective-permute-done.15.wo_ref), channel_id=1, source_target_pairs={{0,1},{1,0},{2,3},{3,2},{4,5},{5,4},{6,7},{7,6},{8,9},{9,8},{10,11... | collective-permute-start | bytes 6291464 | tf_op jit(solution)/shard_map/ppermute | solution.py:428
  73.3 11.3 %collective-permute-start.8 = (bf16[2,2,256,128]{3,2,1,0:T(8,128)(2,1)S(1)}, bf16[2,2,256,128]{3,2,1,0:T(8,128)(2,1)S(1)}, u32[]{:S(2)}, u32[]{:S(2)}) collective-permute-start(bf16[2,2,256,128]{3,2,1,0:T(8,128)(2,1)S(1)} %collective-permute-done.7.refs_0_), channel_id=1, source_target_pairs={{0,24},{1,97},{2,26},{3,99},{4,28},{5,101},{6,30},{7,103},{8,0},{9... | collective-permute-start | bytes 786440 | tf_op jit(solution)/shard_map/ppermute | solution.py:430
  77.4 21.7 %collective-permute-start.6 = (bf16[6,2,256,128]{3,2,1,0:T(8,128)(2,1)S(1)}, bf16[6,2,256,128]{3,2,1,0:T(8,128)(2,1)S(1)}, u32[]{:S(2)}, u32[]{:S(2)}) collective-permute-start(bf16[6,2,256,128]{3,2,1,0:T(8,128)(2,1)S(1)} %collective-permute-done.5.refs_0_), channel_id=1, source_target_pairs={{0,24},{1,97},{2,26},{3,99},{4,28},{5,101},{6,30},{7,103},{8,0},{9... | collective-permute-start | bytes 2359304 | tf_op jit(solution)/shard_map/ppermute | solution.py:431
  84.6 10.5 %collective-permute-start.10 = (bf16[2,2,256,128]{3,2,1,0:T(8,128)(2,1)S(1)}, bf16[2,2,256,128]{3,2,1,0:T(8,128)(2,1)S(1)}, u32[]{:S(2)}, u32[]{:S(2)}) collective-permute-start(bf16[2,2,256,128]{3,2,1,0:T(8,128)(2,1)S(1)} %collective-permute-done.7.refs_0_), channel_id=1, source_target_pairs={{0,8},{1,33},{2,10},{3,35},{4,12},{5,37},{6,14},{7,39},{8,16},{9,4... | collective-permute-start | bytes 786440 | tf_op jit(solution)/shard_map/ppermute | solution.py:430
  88.7 10.4 %collective-permute-start.9 = (bf16[2,2,256,128]{3,2,1,0:T(8,128)(2,1)S(1)}, bf16[2,2,256,128]{3,2,1,0:T(8,128)(2,1)S(1)}, u32[]{:S(2)}, u32[]{:S(2)}) collective-permute-start(bf16[2,2,256,128]{3,2,1,0:T(8,128)(2,1)S(1)} %collective-permute-done.8.refs_1_), channel_id=1, source_target_pairs={{0,24},{1,97},{2,26},{3,99},{4,28},{5,101},{6,30},{7,103},{8,0},{9... | collective-permute-start | bytes 786440 | tf_op jit(solution)/shard_map/ppermute | solution.py:432
  95.2 22.9 %slice-start.2 = ((s8[8388608]{0:T(1024)(128)(4,1)}), s8[4194304]{0:T(1024)(128)(4,1)S(1)}, s32[]{:S(2)}) async-start(s8[8388608]{0:T(1024)(128)(4,1)} %bitcast.8), calls=%async_computation.2 | async-start | bytes 8388608
  99.1 18.9 %slice-start = ((s8[8388608]{0:T(1024)(128)(4,1)}), s8[4194304]{0:T(1024)(128)(4,1)S(1)}, s32[]{:S(2)}) async-start(s8[8388608]{0:T(1024)(128)(4,1)} %bitcast.6), calls=%async_computation | async-start | bytes 8388608
  99.1 18.9 %slice-start.3 = ((s8[8388608]{0:T(1024)(128)(4,1)}), s8[4194304]{0:T(1024)(128)(4,1)S(1)}, s32[]{:S(2)}) async-start(s8[8388608]{0:T(1024)(128)(4,1)} %bitcast.8), calls=%async_computation.3 | async-start | bytes 8388608
  104.1 3.6 %collective-permute-start.12 = (f32[4,80,512]{2,1,0:T(8,128)S(1)}, f32[4,80,512]{2,1,0:T(8,128)S(1)}, u32[]{:S(2)}, u32[]{:S(2)}) collective-permute-start(f32[4,80,512]{2,1,0:T(8,128)S(1)} %get-tuple-element.43), channel_id=1, source_target_pairs={{0,1},{1,0},{2,3},{3,2},{4,5},{5,4},{6,7},{7,6},{8,9},{9,8},{10,11... | collective-permute-start | bytes 1966088 | tf_op jit(solution)/shard_map/ppermute | solution.py:457
  107.9 7.6 %copy-start = (bf16[256,2048]{1,0:T(8,128)(2,1)S(1)}, bf16[256,2048]{1,0:T(8,128)(2,1)}, u32[]{:S(2)}) copy-start(bf16[256,2048]{1,0:T(8,128)(2,1)} %tok_ref.3) | copy-start | bytes 3145732
  107.9 7.6 %copy-start.3 = (f32[2048]{0:T(1024)S(1)}, f32[2048]{0:T(1024)}, u32[]{:S(2)}) copy-start(f32[2048]{0:T(1024)} %param.15) | copy-start | bytes 24580
  107.9 10.1 %slice-start.1 = ((s8[8388608]{0:T(1024)(128)(4,1)}), s8[4194304]{0:T(1024)(128)(4,1)S(1)}, s32[]{:S(2)}) async-start(s8[8388608]{0:T(1024)(128)(4,1)} %bitcast.6), calls=%async_computation.1 | async-start | bytes 8388608
  107.9 7.6 %collective-permute-start.14 = (bf16[128,1024]{1,0:T(8,128)(2,1)S(1)}, bf16[128,1024]{1,0:T(8,128)(2,1)S(1)}, u32[]{:S(2)}, u32[]{:S(2)}) collective-permute-start(bf16[128,1024]{1,0:T(8,128)(2,1)S(1)} %shard_map.128.heads_ref), channel_id=1, source_target_pairs={{0,2},{2,0},{1,3},{3,1},{4,6},{6,4},{5,7},{7,5},{8,10},{10,8},{9,1... | collective-permute-start | bytes 786440 | tf_op jit(solution)/shard_map/ppermute | solution.py:459
  115.5 5.6 %slice-start.4 = ((s8[8388608]{0:T(1024)(128)(4,1)}), s8[4194304]{0:T(1024)(128)(4,1)S(1)}, s32[]{:S(2)}) async-start(s8[8388608]{0:T(1024)(128)(4,1)} %bitcast.10), calls=%async_computation.4 | async-start | bytes 8388608
  116.5 4.6 %collective-permute-start.17 = (bf16[128,2048]{1,0:T(8,128)(2,1)S(1)}, bf16[128,2048]{1,0:T(8,128)(2,1)S(1)}, u32[]{:S(2)}, u32[]{:S(2)}) collective-permute-start(bf16[128,2048]{1,0:T(8,128)(2,1)S(1)} %get-tuple-element.44), channel_id=1, source_target_pairs={{0,1},{1,0},{2,3},{3,2},{4,5},{5,4},{6,7},{7,6},{8,9},{9,8},{10,11... | collective-permute-start | bytes 1572872 | tf_op jit(solution)/shard_map/ppermute | solution.py:477
  118.1 3.0 %slice-start.5 = ((s8[8388608]{0:T(1024)(128)(4,1)}), s8[4194304]{0:T(1024)(128)(4,1)S(1)}, s32[]{:S(2)}) async-start(s8[8388608]{0:T(1024)(128)(4,1)} %bitcast.10), calls=%async_computation.5 | async-start | bytes 8388608
  125.7 2.0 %collective-permute-start.19 = (bf16[256,512]{1,0:T(8,128)(2,1)S(1)}, bf16[256,512]{1,0:T(8,128)(2,1)S(1)}, u32[]{:S(2)}, u32[]{:S(2)}) collective-permute-start(bf16[256,512]{1,0:T(8,128)(2,1)S(1)} %get-tuple-element.52), channel_id=1, source_target_pairs={{0,1},{1,0},{2,3},{3,2},{4,5},{5,4},{6,7},{7,6},{8,9},{9,8},{10,11... | collective-permute-start | bytes 786440 | tf_op jit(solution)/shard_map/ppermute | solution.py:485
  127.2 1.7 %collective-permute-start.18 = (bf16[256,512]{1,0:T(8,128)(2,1)S(1)}, bf16[256,512]{1,0:T(8,128)(2,1)S(1)}, u32[]{:S(2)}, u32[]{:S(2)}) collective-permute-start(bf16[256,512]{1,0:T(8,128)(2,1)S(1)} %get-tuple-element.50), channel_id=1, source_target_pairs={{0,1},{1,0},{2,3},{3,2},{4,5},{5,4},{6,7},{7,6},{8,9},{9,8},{10,11... | collective-permute-start | bytes 786440 | tf_op jit(solution)/shard_map/ppermute | solution.py:492
  127.8 7.9 %collective-permute-start.20 = (bf16[256,512]{1,0:T(8,128)(2,1)S(1)}, bf16[256,512]{1,0:T(8,128)(2,1)S(1)}, u32[]{:S(2)}, u32[]{:S(2)}) collective-permute-start(bf16[256,512]{1,0:T(8,128)(2,1)S(1)} %shard_map.134), channel_id=1, source_target_pairs={{0,2},{2,0},{1,3},{3,1},{4,6},{6,4},{5,7},{7,5},{8,10},{10,8},{9,1... | collective-permute-start | bytes 786440 | tf_op jit(solution)/shard_map/ppermute | solution.py:487

commit v4 on v3

--- a/solution.py
+++ b/solution.py
@@ -281,15 +281,17 @@
 
 def gated(normed, wg, wu, store):
     tf = 512
-
-    def body(t, carry):
-        c = pl.ds(pl.multiple_of(t * tf, tf), tf)
-        gate = dot(normed[...], wg[:, c])
-        up = dot(normed[...], wu[:, c])
-        store(c, (gate / (1.0 + jnp.exp(-gate)) * up).astype(BF))
-        return carry
-
-    lax.fori_loop(0, wg.shape[1] // tf, body, 0)
+    waiting = []
+    for t in range(wg.shape[1] // tf):
+        c = slice(t * tf, (t + 1) * tf)
+        waiting.append((c, dot(normed[...], wg[:, c]), dot(normed[...], wu[:, c])))
+        if t > 0:
+            activate(store, *waiting.pop(0))
+    activate(store, *waiting.pop(0))
+
+
+def activate(store, c, gate, up):
+    store(c, (gate / (1.0 + jnp.exp(-gate)) * up).astype(BF))
 
 
 def hidden_kernel(normed_ref, wg, wu, hidden_ref):
@@ -429,7 +431,7 @@
     far = {k: lax.ppermute(six, every, along(True, k)) for k in (3, 1)}
     side = {k: lax.ppermute(column, every, along(True, k)) for k in (3, 1)}
     far[2] = lax.ppermute(far[3], every, along(True, 3))
-    side[2] = lax.ppermute(side[3], every, along(True, 3))
+    side[2] = lax.ppermute(side[1], every, along(True, 1))
     side[0] = column
 
     state = [sds((4, 1, 1024), F32), sds((4, 80, 1024), F32)]

time: 137 us -> 134 us (0.978)
  starting transfers between devices: 32.6 us -> 28.3 us
  waiting for transfers between devices: 67.4 us -> 70.5 us
    ppermute x2, starting transfers between devices: 3.61 us -> 0.54 us  [layer(): side = {k: lax.ppermute(column, every, along(True, k)) for k in (3, 1)}]
    ppermute x2, waiting for transfers between devices: 0.74 us -> 3.82 us  [layer(): far = {k: lax.ppermute(six, every, along(True, k)) for k in (3, 1)}]
where the time goes in v4:
time: 134 us
  waiting for transfers between devices  70.5 us (53%)
  Pallas kernels  34.9 us (26%)
  starting transfers between devices  28.3 us (21%)
    ppermute x1, waiting for transfers between devices, layer(): other = lax.ppermute(one, 'blk', FLIP_X)  43 us
    pallas_call x18, Pallas kernels, call(): pl.pallas_call(kernel, out_shape=out, in_specs=ins, out_specs=outs, scrat...  34.9 us
    ppermute x1, waiting for transfers between devices, layer(): far_sum = lax.ppermute(away, 'tp', CHIPS)  6.79 us
    ppermute x1, waiting for transfers between devices, layer(): there = lax.ppermute(heads, 'tp', CHIPS)  6.74 us
    ppermute x1, waiting for transfers between devices, layer(): column = lax.ppermute(near[1], every, along(False, 3))  4.2 us
    ppermute x2, starting transfers between devices, layer(): far = {k: lax.ppermute(six, every, along(True, k)) for k in (3, 1)}  3.83 us
    ppermute x2, waiting for transfers between devices, layer(): far = {k: lax.ppermute(six, every, along(True, k)) for k in (3, 1)}  3.82 us
    ppermute x1, starting transfers between devices, layer(): far[2] = lax.ppermute(far[3], every, along(True, 3))  3.41 us
  transfers between devices with their start and end apart: 21, of which 9 were waited for; matrix products, arithmetic and copies ran while one was open for 0% of the time, Pallas kernels for 22%

profile of v4, /device:TPU:1, one launch (start us, length us, event | category | flops | bytes accessed | tf_op | source)
XLA Modules:
  0.0 134.0 jit_solution(10013189447912997922)
XLA Ops:
  0.0 2.0 %collective-permute-start.15 = (bf16[512,2048]{1,0:T(8,128)(2,1)}, bf16[512,2048]{1,0:T(8,128)(2,1)S(1)}, u32[]{:S(2)}, u32[]{:S(2)}) collective-permute-start(bf16[512,2048]{1,0:T(8,128)(2,1)} %wo_ref.1), channel_id=1, source_target_pairs={{0,2},{2,0},{1,3},{3,1},{4,6},{6,4},{5,7},{7,5},{8,10},{10,8},{9,1... | collective-permute-start | bytes 6291464 | tf_op jit(solution)/shard_map/ppermute | solution.py:429
  2.0 3.0 %shard_map.118 = (bf16[256,2048]{1,0:T(8,128)(2,1)S(1)}, bf16[256,128]{1,0:T(8,128)(2,1)S(1)}, bf16[256,128]{1,0:T(8,128)(2,1)S(1)}, f32[256,128]{1,0:T(8,128)S(1)}, f32[256,128]{1,0:T(8,128)S(1)}) custom-call(s32[64]{0:T(128)} %order_ref.11, bf16[256,2048]{1,0:T(8,128)(2,1)} %tok_ref.3, f32[1,2048]{1,0:T(1,128)} %bitcast.18, bf16[2048,128]{1,0:T(8,128)(2,1)} %wk_hbm.1, ...), custom_call_target="tpu_custom_call" | custom-call | flops 10000000 | bytes 1048576 | tf_op jit(solution)/shard_map/pallas_call | solution.py:375
  5.0 1.0 collective-permute-start.1
  6.1 0.9 collective-permute-done.1
  7.0 2.5 %collective-permute-start.2 = (bf16[2,256,128]{2,1,0:T(8,128)(2,1)S(1)}, bf16[2,256,128]{2,1,0:T(8,128)(2,1)S(1)}, u32[]{:S(2)}, u32[]{:S(2)}) collective-permute-start(bf16[2,256,128]{2,1,0:T(8,128)(2,1)S(1)} %shard_map.120), channel_id=1, source_target_pairs={{0,4},{4,0},{8,12},{12,8},{16,20},{20,16},{24,28},{28,24},{32,36},... | collective-permute-start | bytes 393224 | tf_op jit(solution)/shard_map/ppermute | solution.py:413
  9.5 43.0 %collective-permute-done.2 = bf16[2,256,128]{2,1,0:T(8,128)(2,1)S(1)} collective-permute-done((bf16[2,256,128]{2,1,0:T(8,128)(2,1)S(1)}, bf16[2,256,128]{2,1,0:T(8,128)(2,1)S(1)}, u32[]{:S(2)}, u32[]{:S(2)}) %collective-permute-start.2) | collective-permute-done | bytes 131104 | tf_op jit(solution)/shard_map/ppermute | solution.py:413
  52.6 2.8 %collective-permute-start.4 = (bf16[2,2,256,128]{3,2,1,0:T(8,128)(2,1)S(1)}, bf16[2,2,256,128]{3,2,1,0:T(8,128)(2,1)S(1)}, u32[]{:S(2)}, u32[]{:S(2)}) collective-permute-start(bf16[2,2,256,128]{3,2,1,0:T(8,128)(2,1)S(1)} %shard_map.121.refs_0_), channel_id=1, source_target_pairs={{0,96},{1,25},{2,98},{3,27},{4,100},{5,29},{6,102},{7,31},{8,104},... | collective-permute-start | bytes 786440 | tf_op jit(solution)/shard_map/ppermute | solution.py:417
  55.4 1.3 shard_map.119.q_ref
  56.7 2.9 %collective-permute-start = (bf16[2,128,1024]{2,1,0:T(8,128)(2,1)S(1)}, bf16[2,128,1024]{2,1,0:T(8,128)(2,1)S(1)}, u32[]{:S(2)}, u32[]{:S(2)}) collective-permute-start(bf16[2,128,1024]{2,1,0:T(8,128)(2,1)S(1)} %shard_map.119.q_ref), channel_id=1, source_target_pairs={{0,1},{1,0},{2,3},{3,2},{4,5},{5,4},{6,7},{7,6},{8,9},{9,8},{10,11... | collective-permute-start | bytes 1572872 | tf_op jit(solution)/shard_map/ppermute | solution.py:427
  59.6 2.2 %collective-permute-done.3.refs_1_ = bf16[2,2,256,128]{3,2,1,0:T(8,128)(2,1)S(1)} collective-permute-done((bf16[2,2,256,128]{3,2,1,0:T(8,128)(2,1)S(1)}, bf16[2,2,256,128]{3,2,1,0:T(8,128)(2,1)S(1)}, u32[]{:S(2)}, u32[]{:S(2)}) %collective-permute-start.3) | collective-permute-done | bytes 262176 | tf_op jit(solution)/shard_map/ppermute | solution.py:417
  61.9 3.8 %collective-permute-start.5 = (bf16[6,2,256,128]{3,2,1,0:T(8,128)(2,1)S(1)}, bf16[6,2,256,128]{3,2,1,0:T(8,128)(2,1)S(1)}, u32[]{:S(2)}, u32[]{:S(2)}) collective-permute-start(bf16[6,2,256,128]{3,2,1,0:T(8,128)(2,1)S(1)} %shard_map.122.kv_ref), channel_id=1, source_target_pairs={{0,24},{1,97},{2,26},{3,99},{4,28},{5,101},{6,30},{7,103},{8,0},{9... | collective-permute-start | bytes 2359304 | tf_op jit(solution)/shard_map/ppermute | solution.py:431
  66.0 3.0 %collective-permute-start.13 = (bf16[512,2048]{1,0:T(8,128)(2,1)S(1)}, bf16[512,2048]{1,0:T(8,128)(2,1)S(1)}, u32[]{:S(2)}, u32[]{:S(2)}) collective-permute-start(bf16[512,2048]{1,0:T(8,128)(2,1)S(1)} %copy-done.1), channel_id=1, source_target_pairs={{0,1},{1,0},{2,3},{3,2},{4,5},{5,4},{6,7},{7,6},{8,9},{9,8},{10,11... | collective-permute-start | bytes 6291464 | tf_op jit(solution)/shard_map/ppermute | solution.py:428
  69.1 4.2 %collective-permute-done.7.refs_0_ = bf16[2,2,256,128]{3,2,1,0:T(8,128)(2,1)S(1)} collective-permute-done((bf16[2,2,256,128]{3,2,1,0:T(8,128)(2,1)S(1)}, bf16[2,2,256,128]{3,2,1,0:T(8,128)(2,1)S(1)}, u32[]{:S(2)}, u32[]{:S(2)}) %collective-permute-start.7) | collective-permute-done | bytes 262176 | tf_op jit(solution)/shard_map/ppermute | solution.py:419
  73.6 3.8 %collective-permute-done.5.refs_0_ = bf16[6,2,256,128]{3,2,1,0:T(8,128)(2,1)S(1)} collective-permute-done((bf16[6,2,256,128]{3,2,1,0:T(8,128)(2,1)S(1)}, bf16[6,2,256,128]{3,2,1,0:T(8,128)(2,1)S(1)}, u32[]{:S(2)}, u32[]{:S(2)}) %collective-permute-start.5) | collective-permute-done | bytes 786464 | tf_op jit(solution)/shard_map/ppermute | solution.py:431
  77.4 3.4 %collective-permute-start.6 = (bf16[6,2,256,128]{3,2,1,0:T(8,128)(2,1)S(1)}, bf16[6,2,256,128]{3,2,1,0:T(8,128)(2,1)S(1)}, u32[]{:S(2)}, u32[]{:S(2)}) collective-permute-start(bf16[6,2,256,128]{3,2,1,0:T(8,128)(2,1)S(1)} %collective-permute-done.5.refs_0_), channel_id=1, source_target_pairs={{0,24},{1,97},{2,26},{3,99},{4,28},{5,101},{6,30},{7,103},{8,0},{9... | collective-permute-start | bytes 2359304 | tf_op jit(solution)/shard_map/ppermute | solution.py:433
  80.8 3.8 %shard_map.123 = (f32[4,1,1024]{2,1,0:T(1,128)S(1)}, f32[4,80,1024]{2,1,0:T(8,128)S(1)}) custom-call(s32[64]{0:T(128)} %order_ref.11, bf16[2,128,1024]{2,1,0:T(8,128)(2,1)S(1)} %shard_map.119.q_ref, bf16[2,128,1024]{2,1,0:T(8,128)(2,1)S(1)} %collective-permute-done.q2_ref, bf16[6,2,256,128]{3,2,1,0:T(8,128)(2,1)S(1)} %shard_map.122.kv_ref), custom_call_target="tpu_custom_call" | custom-call | flops 2000000000 | bytes 2097152 | tf_op jit(solution)/shard_map/pallas_call | solution.py:375
  84.9 3.8 %shard_map.124 = (f32[4,1,1024]{2,1,0:T(1,128)S(1)}, f32[4,80,1024]{2,1,0:T(8,128)S(1)}) custom-call(s32[64]{0:T(128)} %order_ref.11, bf16[2,128,1024]{2,1,0:T(8,128)(2,1)S(1)} %shard_map.119.q_ref, bf16[2,128,1024]{2,1,0:T(8,128)(2,1)S(1)} %collective-permute-done.q2_ref, bf16[6,2,256,128]{3,2,1,0:T(8,128)(2,1)S(1)} %collective-permute-done.5.refs_0_, ...), custom_call_target="tpu_custom_call" | custom-call | flops 2000000000 | bytes 2097152 | tf_op jit(solution)/shard_map/pallas_call | solution.py:375
  88.7 1.5 %collective-permute-start.9 = (bf16[2,2,256,128]{3,2,1,0:T(8,128)(2,1)S(1)}, bf16[2,2,256,128]{3,2,1,0:T(8,128)(2,1)S(1)}, u32[]{:S(2)}, u32[]{:S(2)}) collective-permute-start(bf16[2,2,256,128]{3,2,1,0:T(8,128)(2,1)S(1)} %collective-permute-done.8.refs_2_), channel_id=1, source_target_pairs={{0,8},{1,33},{2,10},{3,35},{4,12},{5,37},{6,14},{7,39},{8,16},{9,4... | collective-permute-start | bytes 786440 | tf_op jit(solution)/shard_map/ppermute | solution.py:434
  90.2 3.8 %shard_map.125 = (f32[4,1,1024]{2,1,0:T(1,128)S(1)}, f32[4,80,1024]{2,1,0:T(8,128)S(1)}) custom-call(s32[64]{0:T(128)} %order_ref.11, bf16[2,128,1024]{2,1,0:T(8,128)(2,1)S(1)} %shard_map.119.q_ref, bf16[2,128,1024]{2,1,0:T(8,128)(2,1)S(1)} %collective-permute-done.q2_ref, bf16[6,2,256,128]{3,2,1,0:T(8,128)(2,1)S(1)} %collective-permute-done.11.refs_0_, ...), custom_call_target="tpu_custom_call" | custom-call | flops 2000000000 | bytes 2097152 | tf_op jit(solution)/shard_map/pallas_call | solution.py:375
  94.0 3.9 %shard_map.126 = (f32[4,1,1024]{2,1,0:T(1,128)S(1)}, f32[4,80,1024]{2,1,0:T(8,128)S(1)}) custom-call(s32[64]{0:T(128)} %order_ref.11, bf16[2,128,1024]{2,1,0:T(8,128)(2,1)S(1)} %shard_map.119.q_ref, bf16[2,128,1024]{2,1,0:T(8,128)(2,1)S(1)} %collective-permute-done.q2_ref, bf16[2,2,256,128]{3,2,1,0:T(8,128)(2,1)S(1)} %collective-permute-done.7.refs_0_, ...), custom_call_target="tpu_custom_call" | custom-call | flops 2000000000 | bytes 2097152 | tf_op jit(solution)/shard_map/pallas_call | solution.py:375
  97.9 4.9 %shard_map.127 = (f32[4,80,512]{2,1,0:T(8,128)S(1)}, f32[4,80,512]{2,1,0:T(8,128)S(1)}) custom-call(s32[64]{0:T(128)} %order_ref.11, bf16[2,128,1024]{2,1,0:T(8,128)(2,1)S(1)} %shard_map.119.q_ref, bf16[2,128,1024]{2,1,0:T(8,128)(2,1)S(1)} %collective-permute-done.q2_ref, bf16[6,2,256,128]{3,2,1,0:T(8,128)(2,1)S(1)} %collective-permute-done.6.refs_0_, ...), custom_call_target="tpu_custom_call" | custom-call | flops 2000000000 | bytes 2097152 | tf_op jit(solution)/shard_map/pallas_call | solution.py:375
  102.9 1.9 %collective-permute-start.12 = (f32[4,80,512]{2,1,0:T(8,128)S(1)}, f32[4,80,512]{2,1,0:T(8,128)S(1)}, u32[]{:S(2)}, u32[]{:S(2)}) collective-permute-start(f32[4,80,512]{2,1,0:T(8,128)S(1)} %get-tuple-element.43), channel_id=1, source_target_pairs={{0,1},{1,0},{2,3},{3,2},{4,5},{5,4},{6,7},{7,6},{8,9},{9,8},{10,11... | collective-permute-start | bytes 1966088 | tf_op jit(solution)/shard_map/ppermute | solution.py:459
  104.8 1.7 %collective-permute-done.12.got_ref = f32[4,80,512]{2,1,0:T(8,128)S(1)} collective-permute-done((f32[4,80,512]{2,1,0:T(8,128)S(1)}, f32[4,80,512]{2,1,0:T(8,128)S(1)}, u32[]{:S(2)}, u32[]{:S(2)}) %collective-permute-start.12) | collective-permute-done | bytes 655392 | tf_op jit(solution)/shard_map/ppermute | solution.py:459
  107.5 6.7 %collective-permute-done.14.heads_ref = bf16[128,1024]{1,0:T(8,128)(2,1)S(1)} collective-permute-done((bf16[128,1024]{1,0:T(8,128)(2,1)S(1)}, bf16[128,1024]{1,0:T(8,128)(2,1)S(1)}, u32[]{:S(2)}, u32[]{:S(2)}) %collective-permute-start.14) | collective-permute-done | bytes 262176 | tf_op jit(solution)/shard_map/ppermute | solution.py:461
  114.3 1.0 shard_map.130
  115.3 1.5 %collective-permute-start.17 = (bf16[128,2048]{1,0:T(8,128)(2,1)S(1)}, bf16[128,2048]{1,0:T(8,128)(2,1)S(1)}, u32[]{:S(2)}, u32[]{:S(2)}) collective-permute-start(bf16[128,2048]{1,0:T(8,128)(2,1)S(1)} %get-tuple-element.44), channel_id=1, source_target_pairs={{0,1},{1,0},{2,3},{3,2},{4,5},{5,4},{6,7},{7,6},{8,9},{9,8},{10,11... | collective-permute-start | bytes 1572872 | tf_op jit(solution)/shard_map/ppermute | solution.py:479
  116.9 2.4 %shard_map.131.mine_ref = bf16[128,2048]{1,0:T(8,128)(2,1)S(1)} custom-call(bf16[128,2048]{1,0:T(8,128)(2,1)S(1)} %get-tuple-element.45.normed_ref, bf16[2048,2048]{1,0:T(8,128)(2,1)S(1)} %bitcast.7, bf16[2048,2048]{1,0:T(8,128)(2,1)S(1)} %bitcast.9), custom_call_target="tpu_custom_call" | custom-call | flops 2000000000 | bytes 1048576 | tf_op jit(solution)/shard_map/pallas_call | solution.py:375
  119.3 3.9 %shard_map.132 = (f32[128,512]{1,0:T(8,128)S(1)}, bf16[256,2048]{1,0:T(8,128)(2,1)S(1)}, f32[256,512]{1,0:T(8,128)S(1)}, bf16[256,512]{1,0:T(8,128)(2,1)S(1)}) custom-call(bf16[256,2048]{1,0:T(8,128)(2,1)S(1)} %copy-done, bf16[128,2048]{1,0:T(8,128)(2,1)S(1)} %collective-permute-done.17.att_ref, f32[1,2048]{1,0:T(1,128)S(1)} %bitcast.17, ...), custom_call_target="tpu_custom_call" | custom-call | flops 4000000000 | bytes 1048576 | tf_op jit(solution)/shard_map/pallas_call | solution.py:375
  123.4 1.4 %shard_map.133 = (f32[256,512]{1,0:T(8,128)S(1)}, bf16[256,512]{1,0:T(8,128)(2,1)S(1)}) custom-call(bf16[256,2048]{1,0:T(8,128)(2,1)S(1)} %get-tuple-element.46.hidden_ref, bf16[2048,2048]{1,0:T(8,128)(2,1)S(1)} %bitcast.11, f32[128,512]{1,0:T(8,128)S(1)} %get-tuple-element.47.own_ref, f32[128,512]{1,0:T(8,128)S(1)} %get-tuple-element.48.other_ref), custom_call_target="tpu_custom_call" | custom-call | flops 1000000000 | bytes 1048576 | tf_op jit(solution)/shard_map/pallas_call | solution.py:375
  125.4 1.0 collective-permute-done.18.a_ref
  126.4 6.8 %collective-permute-done.20.b_ref = bf16[256,512]{1,0:T(8,128)(2,1)S(1)} collective-permute-done((bf16[256,512]{1,0:T(8,128)(2,1)S(1)}, bf16[256,512]{1,0:T(8,128)(2,1)S(1)}, u32[]{:S(2)}, u32[]{:S(2)}) %collective-permute-start.20) | collective-permute-done | bytes 262176 | tf_op jit(solution)/shard_map/ppermute | solution.py:489
  133.2 0.8 shard_map.135
  (51 shorter events, 2.9 us)
Async XLA Ops:
  0.0 55.4 %copy-start.2 = (bf16[2048,512]{1,0:T(8,128)(2,1)S(1)}, bf16[2048,512]{1,0:T(8,128)(2,1)}, u32[]{:S(2)}) copy-start(bf16[2048,512]{1,0:T(8,128)(2,1)} %wq_hbm.1) | copy-start | bytes 6291460
  0.0 69.0 %collective-permute-start.15 = (bf16[512,2048]{1,0:T(8,128)(2,1)}, bf16[512,2048]{1,0:T(8,128)(2,1)S(1)}, u32[]{:S(2)}, u32[]{:S(2)}) collective-permute-start(bf16[512,2048]{1,0:T(8,128)(2,1)} %wo_ref.1), channel_id=1, source_target_pairs={{0,2},{2,0},{1,3},{3,1},{4,6},{6,4},{5,7},{7,5},{8,10},{10,8},{9,1... | collective-permute-start | bytes 6291464 | tf_op jit(solution)/shard_map/ppermute | solution.py:429
  5.0 1.9 %collective-permute-start.1 = (bf16[256,128]{1,0:T(8,128)(2,1)S(1)}, bf16[256,128]{1,0:T(8,128)(2,1)S(1)}, u32[]{:S(2)}, u32[]{:S(2)}) collective-permute-start(bf16[256,128]{1,0:T(8,128)(2,1)S(1)} %get-tuple-element.33), channel_id=1, source_target_pairs={{0,1},{1,0},{2,3},{3,2},{4,5},{5,4},{6,7},{7,6},{8,9},{9,8},{10,11... | collective-permute-start | bytes 196616 | tf_op jit(solution)/shard_map/ppermute | solution.py:411
  7.0 45.6 %collective-permute-start.2 = (bf16[2,256,128]{2,1,0:T(8,128)(2,1)S(1)}, bf16[2,256,128]{2,1,0:T(8,128)(2,1)S(1)}, u32[]{:S(2)}, u32[]{:S(2)}) collective-permute-start(bf16[2,256,128]{2,1,0:T(8,128)(2,1)S(1)} %shard_map.120), channel_id=1, source_target_pairs={{0,4},{4,0},{8,12},{12,8},{16,20},{20,16},{24,28},{28,24},{32,36},... | collective-permute-start | bytes 393224 | tf_op jit(solution)/shard_map/ppermute | solution.py:413
  52.6 7.0 %collective-permute-start.4 = (bf16[2,2,256,128]{3,2,1,0:T(8,128)(2,1)S(1)}, bf16[2,2,256,128]{3,2,1,0:T(8,128)(2,1)S(1)}, u32[]{:S(2)}, u32[]{:S(2)}) collective-permute-start(bf16[2,2,256,128]{3,2,1,0:T(8,128)(2,1)S(1)} %shard_map.121.refs_0_), channel_id=1, source_target_pairs={{0,96},{1,25},{2,98},{3,27},{4,100},{5,29},{6,102},{7,31},{8,104},... | collective-permute-start | bytes 786440 | tf_op jit(solution)/shard_map/ppermute | solution.py:417
  55.4 6.4 %collective-permute-start.3 = (bf16[2,2,256,128]{3,2,1,0:T(8,128)(2,1)S(1)}, bf16[2,2,256,128]{3,2,1,0:T(8,128)(2,1)S(1)}, u32[]{:S(2)}, u32[]{:S(2)}) collective-permute-start(bf16[2,2,256,128]{3,2,1,0:T(8,128)(2,1)S(1)} %shard_map.121.refs_0_), channel_id=1, source_target_pairs={{0,32},{1,9},{2,34},{3,11},{4,36},{5,13},{6,38},{7,15},{8,40},{9,1... | collective-permute-start | bytes 786440 | tf_op jit(solution)/shard_map/ppermute | solution.py:417
  55.4 10.6 %copy-start.1 = (bf16[512,2048]{1,0:T(8,128)(2,1)S(1)}, bf16[512,2048]{1,0:T(8,128)(2,1)}, u32[]{:S(2)}) copy-start(bf16[512,2048]{1,0:T(8,128)(2,1)} %wo_ref.1) | copy-start | bytes 6291460
  56.7 9.3 %collective-permute-start = (bf16[2,128,1024]{2,1,0:T(8,128)(2,1)S(1)}, bf16[2,128,1024]{2,1,0:T(8,128)(2,1)S(1)}, u32[]{:S(2)}, u32[]{:S(2)}) collective-permute-start(bf16[2,128,1024]{2,1,0:T(8,128)(2,1)S(1)} %shard_map.119.q_ref), channel_id=1, source_target_pairs={{0,1},{1,0},{2,3},{3,2},{4,5},{5,4},{6,7},{7,6},{8,9},{9,8},{10,11... | collective-permute-start | bytes 1572872 | tf_op jit(solution)/shard_map/ppermute | solution.py:427
  61.9 15.6 %collective-permute-start.5 = (bf16[6,2,256,128]{3,2,1,0:T(8,128)(2,1)S(1)}, bf16[6,2,256,128]{3,2,1,0:T(8,128)(2,1)S(1)}, u32[]{:S(2)}, u32[]{:S(2)}) collective-permute-start(bf16[6,2,256,128]{3,2,1,0:T(8,128)(2,1)S(1)} %shard_map.122.kv_ref), channel_id=1, source_target_pairs={{0,24},{1,97},{2,26},{3,99},{4,28},{5,101},{6,30},{7,103},{8,0},{9... | collective-permute-start | bytes 2359304 | tf_op jit(solution)/shard_map/ppermute | solution.py:431
  65.7 23.0 %collective-permute-start.11 = (bf16[6,2,256,128]{3,2,1,0:T(8,128)(2,1)S(1)}, bf16[6,2,256,128]{3,2,1,0:T(8,128)(2,1)S(1)}, u32[]{:S(2)}, u32[]{:S(2)}) collective-permute-start(bf16[6,2,256,128]{3,2,1,0:T(8,128)(2,1)S(1)} %shard_map.122.kv_ref), channel_id=1, source_target_pairs={{0,8},{1,33},{2,10},{3,35},{4,12},{5,37},{6,14},{7,39},{8,16},{9,4... | collective-permute-start | bytes 2359304 | tf_op jit(solution)/shard_map/ppermute | solution.py:431
  65.7 7.6 %collective-permute-start.7 = (bf16[2,2,256,128]{3,2,1,0:T(8,128)(2,1)S(1)}, bf16[2,2,256,128]{3,2,1,0:T(8,128)(2,1)S(1)}, u32[]{:S(2)}, u32[]{:S(2)}) collective-permute-start(bf16[2,2,256,128]{3,2,1,0:T(8,128)(2,1)S(1)} %collective-permute-done.4.refs_2_), channel_id=1, source_target_pairs={{0,96},{1,25},{2,98},{3,27},{4,100},{5,29},{6,102},{7,31},{8,104},... | collective-permute-start | bytes 786440 | tf_op jit(solution)/shard_map/ppermute | solution.py:419
  66.0 40.8 %collective-permute-start.13 = (bf16[512,2048]{1,0:T(8,128)(2,1)S(1)}, bf16[512,2048]{1,0:T(8,128)(2,1)S(1)}, u32[]{:S(2)}, u32[]{:S(2)}) collective-permute-start(bf16[512,2048]{1,0:T(8,128)(2,1)S(1)} %copy-done.1), channel_id=1, source_target_pairs={{0,1},{1,0},{2,3},{3,2},{4,5},{5,4},{6,7},{7,6},{8,9},{9,8},{10,11... | collective-permute-start | bytes 6291464 | tf_op jit(solution)/shard_map/ppermute | solution.py:428
  69.0 45.2 %collective-permute-start.16 = (bf16[512,2048]{1,0:T(8,128)(2,1)S(1)}, bf16[512,2048]{1,0:T(8,128)(2,1)S(1)}, u32[]{:S(2)}, u32[]{:S(2)}) collective-permute-start(bf16[512,2048]{1,0:T(8,128)(2,1)S(1)} %collective-permute-done.15.wo_ref), channel_id=1, source_target_pairs={{0,1},{1,0},{2,3},{3,2},{4,5},{5,4},{6,7},{7,6},{8,9},{9,8},{10,11... | collective-permute-start | bytes 6291464 | tf_op jit(solution)/shard_map/ppermute | solution.py:430
  73.3 11.3 %collective-permute-start.8 = (bf16[2,2,256,128]{3,2,1,0:T(8,128)(2,1)S(1)}, bf16[2,2,256,128]{3,2,1,0:T(8,128)(2,1)S(1)}, u32[]{:S(2)}, u32[]{:S(2)}) collective-permute-start(bf16[2,2,256,128]{3,2,1,0:T(8,128)(2,1)S(1)} %collective-permute-done.7.refs_0_), channel_id=1, source_target_pairs={{0,8},{1,33},{2,10},{3,35},{4,12},{5,37},{6,14},{7,39},{8,16},{9,4... | collective-permute-start | bytes 786440 | tf_op jit(solution)/shard_map/ppermute | solution.py:432
  77.4 20.5 %collective-permute-start.6 = (bf16[6,2,256,128]{3,2,1,0:T(8,128)(2,1)S(1)}, bf16[6,2,256,128]{3,2,1,0:T(8,128)(2,1)S(1)}, u32[]{:S(2)}, u32[]{:S(2)}) collective-permute-start(bf16[6,2,256,128]{3,2,1,0:T(8,128)(2,1)S(1)} %collective-permute-done.5.refs_0_), channel_id=1, source_target_pairs={{0,24},{1,97},{2,26},{3,99},{4,28},{5,101},{6,30},{7,103},{8,0},{9... | collective-permute-start | bytes 2359304 | tf_op jit(solution)/shard_map/ppermute | solution.py:433
  84.6 9.3 %collective-permute-start.10 = (bf16[2,2,256,128]{3,2,1,0:T(8,128)(2,1)S(1)}, bf16[2,2,256,128]{3,2,1,0:T(8,128)(2,1)S(1)}, u32[]{:S(2)}, u32[]{:S(2)}) collective-permute-start(bf16[2,2,256,128]{3,2,1,0:T(8,128)(2,1)S(1)} %collective-permute-done.7.refs_0_), channel_id=1, source_target_pairs={{0,24},{1,97},{2,26},{3,99},{4,28},{5,101},{6,30},{7,103},{8,0},{9... | collective-permute-start | bytes 786440 | tf_op jit(solution)/shard_map/ppermute | solution.py:432
  88.7 9.2 %collective-permute-start.9 = (bf16[2,2,256,128]{3,2,1,0:T(8,128)(2,1)S(1)}, bf16[2,2,256,128]{3,2,1,0:T(8,128)(2,1)S(1)}, u32[]{:S(2)}, u32[]{:S(2)}) collective-permute-start(bf16[2,2,256,128]{3,2,1,0:T(8,128)(2,1)S(1)} %collective-permute-done.8.refs_2_), channel_id=1, source_target_pairs={{0,8},{1,33},{2,10},{3,35},{4,12},{5,37},{6,14},{7,39},{8,16},{9,4... | collective-permute-start | bytes 786440 | tf_op jit(solution)/shard_map/ppermute | solution.py:434
  94.0 22.9 %slice-start.2 = ((s8[8388608]{0:T(1024)(128)(4,1)}), s8[4194304]{0:T(1024)(128)(4,1)S(1)}, s32[]{:S(2)}) async-start(s8[8388608]{0:T(1024)(128)(4,1)} %bitcast.8), calls=%async_computation.2 | async-start | bytes 8388608
  97.9 18.9 %slice-start = ((s8[8388608]{0:T(1024)(128)(4,1)}), s8[4194304]{0:T(1024)(128)(4,1)S(1)}, s32[]{:S(2)}) async-start(s8[8388608]{0:T(1024)(128)(4,1)} %bitcast.6), calls=%async_computation | async-start | bytes 8388608
  97.9 18.9 %slice-start.3 = ((s8[8388608]{0:T(1024)(128)(4,1)}), s8[4194304]{0:T(1024)(128)(4,1)S(1)}, s32[]{:S(2)}) async-start(s8[8388608]{0:T(1024)(128)(4,1)} %bitcast.8), calls=%async_computation.3 | async-start | bytes 8388608
  102.9 3.6 %collective-permute-start.12 = (f32[4,80,512]{2,1,0:T(8,128)S(1)}, f32[4,80,512]{2,1,0:T(8,128)S(1)}, u32[]{:S(2)}, u32[]{:S(2)}) collective-permute-start(f32[4,80,512]{2,1,0:T(8,128)S(1)} %get-tuple-element.43), channel_id=1, source_target_pairs={{0,1},{1,0},{2,3},{3,2},{4,5},{5,4},{6,7},{7,6},{8,9},{9,8},{10,11... | collective-permute-start | bytes 1966088 | tf_op jit(solution)/shard_map/ppermute | solution.py:459
  106.7 7.6 %copy-start = (bf16[256,2048]{1,0:T(8,128)(2,1)S(1)}, bf16[256,2048]{1,0:T(8,128)(2,1)}, u32[]{:S(2)}) copy-start(bf16[256,2048]{1,0:T(8,128)(2,1)} %tok_ref.3) | copy-start | bytes 3145732
  106.7 7.6 %copy-start.3 = (f32[2048]{0:T(1024)S(1)}, f32[2048]{0:T(1024)}, u32[]{:S(2)}) copy-start(f32[2048]{0:T(1024)} %param.15) | copy-start | bytes 24580
  106.7 10.1 %slice-start.1 = ((s8[8388608]{0:T(1024)(128)(4,1)}), s8[4194304]{0:T(1024)(128)(4,1)S(1)}, s32[]{:S(2)}) async-start(s8[8388608]{0:T(1024)(128)(4,1)} %bitcast.6), calls=%async_computation.1 | async-start | bytes 8388608
  106.7 7.6 %collective-permute-start.14 = (bf16[128,1024]{1,0:T(8,128)(2,1)S(1)}, bf16[128,1024]{1,0:T(8,128)(2,1)S(1)}, u32[]{:S(2)}, u32[]{:S(2)}) collective-permute-start(bf16[128,1024]{1,0:T(8,128)(2,1)S(1)} %shard_map.128.heads_ref), channel_id=1, source_target_pairs={{0,2},{2,0},{1,3},{3,1},{4,6},{6,4},{5,7},{7,5},{8,10},{10,8},{9,1... | collective-permute-start | bytes 786440 | tf_op jit(solution)/shard_map/ppermute | solution.py:461
  114.3 5.0 %slice-start.4 = ((s8[8388608]{0:T(1024)(128)(4,1)}), s8[4194304]{0:T(1024)(128)(4,1)S(1)}, s32[]{:S(2)}) async-start(s8[8388608]{0:T(1024)(128)(4,1)} %bitcast.10), calls=%async_computation.4 | async-start | bytes 8388608
  115.3 4.0 %collective-permute-start.17 = (bf16[128,2048]{1,0:T(8,128)(2,1)S(1)}, bf16[128,2048]{1,0:T(8,128)(2,1)S(1)}, u32[]{:S(2)}, u32[]{:S(2)}) collective-permute-start(bf16[128,2048]{1,0:T(8,128)(2,1)S(1)} %get-tuple-element.44), channel_id=1, source_target_pairs={{0,1},{1,0},{2,3},{3,2},{4,5},{5,4},{6,7},{7,6},{8,9},{9,8},{10,11... | collective-permute-start | bytes 1572872 | tf_op jit(solution)/shard_map/ppermute | solution.py:479
  116.9 2.5 %slice-start.5 = ((s8[8388608]{0:T(1024)(128)(4,1)}), s8[4194304]{0:T(1024)(128)(4,1)S(1)}, s32[]{:S(2)}) async-start(s8[8388608]{0:T(1024)(128)(4,1)} %bitcast.10), calls=%async_computation.5 | async-start | bytes 8388608
  123.2 2.0 %collective-permute-start.19 = (bf16[256,512]{1,0:T(8,128)(2,1)S(1)}, bf16[256,512]{1,0:T(8,128)(2,1)S(1)}, u32[]{:S(2)}, u32[]{:S(2)}) collective-permute-start(bf16[256,512]{1,0:T(8,128)(2,1)S(1)} %get-tuple-element.52), channel_id=1, source_target_pairs={{0,1},{1,0},{2,3},{3,2},{4,5},{5,4},{6,7},{7,6},{8,9},{9,8},{10,11... | collective-permute-start | bytes 786440 | tf_op jit(solution)/shard_map/ppermute | solution.py:487
  124.7 1.7 %collective-permute-start.18 = (bf16[256,512]{1,0:T(8,128)(2,1)S(1)}, bf16[256,512]{1,0:T(8,128)(2,1)S(1)}, u32[]{:S(2)}, u32[]{:S(2)}) collective-permute-start(bf16[256,512]{1,0:T(8,128)(2,1)S(1)} %get-tuple-element.50), channel_id=1, source_target_pairs={{0,1},{1,0},{2,3},{3,2},{4,5},{5,4},{6,7},{7,6},{8,9},{9,8},{10,11... | collective-permute-start | bytes 786440 | tf_op jit(solution)/shard_map/ppermute | solution.py:494
  125.3 7.9 %collective-permute-start.20 = (bf16[256,512]{1,0:T(8,128)(2,1)S(1)}, bf16[256,512]{1,0:T(8,128)(2,1)S(1)}, u32[]{:S(2)}, u32[]{:S(2)}) collective-permute-start(bf16[256,512]{1,0:T(8,128)(2,1)S(1)} %shard_map.134), channel_id=1, source_target_pairs={{0,2},{2,0},{1,3},{3,1},{4,6},{6,4},{5,7},{7,5},{8,10},{10,8},{9,1... | collective-permute-start | bytes 786440 | tf_op jit(solution)/shard_map/ppermute | solution.py:489
